TPU v7x, 128 devices: a whole 4x4x4 slice. The times are simulated.
128 devices in a mesh: dom: 32 (over x, y, core), grp: 4 (over z).
Axes of the slice: x: 4, y: 4, z: 4, core: 2. Of those that a mesh axis runs over, the one named last changes fastest.
Arguments:
- features: bfloat16 [262144, 256], P(('dom', 'grp')), may hold values from -6 to 6
- edge_src: int32 [2097152], P(('dom', 'grp')), may hold values from 0 to 3071, as said below
- edge_dst: int32 [2097152], P(('dom', 'grp')), may hold values from 0 to 2047, as said below
- edge_count: int32 [128], P(('dom', 'grp')), may hold values from 4096 to 16384, as said below
- halo_index: int32 [128, 128, 8], P(('dom', 'grp')), may hold values from 0 to 2047
- request_rows: int32 [128, 128, 16], P(('dom', 'grp')), may hold values from 0 to 2047, as said below
- pair_ends: int32 [262144, 2], P(('dom', 'grp')), may hold values from 0 to 2047
- labels: int32 [262144], P(('dom', 'grp')), may hold values 0 or 1
- pair_weight: float32 [262144], P(('dom', 'grp')), may hold values from 0.25 to 4
- w_self: bfloat16 [256, 256], replicated, may hold values from -0.375 to 0.375
- w_neigh: bfloat16 [256, 256], replicated, may hold values from -0.375 to 0.375
- w_hidden: bfloat16 [512, 256], replicated, may hold values from -0.25 to 0.25
- b_hidden: float32 [256], replicated, may hold values from -3 to 3
- w_out: float32 [256], replicated, may hold values from -0.375 to 0.375
Outputs:
- logits: float32 [262144], P(('dom', 'grp'))
- grad_features: float32 [262144, 256], P(('dom', 'grp'))
- grad_w_self: float32 [256, 256], replicated
- grad_w_neigh: float32 [256, 256], replicated
- grad_w_hidden: float32 [512, 256], replicated
- grad_b_hidden: float32 [256], replicated
- grad_w_out: float32 [256], replicated
Inputs may be any that keep to these rules, and one draw needn't show every extreme that they name: `edge_src`: a row of the partition's own table. `edge_dst`: a local node of the partition; slots at or past edge_count are not live and hold arbitrary values. `edge_count`: some partition has exactly 16384 live slots. `halo_index`: local rows of the sending partition; 8 to every partition, itself included. `request_rows`: local rows of the owning partition, distinct and increasing within each list of 16. `pair_ends`: rows of the shard's own received rows.
All inputs are finite; a program needn't handle non-finite values. No bound on the sum of `labels` on one device may be relied on, other than what follows from the above.
Results may differ from a plain program's by a relative error of at most 0.02.
The roundings to bfloat16 on the way count: a program that leaves them out, or rounds other values in their place, can miss the bound.
Values may be sent and summed in bfloat16 or wider, within the bound.
No kernel may reach another device: no remote copies, remote signals or barrier semaphores. Data moves between devices by JAX's collectives and lax.ppermute only.
A program may use at most 192 MiB of HBM per device.

v0:
```python
import jax
import jax.numpy as jnp
from jax import lax
from jax.sharding import PartitionSpec as P


def in_one(arrays, axis):
    vector, at, outs = (jnp.concatenate([a.reshape(-1) for a in arrays]), 0, [])
    total = lax.psum(vector, axis)
    for a in arrays:
        outs.append(total[at : at + a.size].reshape(a.shape))
        at += a.size
    return tuple(outs)


def contract_rows(left, right):
    return lax.dot_general(
        left, right, (((0,), (0,)), ((), ())), preferred_element_type=jnp.float32
    )


def per_device(
    features,
    edge_src,
    edge_dst,
    edge_count,
    halo_index,
    request_rows,
    pair_ends,
    labels,
    pair_weight,
    w_self,
    w_neigh,
    w_hidden,
    b_hidden,
    w_out,
):
    node_rows, feat_width = features.shape
    dom_count = lax.axis_size("dom")
    grp_count = lax.axis_size("grp")
    peer_count = dom_count * grp_count
    halo_len = halo_index.shape[2]
    outgoing = features[halo_index[0]]
    arrived = lax.all_to_all(outgoing, ("dom", "grp"), split_axis=0, concat_axis=0, tiled=True)
    row_table = jnp.concatenate(
        [features, arrived.reshape(peer_count * halo_len, feat_width)], axis=0
    )
    table_rows = row_table.shape[0]
    slot_total = edge_src.shape[0]
    alive_slot = jnp.arange(slot_total, dtype=jnp.int32) < edge_count[0]
    dst_index = jnp.where(alive_slot, edge_dst, node_rows)
    adjacency = (
        jnp.zeros((node_rows + 1, table_rows), jnp.float32)
        .at[dst_index, edge_src]
        .add(1.0)[:node_rows]
    )
    degree = jnp.sum(adjacency, axis=1)
    floor_deg = jnp.maximum(degree, 1.0)[:, None]
    agg_sums = jnp.dot(adjacency, row_table.astype(jnp.float32))
    aggregate = (agg_sums / floor_deg).astype(jnp.bfloat16)
    embedding = (
        jnp.dot(features, w_self, preferred_element_type=jnp.float32)
        + jnp.dot(aggregate, w_neigh, preferred_element_type=jnp.float32)
    ).astype(jnp.bfloat16)
    wanted = lax.all_to_all(
        request_rows[0], ("dom", "grp"), split_axis=0, concat_axis=0, tiled=True
    )
    req_len = wanted.shape[1]
    served = embedding[wanted]
    received = lax.all_to_all(served, ("dom", "grp"), split_axis=0, concat_axis=0, tiled=True)
    recv_rows = peer_count * req_len
    received = received.reshape(recv_rows, feat_width)
    slot_ids = jnp.arange(recv_rows, dtype=jnp.int32)[None, :]
    select_left = (pair_ends[:, 0][:, None] == slot_ids).astype(jnp.float32)
    select_right = (pair_ends[:, 1][:, None] == slot_ids).astype(jnp.float32)
    left_rows = jnp.dot(
        select_left.astype(jnp.bfloat16), received, preferred_element_type=jnp.float32
    ).astype(jnp.bfloat16)
    right_rows = jnp.dot(
        select_right.astype(jnp.bfloat16), received, preferred_element_type=jnp.float32
    ).astype(jnp.bfloat16)
    pair_input = jnp.concatenate([left_rows, right_rows], axis=1)
    pre_act = jnp.dot(pair_input, w_hidden, preferred_element_type=jnp.float32) + b_hidden
    hidden = jnp.maximum(pre_act, 0.0)
    logits = jnp.dot(hidden, w_out)
    slope_term = pair_weight * (jax.nn.sigmoid(logits) - labels.astype(jnp.float32))
    grad_out = jnp.dot(slope_term, hidden)
    delta_act = jnp.where(pre_act > 0, slope_term[:, None] * w_out[None, :], 0.0)
    grad_bias = jnp.sum(delta_act, axis=0)
    delta_b = delta_act.astype(jnp.bfloat16)
    grad_hidden = jnp.dot(pair_input.T, delta_b, preferred_element_type=jnp.float32)
    pair_grad = jnp.dot(delta_b, w_hidden.T, preferred_element_type=jnp.float32)
    received_grad = contract_rows(select_left, pair_grad[:, :feat_width]) + contract_rows(
        select_right, pair_grad[:, feat_width:]
    )
    received_grad_b = received_grad.astype(jnp.bfloat16)
    back_rows = lax.all_to_all(
        received_grad_b.reshape(peer_count, req_len, feat_width),
        ("dom", "grp"),
        split_axis=0,
        concat_axis=0,
        tiled=True,
    )
    embedding_grad = (
        jnp.zeros((node_rows, feat_width), jnp.float32)
        .at[wanted.reshape(recv_rows)]
        .add(back_rows.reshape(recv_rows, feat_width).astype(jnp.float32))
    )
    grad_b = embedding_grad.astype(jnp.bfloat16)
    grad_self = jnp.dot(features.T, grad_b, preferred_element_type=jnp.float32)
    grad_neigh = jnp.dot(aggregate.T, grad_b, preferred_element_type=jnp.float32)
    direct = jnp.dot(grad_b, w_self.T, preferred_element_type=jnp.float32)
    agg_grad = jnp.dot(grad_b, w_neigh.T, preferred_element_type=jnp.float32) / floor_deg
    table_grad = contract_rows(adjacency, agg_grad)
    returned = table_grad[node_rows:].reshape(peer_count, halo_len, feat_width)
    halo_back = lax.all_to_all(
        returned.astype(jnp.bfloat16), ("dom", "grp"), split_axis=0, concat_axis=0, tiled=True
    ).astype(returned.dtype)
    grad_features = (
        (direct + table_grad[:node_rows])
        .at[halo_index[0].reshape(peer_count * halo_len)]
        .add(halo_back.reshape(peer_count * halo_len, feat_width))
    )
    summed = in_one((grad_self, grad_neigh, grad_hidden, grad_bias, grad_out), ("dom", "grp"))
    return (logits, grad_features, summed[0], summed[1], summed[2], summed[3], summed[4])


def solution(mesh):
    in_specs = (
        P(("dom", "grp"), None),
        P(("dom", "grp")),
        P(("dom", "grp")),
        P(("dom", "grp")),
        P(("dom", "grp"), None, None),
        P(("dom", "grp"), None, None),
        P(("dom", "grp"), None),
        P(("dom", "grp")),
        P(("dom", "grp")),
        P(),
        P(),
        P(),
        P(),
        P(),
    )
    out_specs = (P(("dom", "grp")), P(("dom", "grp"), None), P(), P(), P(), P(), P())
    return jax.shard_map(
        per_device, mesh=mesh, in_specs=in_specs, out_specs=out_specs, check_vma=False
    )
```

profile of v0, /device:TPU:1, one launch (start us, length us, event | category | flops | bytes accessed | tf_op | source)
XLA Modules:
  0.0 484.6 jit_solution(14658335759810923802)
XLA Ops:
  7.2 1.5 copy.31
  8.7 11.5 %all-to-all-start.1 = ((s32[128,1,16]{2,1,0:T(1,128)}), s32[128,1,16]{2,1,0:T(1,128)S(1)}, u32[]{:S(2)}, u32[]{:S(2)}) async-start(s32[128,1,16]{2,1,0:T(1,128)} %bitcast.7), calls=%async_computation.1 | async-start | bytes 131072 | tf_op jit(solution)/shard_map/all_to_all | solution.py:65
  20.8 0.9 compare_select_fusion.1
  21.6 0.9 compare_select_fusion.2
  22.5 0.9 multiply_reduce_fusion
  23.4 1.0 and_reduce_fusion
  24.4 0.7 compare_select_fusion.5
  25.1 0.1 copy.30
  25.2 0.1 reshape.214
  25.3 3.0 fusion.59
  28.3 95.7 %scatter_custom_fusion.2 = f32[6294528]{0:T(1024)} fusion(s32[16384]{0:T(1024)S(1)} %broadcast_select_fusion, f32[16384]{0:T(1024)S(1)} %broadcast.84, f32[]{:T(128)} %constant.6.clone.1), kind=kCustom, calls=%fused_computation.11 | custom fusion | flops 16384 | bytes 25178116
  124.0 16.7 %slice.87 = f32[6291456]{0:T(1024)} slice(f32[6294528]{0:T(1024)} %scatter_custom_fusion.2), slice={[0:6291456]} | slice | bytes 50331648 | tf_op jit(solution)/shard_map/slice | solution.py:53
  140.7 27.1 %reshape.208 = f32[2048,3072]{1,0:T(8,128)} reshape(f32[6291456]{0:T(1024)} %slice.87) | data formatting | bytes 50331648 | tf_op jit(solution)/shard_map/slice | solution.py:53
  167.8 9.2 %reduce_sum.18 = f32[2048]{0:T(1024)S(1)} reduce(f32[2048,3072]{1,0:T(8,128)} %reshape.208, f32[]{:T(128)} %constant.6.clone.1), dimensions={1}, to_apply=%region_1.2 | reduce | flops 6289408 | bytes 25174020 | tf_op jit(solution)/shard_map/reduce_sum | solution.py:57
  177.1 5.0 %gather_fusion = bf16[1024,256]{1,0:T(8,128)(2,1)} fusion(bf16[2048,256]{1,0:T(8,128)(2,1)S(1)} %copy-done.1, s32[1024]{0:T(1024)S(1)} %broadcast_clamp_fusion.1), kind=kCustom, calls=%fused_computation | custom fusion | bytes 1052672 | tf_op jit(solution)/shard_map/gather | solution.py:43
  182.0 10.1 %all-to-all-start = ((bf16[128,8,256]{2,1,0:T(8,128)(2,1)}), bf16[128,8,256]{2,1,0:T(8,128)(2,1)S(1)}, u32[]{:S(2)}, u32[]{:S(2)}) async-start(bf16[128,8,256]{2,1,0:T(8,128)(2,1)} %bitcast.5), calls=%async_computation | async-start | bytes 1048576 | tf_op jit(solution)/shard_map/all_to_all | solution.py:44
  192.2 0.1 reshape.222
  192.3 13.7 %all-to-all-done = bf16[128,8,256]{2,1,0:T(8,128)(2,1)S(1)} async-done(((bf16[128,8,256]{2,1,0:T(8,128)(2,1)}), bf16[128,8,256]{2,1,0:T(8,128)(2,1)S(1)}, u32[]{:S(2)}, u32[]{:S(2)}) %all-to-all-start) | async-done | bytes 524320 | tf_op jit(solution)/shard_map/all_to_all | solution.py:44
  205.9 11.9 %fusion.15 = bf16[2048,256]{1,0:T(8,128)(2,1)S(1)} fusion(f32[2048,3072]{1,0:T(8,128)} %reshape.208, bf16[1024,256]{1,0:T(8,128)(2,1)S(1)} %bitcast.67, bf16[2048,256]{1,0:T(8,128)(2,1)S(1)} %copy-done.1, f32[2048]{0:T(1024)S(1)} %broadcast_maximum_fusion), kind=kOutput, calls=%fused_computation.29 | convolution fusion | flops 3225419776 | bytes 27795456 | tf_op jit(solution)/shard_map/dot_general | solution.py:59
  217.8 0.4 fusion.12
  218.3 9.1 %gather_fusion.1 = bf16[2048,256]{1,0:T(8,128)(2,1)} fusion(bf16[2048,256]{1,0:T(8,128)(2,1)S(1)} %fusion.12, s32[2048]{0:T(1024)S(1)} %broadcast_clamp_fusion), kind=kCustom, calls=%fused_computation.1 | custom fusion | bytes 2105344 | tf_op jit(solution)/shard_map/gather | solution.py:69
  227.3 4.1 all-to-all-start.2
  231.5 19.5 %all-to-all-done.2 = bf16[128,16,256]{2,1,0:T(8,128)(2,1)S(1)} async-done(((bf16[128,16,256]{2,1,0:T(8,128)(2,1)}), bf16[128,16,256]{2,1,0:T(8,128)(2,1)S(1)}, u32[]{:S(2)}, u32[]{:S(2)}) %all-to-all-start.2) | async-done | bytes 1048608 | tf_op jit(solution)/shard_map/all_to_all | solution.py:70
  251.0 2.9 fusion.13
  253.9 3.1 fusion.14
  257.1 0.7 convolution_add_fusion
  257.9 0.2 copy-done.22
  258.1 0.4 fusion.25
  258.4 0.3 copy-done.16
  258.8 1.1 fusion.21
  259.9 0.7 fusion.33
  260.7 4.9 %fusion = f32[2048,256]{1,0:T(8,128)S(1)} fusion(s32[2048]{0:T(1024)S(1)} %bitcast.87, bf16[2048,512]{1,0:T(8,128)(2,1)S(1)} %fusion.33), kind=kOutput, calls=%fused_computation.7 | convolution fusion | flops 2151677952 | bytes 3153920 | tf_op jit(solution)/shard_map/dot_general | solution.py:17
  265.6 6.3 %fusion.11 = bf16[2048,256]{1,0:T(8,128)(2,1)} fusion(f32[2048,256]{1,0:T(8,128)S(1)} %fusion, s32[2048]{0:T(1024)S(1)} %bitcast.85, bf16[2048,512]{1,0:T(8,128)(2,1)S(1)} %fusion.33), kind=kOutput, calls=%fused_computation.24 | convolution fusion | flops 2152726528 | bytes 4202496 | tf_op jit(solution)/shard_map/dot_general | solution.py:17
  271.9 3.9 all-to-all-start.3
  275.9 0.8 copy.32
  276.7 0.7 reshape_squeeze.3
  277.4 0.5 broadcast.126
  277.9 0.8 reduce.7
  278.7 0.1 reshape.197
  278.8 2.7 fusion.31
  281.5 1.1 copy.36
  282.6 0.3 fusion.23
  282.8 12.5 %all-to-all-done.3 = bf16[128,16,256]{2,1,0:T(8,128)(2,1)S(1)} async-done(((bf16[128,16,256]{2,1,0:T(8,128)(2,1)}), bf16[128,16,256]{2,1,0:T(8,128)(2,1)S(1)}, u32[]{:S(2)}, u32[]{:S(2)}) %all-to-all-start.3) | async-done | bytes 1048608 | tf_op jit(solution)/shard_map/all_to_all | solution.py:97
  295.4 13.0 %scatter_custom_fusion = f32[2048,256]{1,0:T(8,128)} fusion(s32[2048]{0:T(1024)S(1)} %bitcast.83, bf16[2048,256]{1,0:T(8,128)(2,1)S(1)} %bitcast.66, f32[]{:T(128)} %constant.6.clone.1), kind=kCustom, calls=%fused_computation.34 | custom fusion | flops 1048576 | bytes 3145732 | tf_op jit(solution)/shard_map/scatter-add | solution.py:107
  308.4 1.7 convert_element_type.61
  310.1 1.2 convolution_bitcast_fusion
  311.3 0.5 convolution_bitcast_fusion.1
  311.8 12.3 %fusion.16 = f32[3072,256]{1,0:T(8,128)} fusion(f32[2048,3072]{1,0:T(8,128)} %reshape.208, bf16[2048,256]{1,0:T(8,128)(2,1)S(1)} %convert_element_type.61, bf16[256,256]{1,0:T(8,128)(2,1)S(1)} %copy-done.10, f32[2048]{0:T(1024)S(1)} %broadcast_maximum_fusion), kind=kOutput, calls=%fused_computation.30 | convolution fusion | flops 3490185216 | bytes 29499392 | tf_op jit(solution)/shard_map/dot_general | solution.py:17
  324.1 0.1 copy.35
  324.2 0.1 copy.33
  324.4 0.1 copy.34
  324.6 0.6 copy-done.5
  325.2 1.0 copy-done.6
  326.2 2.1 fusion.47
  328.3 4.3 all-to-all-start.4
  332.7 3.4 convolution_add_fusion.1
  336.0 10.8 %all-to-all-done.4 = bf16[128,8,256]{2,1,0:T(8,128)(2,1)S(1)} async-done(((bf16[128,8,256]{2,1,0:T(8,128)(2,1)}), bf16[128,8,256]{2,1,0:T(8,128)(2,1)S(1)}, u32[]{:S(2)}, u32[]{:S(2)}) %all-to-all-start.4) | async-done | bytes 524320 | tf_op jit(solution)/shard_map/all_to_all | solution.py:116
  346.9 9.0 %scatter_custom_fusion.1 = f32[2048,256]{1,0:T(8,128)} fusion(f32[2048,256]{1,0:T(8,128)} %convolution_add_fusion.1, s32[1024]{0:T(1024)S(1)} %bitcast.90, bf16[128,8,256]{2,1,0:T(8,128)(2,1)S(1)} %all-to-all-done.4), kind=kCustom, calls=%fused_computation.52 | custom fusion | flops 524288 | bytes 2621440 | tf_op jit(solution)/shard_map/scatter-add | solution.py:122
  355.8 117.2 %all-reduce.2.cloned.1.call-done = f32[262656]{0:T(1024)} async-done(((f32[262656]{0:T(1024)}), f32[262656]{0:T(1024)}) %all-reduce.2.cloned.1.call-update) | async-done | bytes 1050640 | tf_op jit(solution)/shard_map/psum | solution.py:9
  473.0 1.2 slice.94
  474.2 0.9 slice.79
  475.2 0.8 slice.75
  475.9 0.8 slice.77
  476.7 0.6 fusion.56
  (61 shorter events, 0.4 us)
Async XLA Ops:
  7.2 249.9 %copy-start = (bf16[512,256]{1,0:T(8,128)(2,1)S(1)}, bf16[512,256]{1,0:T(8,128)(2,1)}, u32[]{:S(2)}) copy-start(bf16[512,256]{1,0:T(8,128)(2,1)} %param.25) | copy-start | bytes 786436
  8.7 173.4 %all-to-all-start.1 = ((s32[128,1,16]{2,1,0:T(1,128)}), s32[128,1,16]{2,1,0:T(1,128)S(1)}, u32[]{:S(2)}, u32[]{:S(2)}) async-start(s32[128,1,16]{2,1,0:T(1,128)} %bitcast.7), calls=%async_computation.1 | async-start | bytes 131072 | tf_op jit(solution)/shard_map/all_to_all | solution.py:65
  167.8 9.2 %copy-start.1 = (bf16[2048,256]{1,0:T(8,128)(2,1)S(1)}, bf16[2048,256]{1,0:T(8,128)(2,1)}, u32[]{:S(2)}) copy-start(bf16[2048,256]{1,0:T(8,128)(2,1)} %param.14) | copy-start | bytes 3145732
  182.0 23.9 %all-to-all-start = ((bf16[128,8,256]{2,1,0:T(8,128)(2,1)}), bf16[128,8,256]{2,1,0:T(8,128)(2,1)S(1)}, u32[]{:S(2)}, u32[]{:S(2)}) async-start(bf16[128,8,256]{2,1,0:T(8,128)(2,1)} %bitcast.5), calls=%async_computation | async-start | bytes 1048576 | tf_op jit(solution)/shard_map/all_to_all | solution.py:44
  205.9 11.9 %copy-start.4 = (f32[2048,256]{1,0:T(8,128)S(1)}, f32[2048,256]{1,0:T(8,128)}, u32[]{:S(2)}) copy-start(f32[2048,256]{1,0:T(8,128)} %fusion.59) | copy-start | bytes 6291460
  205.9 11.9 %copy-start.9 = (bf16[256,256]{1,0:T(8,128)(2,1)S(1)}, bf16[256,256]{1,0:T(8,128)(2,1)}, u32[]{:S(2)}) copy-start(bf16[256,256]{1,0:T(8,128)(2,1)} %param.24) | copy-start | bytes 393220
  227.3 4.1 copy-start.15
  227.3 23.7 %all-to-all-start.2 = ((bf16[128,16,256]{2,1,0:T(8,128)(2,1)}), bf16[128,16,256]{2,1,0:T(8,128)(2,1)S(1)}, u32[]{:S(2)}, u32[]{:S(2)}) async-start(bf16[128,16,256]{2,1,0:T(8,128)(2,1)} %bitcast.65), calls=%async_computation.2 | async-start | bytes 2097152 | tf_op jit(solution)/shard_map/all_to_all | solution.py:70
  253.9 3.2 copy-start.21
  253.9 3.2 copy-start.20
  257.1 1.0 copy-start.22
  257.1 1.0 copy-start.18
  258.1 1.9 copy-start.2
  258.1 0.7 copy-start.16
  258.1 0.8 copy-start.17
  258.4 2.2 copy-start.13
  259.9 5.7 %copy-start.11 = (pred[2048,256]{1,0:T(32,128)(4,1)}, pred[2048,256]{1,0:T(32,128)(4,1)S(1)}, u32[]{:S(2)}) copy-start(pred[2048,256]{1,0:T(32,128)(4,1)S(1)} %get-tuple-element.8) | copy-start | bytes 1572868
  271.9 23.4 %all-to-all-start.3 = ((bf16[128,16,256]{2,1,0:T(8,128)(2,1)}), bf16[128,16,256]{2,1,0:T(8,128)(2,1)S(1)}, u32[]{:S(2)}, u32[]{:S(2)}) async-start(bf16[128,16,256]{2,1,0:T(8,128)(2,1)} %bitcast.69), calls=%async_computation.3 | async-start | bytes 2097152 | tf_op jit(solution)/shard_map/all_to_all | solution.py:97
  275.8 197.2 %all-reduce.2.cloned.1.call-start = ((), (), s32[]{:S(2)}) async-start(), calls=%async_computation.5 | async-start | bytes 2105344 | tf_op jit(solution)/shard_map/psum | solution.py:9
  278.8 3.8 copy-start.3
  310.1 1.7 copy-start.10
  311.8 12.3 %copy-start.8 = (f32[32,2,8,128]{3,2,1,0:T(8,128)S(1)}, f32[32,2,8,128]{3,2,1,0:T(8,128)}, u32[]{:S(2)}) copy-start(f32[32,2,8,128]{3,2,1,0:T(8,128)} %convolution_bitcast_fusion) | copy-start | bytes 786436
  324.1 1.0 copy-start.5
  324.1 1.1 copy-start.19
  325.1 7.5 %copy-start.14 = (s32[1024,1]{0,1:T(1,128)S(1)}, s32[1024,1]{0,1:T(1,128)}, u32[]{:S(2)}) copy-start(s32[1024,1]{0,1:T(1,128)} %reshape_squeeze.3) | copy-start | bytes 12292
  325.1 7.5 %copy-start.12 = (bf16[256,256]{1,0:T(8,128)(2,1)S(1)}, bf16[256,256]{1,0:T(8,128)(2,1)}, u32[]{:S(2)}) copy-start(bf16[256,256]{1,0:T(8,128)(2,1)} %param.23) | copy-start | bytes 393220
  325.2 1.0 copy-start.6
  328.3 18.6 %all-to-all-start.4 = ((bf16[128,8,256]{2,1,0:T(8,128)(2,1)}), bf16[128,8,256]{2,1,0:T(8,128)(2,1)S(1)}, u32[]{:S(2)}, u32[]{:S(2)}) async-start(bf16[128,8,256]{2,1,0:T(8,128)(2,1)} %fusion.47), calls=%async_computation.4 | async-start | bytes 1048576 | tf_op jit(solution)/shard_map/all_to_all | solution.py:116
  473.0 2.1 copy-start.7
Sparse Core Ops, SparseCore 0:
  326.3 146.6 all-reduce.1
where the time goes:
time: 492 us; the launch traced here: 485 us
  waiting for transfers between devices  174 us (35%)
  other arithmetic  135 us (27%)
  local copies, waits for them, and re-layouts  71.9 us (15%)
  matrix products  54.7 us (11%)
  starting transfers between devices  34 us (7%)
  between operations  15.6 us (3%)
    psum x1, waiting for transfers between devices, in_one(): total = lax.psum(vector, axis)  117 us
    unnamed x4, other arithmetic  97.6 us
    slice x2, local copies, waits for them, and re-layouts, per_device(): jnp.zeros((node_rows + 1, table_rows), jnp.float32).at[dst_index, edge_src]  43.9 us
    dot_general x3, matrix products, contract_rows(): lax.dot_general(left, right, (((0,), (0,)), ((), ())), preferred_element_...  23.5 us
    all_to_all x1, waiting for transfers between devices, per_device(): lax.all_to_all(served, ('dom', 'grp'), split_axis=0, concat_axis=0, tiled...  19.5 us
    all_to_all x1, waiting for transfers between devices, per_device(): lax.all_to_all(outgoing, ('dom', 'grp'), split_axis=0, concat_axis=0, til...  13.7 us
    scatter-add x1, other arithmetic, per_device(): embedding_grad = jnp.zeros((node_rows, feat_width), jnp.float32).at[wante...  13 us
    all_to_all x1, waiting for transfers between devices, per_device(): lax.all_to_all(received_grad_b.reshape(peer_count, req_len, feat_width),...  12.5 us
  transfers between devices with their start and end apart: 6, of which 5 were waited for; matrix products, arithmetic and copies ran while one was open for 38% of the time, Pallas kernels for 0%

commit v1 on v0

v1 whole, which is shorter than its diff:
```python
import functools

import jax
import jax.numpy as jnp
from jax import lax
from jax.experimental import pallas as pl
from jax.experimental.pallas import tpu as pltpu
from jax.sharding import PartitionSpec as P

BF16, F32, I16, I32 = jnp.bfloat16, jnp.float32, jnp.int16, jnp.int32
NN = (((1,), (0,)), ((), ()))
NT = (((1,), (1,)), ((), ()))
TN = (((0,), (0,)), ((), ()))
AXES = ("dom", "grp")
DST_BLOCK = 256
SRC_BLOCK = 1024
LIMIT = pltpu.CompilerParams(vmem_limit_bytes=56 * 1024 * 1024)


def mm(left, right, dims=NN):
    return lax.dot_general(left, right, dims, preferred_element_type=F32)


def spread_hot(diff, step, count, axis):
    one, zero = jnp.ones((), BF16), jnp.zeros((), BF16)
    pieces = [jnp.where(diff == jnp.int16(step * k), one, zero) for k in range(count)]
    return jnp.concatenate(pieces, axis=axis)


def hot_rows(row, height):
    width = row.shape[1]
    wide = jnp.broadcast_to(row, (16, width)) - lax.broadcasted_iota(I32, (16, width), 0)
    return spread_hot(wide.astype(I16), 16, height // 16, 0)


def hot_tile(tile, width):
    diff = tile - lax.broadcasted_iota(I32, tile.shape, 1)
    return spread_hot(diff.astype(I16), 128, width // 128, 1)


def whole(memory_space=pltpu.VMEM):
    return pl.BlockSpec(memory_space=memory_space)


def shape_of(shape, dtype):
    return jax.ShapeDtypeStruct(shape, dtype)


def cost(flops, moved):
    return pl.CostEstimate(flops=flops, bytes_accessed=moved, transcendentals=0)


def send_body(slot_ref, halo_ref, want_ref, feat_ref, out_ref):
    parts = out_ref.shape[0]
    want = jnp.transpose(want_ref[...])
    tiled = jnp.concatenate([want] * 8, axis=1)
    lane = lax.broadcasted_iota(I32, tiled.shape, 1)
    mine = lax.shift_right_logical(lane, 4) == slot_ref[0]
    tiled = jnp.where(mine, tiled, 0)
    index = jnp.concatenate(
        [lax.shift_right_logical(tiled, 7).astype(F32), (tiled & 127).astype(F32)], axis=1
    )
    halo = halo_ref[...]
    for at in range(0, parts, 16):
        tile = jnp.concatenate(
            [jnp.broadcast_to(halo[:, p : p + 1], (8, 128)) for p in range(at, at + 16)], axis=0
        )
        rows = mm(hot_tile(tile, feat_ref.shape[0]), feat_ref[...])
        rows = rows.reshape(16, 8, rows.shape[1])
        notes = jnp.broadcast_to(index[at : at + 16, None, :], rows.shape)
        out_ref[at : at + 16] = jnp.concatenate([rows, notes], axis=1).astype(BF16)


def send_rows(slot, halo, want, features):
    parts = want.shape[1]
    return pl.pallas_call(
        send_body,
        out_shape=shape_of((parts, 16, features.shape[1]), BF16),
        in_specs=[whole(pltpu.SMEM), whole(), whole(), whole()],
        out_specs=whole(),
        compiler_params=LIMIT,
        cost_estimate=cost(10**9, 2 * 10**6),
        name="send_rows",
    )(slot, halo, want, features)


def edges_body(src_blocks, starts_ref, keys_ref, count_ref, degree_ref, acc_ref):
    block = pl.program_id(0)
    first, last = starts_ref[block], starts_ref[block + 1]
    top = keys_ref.shape[0] - 1
    row0 = lax.shift_right_logical(first, 7)
    trips = lax.shift_right_logical(lax.shift_right_logical(last + 127, 7) - row0 + 3, 2)

    def hots(trip):
        src, dst = [], []
        for i in range(4):
            row = row0 + 4 * trip + i
            keys = keys_ref[pl.ds(jnp.minimum(row, top), 1), :]
            live = jnp.logical_and(lax.shift_right_logical(keys, 18) == block, row <= top)
            dst.append(jnp.where(live, lax.shift_right_logical(keys, 10) & 255, -1))
            src.append(keys & 1023)
        return jnp.concatenate(src, axis=1), jnp.concatenate(dst, axis=1)

    def visit(trip, add):
        src, dst = hots(trip)
        right = hot_rows(dst, DST_BLOCK)
        for at in range(0, SRC_BLOCK, 256):
            part = mm(hot_rows(src - at, 256), right, NT)
            if add:
                part = acc_ref[at : at + 256, :] + part
            acc_ref[at : at + 256, :] = part

    visit(0, False)

    def again(trip, carry):
        visit(trip, True)
        return carry

    lax.fori_loop(1, trips, again, 0)
    total = acc_ref[...]
    count_ref[...] = total.astype(BF16)
    part = jnp.sum(total.reshape(SRC_BLOCK // 8, 8, DST_BLOCK), axis=0)
    opening = lax.rem(block, src_blocks) == 0

    @pl.when(opening)
    def _():
        degree_ref[...] = part

    @pl.when(jnp.logical_not(opening))
    def _():
        degree_ref[...] += part


def edge_counts(starts, keys, nodes, table):
    src_blocks = table // SRC_BLOCK
    return pl.pallas_call(
        functools.partial(edges_body, src_blocks),
        grid=(nodes // DST_BLOCK * src_blocks,),
        out_shape=(shape_of((table, nodes), BF16), shape_of((8, nodes), F32)),
        in_specs=[whole(pltpu.SMEM), whole()],
        out_specs=(
            pl.BlockSpec((SRC_BLOCK, DST_BLOCK), lambda b: (b % src_blocks, b // src_blocks)),
            pl.BlockSpec((8, DST_BLOCK), lambda b: (0, b // src_blocks)),
        ),
        scratch_shapes=[pltpu.VMEM((SRC_BLOCK, DST_BLOCK), F32)],
        compiler_params=LIMIT,
        cost_estimate=cost(14 * 10**9, 13 * 10**6),
        name="edge_counts",
    )(starts, keys)


def embed_body(
    count_ref, arrived_ref, feat_ref, degree_ref, self_ref, neigh_ref,
    served_ref, agg_ref, want_ref, table_ref, emb_ref,
):
    step = pl.program_id(0)
    nodes = feat_ref.shape[0]

    @pl.when(step == 0)
    def _():
        table_ref[:, :nodes] = jnp.transpose(feat_ref[...])
        arrived = arrived_ref[...].astype(F32)
        halo = arrived[:, :8, :].reshape(-1, arrived.shape[2]).astype(BF16)
        table_ref[:, nodes:] = jnp.transpose(halo)
        notes = arrived[:, 8:, :]
        grouped = notes.reshape(notes.shape[0] // 8, 8, 8, notes.shape[2])
        summed = jnp.sum(grouped, axis=1)[:, 0, :]
        index = summed[:, :128] * 128.0 + summed[:, 128:]
        want_ref[...] = index.astype(I32)

    sums = mm(table_ref[...], count_ref[...])
    degree = jnp.sum(degree_ref[...], axis=0, keepdims=True)
    mean = (sums / jnp.maximum(degree, 1.0)).astype(BF16)
    mean = jnp.transpose(mean)
    agg_ref[...] = mean
    at = pl.multiple_of(step * DST_BLOCK, DST_BLOCK)
    own = feat_ref[pl.ds(at, DST_BLOCK), :]
    emb_ref[pl.ds(at, DST_BLOCK), :] = (mm(own, self_ref[...]) + mm(mean, neigh_ref[...])).astype(BF16)

    @pl.when(step == pl.num_programs(0) - 1)
    def _():
        columns = jnp.transpose(want_ref[...])
        for k in range(columns.shape[1]):
            tile = jnp.broadcast_to(columns[:, k : k + 1], (128, 128))
            served_ref[k * 128 : (k + 1) * 128, :] = mm(hot_tile(tile, nodes), emb_ref[...]).astype(BF16)


def embed(counts, arrived, features, degree, w_self, w_neigh):
    table, nodes = counts.shape
    width = features.shape[1]
    return pl.pallas_call(
        embed_body,
        grid=(nodes // DST_BLOCK,),
        out_shape=(
            shape_of((nodes, width), BF16),
            shape_of((nodes, width), BF16),
            shape_of((16, 128), I32),
        ),
        in_specs=[
            pl.BlockSpec((table, DST_BLOCK), lambda i: (0, i)),
            whole(), whole(),
            pl.BlockSpec((8, DST_BLOCK), lambda i: (0, i)),
            whole(), whole(),
        ],
        out_specs=(
            pl.BlockSpec((nodes, width), lambda i: (0, 0)),
            pl.BlockSpec((DST_BLOCK, width), lambda i: (i, 0)),
            pl.BlockSpec((16, 128), lambda i: (0, 0)),
        ),
        scratch_shapes=[pltpu.VMEM((width, table), BF16), pltpu.VMEM((nodes, width), BF16)],
        compiler_params=LIMIT,
        cost_estimate=cost(6 * 10**9, 16 * 10**6),
        name="embed",
    )(counts, arrived, features, degree, w_self, w_neigh)


def decode_body(
    got_ref, ends_ref, label_ref, weight_ref, hid_ref, bias_ref, wout_ref,
    logit_ref, send_ref, grad_ref, hidden_ref, small_ref,
):
    rows, width = got_ref.shape
    pairs = ends_ref.shape[1]
    block = 256
    hidden_ref[...] = jnp.zeros_like(hidden_ref)
    small_ref[...] = jnp.zeros_like(small_ref)

    def pair_step(i, carry):
        at = pl.multiple_of(i * block, block)
        span = pl.ds(at, block)
        meta = jnp.concatenate(
            [
                ends_ref[:, span].astype(F32),
                label_ref[:, span].astype(F32),
                weight_ref[:, span],
                jnp.zeros((4, block), F32),
            ],
            axis=0,
        )
        cols = jnp.transpose(meta)
        ends = cols.astype(I32)
        left = mm(hot_tile(jnp.broadcast_to(ends[:, 0:1], (block, 128)), rows), got_ref[...])
        right = mm(hot_tile(jnp.broadcast_to(ends[:, 1:2], (block, 128)), rows), got_ref[...])
        both = jnp.concatenate([left, right], axis=1).astype(BF16)
        pre = mm(both, hid_ref[...]) + bias_ref[...]
        hidden = jnp.maximum(pre, 0.0)
        logits = jnp.sum(hidden * wout_ref[...], axis=1, keepdims=True)
        logit_ref[:, span] = jnp.transpose(jnp.broadcast_to(logits, (block, 128)))[0:1, :]
        slope = cols[:, 3:4] * (jax.nn.sigmoid(logits) - cols[:, 2:3])
        delta = jnp.where(pre > 0, slope * wout_ref[...], 0.0)
        small_ref[0:8, :] += jnp.sum(delta.reshape(block // 8, 8, width), axis=0)
        small_ref[8:16, :] += jnp.sum((slope * hidden).reshape(block // 8, 8, width), axis=0)
        delta = delta.astype(BF16)
        hidden_ref[...] += mm(both, delta, TN)
        grad_ref[span, :] = mm(delta, hid_ref[...], NT).astype(BF16)
        return carry

    lax.fori_loop(0, pairs // block, pair_step, 0)

    def row_step(i, carry):
        at = i * block
        grad = mm(hot_rows(ends_ref[0:1, :] - at, block), grad_ref[:, :width])
        grad += mm(hot_rows(ends_ref[1:2, :] - at, block), grad_ref[:, width:])
        send_ref[pl.ds(i * 16, 16), 0:16, :] = grad.reshape(16, 16, width).astype(BF16)
        return carry

    lax.fori_loop(0, rows // block, row_step, 0)
    bias = jnp.sum(small_ref[0:8, :], axis=0, keepdims=True)
    wout = jnp.sum(small_ref[8:16, :], axis=0, keepdims=True)
    lines = []
    for line in (bias, wout):
        high = line.astype(BF16).astype(F32)
        for half in (high, line - high):
            lines += [half[:, :128], half[:, 128:]]
    tail = jnp.concatenate(lines, axis=0)
    total = hidden_ref[...].reshape(-1, 8, width)
    tail = jnp.broadcast_to(tail[None], (total.shape[0], 8, 128))
    even = jnp.concatenate([total[:, :, :128], tail], axis=2)
    odd = jnp.concatenate([total[:, :, 128:], tail], axis=2)
    joined = jnp.stack([even, odd], axis=1).reshape(-1, 8, width)
    send_ref[:, 16:24, :] = joined.astype(BF16)


def decode(got, ends, labels, weights, w_hidden, bias, w_out, parts):
    rows, width = got.shape
    pairs = ends.shape[1]
    return pl.pallas_call(
        decode_body,
        out_shape=(shape_of((1, pairs), F32), shape_of((parts, 24, width), BF16)),
        in_specs=[whole()] * 7,
        out_specs=(whole(), whole()),
        scratch_shapes=[
            pltpu.VMEM((pairs, 2 * width), BF16),
            pltpu.VMEM((2 * width, width), F32),
            pltpu.VMEM((16, width), F32),
        ],
        compiler_params=LIMIT,
        cost_estimate=cost(10 * 10**9, 4 * 10**6),
        name="decode",
    )(got, ends, labels, weights, w_hidden, bias, w_out)


def spread_body(
    count_ref, back_ref, want_ref, feat_ref, agg_ref, degree_ref, self_ref, neigh_ref,
    send_ref, direct_ref, small_ref, grad_ref, mean_ref,
):
    step = pl.program_id(0)
    nodes, width = feat_ref.shape
    halo_steps = 2
    rows = count_ref.shape[0]

    @pl.when(step == 0)
    def _():
        back = back_ref[...].astype(F32)
        tail = jnp.sum(back[:, 16:, :], axis=0)
        small_ref[...] = tail[:, 128:]
        flat = back[:, :16, :].reshape(-1, width).astype(BF16)
        want = jnp.concatenate([want_ref[k : k + 1, :] for k in range(16)], axis=1)
        for at in range(0, nodes, 256):
            grad = mm(hot_rows(want - at, 256), flat).astype(BF16)
            grad_ref[at : at + 256, :] = grad
            degree = jnp.sum(degree_ref[:, at : at + 256], axis=0, keepdims=True)
            column = jnp.transpose(jnp.broadcast_to(jnp.maximum(degree, 1.0), (128, 256)))
            scaled = mm(grad, neigh_ref[...], NT) / jnp.concatenate([column, column], axis=1)
            mean_ref[at : at + 256, :] = scaled.astype(BF16)
        both = jnp.concatenate(
            [mm(feat_ref[...], grad_ref[...], TN), mm(agg_ref[...], grad_ref[...], TN)], axis=0
        )
        both = both.reshape(-1, 8, width)
        tail = jnp.broadcast_to(tail[None, :, :128], (both.shape[0], 8, 128))
        even = jnp.concatenate([both[:, :, :128], tail], axis=2)
        odd = jnp.concatenate([both[:, :, 128:], tail], axis=2)
        joined = jnp.stack([even, odd], axis=1).reshape(-1, 8, width)
        send_ref[:, 8:16, :] = joined.astype(BF16)

    grad = mm(count_ref[...], mean_ref[...])

    @pl.when(step < halo_steps)
    def _():
        peers = rows // 8
        send_ref[pl.ds(step * peers, peers), 0:8, :] = grad.reshape(peers, 8, width).astype(BF16)

    @pl.when(step >= halo_steps)
    def _():
        at = pl.multiple_of((step - halo_steps) * rows, rows)
        direct_ref[...] = mm(grad_ref[pl.ds(at, rows), :], self_ref[...], NT) + grad


def spread(counts, back, want, features, agg, degree, w_self, w_neigh):
    table, nodes = counts.shape
    width = features.shape[1]
    rows = 512
    own = nodes // rows
    return pl.pallas_call(
        spread_body,
        grid=(table // rows,),
        out_shape=(
            shape_of((back.shape[0], 16, width), BF16),
            shape_of((nodes, width), F32),
            shape_of((8, 128), F32),
        ),
        in_specs=[
            pl.BlockSpec((rows, nodes), lambda i: ((i + own) % (table // rows), 0)),
            whole(), whole(), whole(), whole(), whole(), whole(), whole(),
        ],
        out_specs=(
            pl.BlockSpec((back.shape[0], 16, width), lambda i: (0, 0, 0)),
            pl.BlockSpec((rows, width), lambda i: (jnp.maximum(i - 2, 0), 0)),
            pl.BlockSpec((8, 128), lambda i: (0, 0)),
        ),
        scratch_shapes=[pltpu.VMEM((nodes, width), BF16), pltpu.VMEM((nodes, width), BF16)],
        compiler_params=LIMIT,
        cost_estimate=cost(7 * 10**9, 20 * 10**6),
        name="spread",
    )(counts, back, want, features, agg, degree, w_self, w_neigh)


def chunk_body(back_ref, out_ref):
    tail = jnp.sum(back_ref[:, 8:, :].astype(F32), axis=0)[:, :128]
    out_ref[...] = jnp.broadcast_to(tail[None], out_ref.shape).astype(BF16)


def chunk(back):
    return pl.pallas_call(
        chunk_body,
        out_shape=shape_of((back.shape[0], 8, 128), BF16),
        in_specs=[whole()],
        out_specs=whole(),
        compiler_params=LIMIT,
        cost_estimate=cost(10**6, 10**6),
        name="chunk",
    )(back)


def join_lanes(pieces):
    pieces = pieces.reshape(-1, 2, 8, 128)
    return jnp.concatenate([pieces[:, 0], pieces[:, 1]], axis=2).reshape(-1, 256)


def final_body(direct_ref, back_ref, halo_ref, small_ref, out_ref, hidden_ref, bias_ref, wout_ref):
    back = back_ref[...].astype(F32)
    width = back.shape[2]
    flat = back[:, :8, :].reshape(-1, width).astype(BF16)
    halo = jnp.concatenate([halo_ref[k : k + 1, :] for k in range(8)], axis=1)
    for at in range(0, out_ref.shape[0], 256):
        out_ref[at : at + 256, :] = direct_ref[at : at + 256, :] + mm(hot_rows(halo - at, 256), flat)
    hidden_ref[...] = join_lanes(back[:, 8:, 128:])
    bias_ref[...] = small_ref[0:2, :] + small_ref[2:4, :]
    wout_ref[...] = small_ref[4:6, :] + small_ref[6:8, :]


def final(direct, back, halo, small):
    nodes, width = direct.shape
    return pl.pallas_call(
        final_body,
        out_shape=(
            shape_of((nodes, width), F32),
            shape_of((2 * width, width), F32),
            shape_of((2, 128), F32),
            shape_of((2, 128), F32),
        ),
        in_specs=[whole()] * 4,
        out_specs=(whole(),) * 4,
        compiler_params=LIMIT,
        cost_estimate=cost(2 * 10**9, 6 * 10**6),
        name="final",
    )(direct, back, halo, small)


def weights_body(pieces_ref, self_ref, neigh_ref):
    both = join_lanes(pieces_ref[...].astype(F32))
    half = both.shape[0] // 2
    self_ref[...] = both[:half, :]
    neigh_ref[...] = both[half:, :]


def weights(pieces):
    shape = shape_of((256, 256), F32)
    return pl.pallas_call(
        weights_body,
        out_shape=(shape, shape),
        in_specs=[whole()],
        out_specs=(whole(), whole()),
        compiler_params=LIMIT,
        cost_estimate=cost(10**6, 10**6),
        name="weights",
    )(pieces)


def exchange(rows):
    return lax.all_to_all(rows, AXES, split_axis=0, concat_axis=0, tiled=True)


def per_device(
    features, edge_src, edge_dst, edge_count, halo_index, request_rows, pair_ends,
    labels, pair_weight, w_self, w_neigh, w_hidden, b_hidden, w_out,
):
    nodes, width = features.shape
    parts, halo_len = halo_index.shape[1:]
    table = nodes + parts * halo_len
    slots = edge_src.shape[0]
    me = lax.axis_index("dom") * lax.axis_size("grp") + lax.axis_index("grp")

    sent = send_rows((me % 8).reshape(1), halo_index[0].T, request_rows[0].T, features)
    arrived = exchange(sent)

    src_blocks = table // SRC_BLOCK
    buckets = nodes // DST_BLOCK * src_blocks
    bucket = edge_dst // DST_BLOCK * src_blocks + edge_src // SRC_BLOCK
    packed = (bucket << 18) | ((edge_dst % DST_BLOCK) << 10) | (edge_src % SRC_BLOCK)
    live = jnp.arange(slots, dtype=I32) < edge_count[0]
    keys = jnp.where(live, packed, buckets << 18)
    bounds = jnp.arange(buckets + 1, dtype=I32) << 18
    starts = jnp.sum((keys[None, :] < bounds[:, None]).astype(I32), axis=1)
    keys = lax.sort(keys, is_stable=False)
    counts, degree = edge_counts(starts, keys.reshape(slots // 128, 128), nodes, table)

    served, agg, want = embed(counts, arrived, features, degree, w_self, w_neigh)
    got = exchange(served.reshape(parts, -1, width)).reshape(-1, width)
    logits, pair_back = decode(
        got, pair_ends.T, labels.reshape(1, -1), pair_weight.reshape(1, -1),
        w_hidden, b_hidden.reshape(1, -1), w_out.reshape(1, -1), parts,
    )
    back = exchange(pair_back)
    halo_back, direct, small = spread(counts, back, want, features, agg, degree, w_self, w_neigh)
    returned = exchange(halo_back)
    pieces = exchange(chunk(returned))
    grad_features, grad_hidden, grad_bias, grad_out = final(
        direct, returned, halo_index[0].reshape(8, -1), small
    )
    grad_self, grad_neigh = weights(pieces)
    return (
        logits.reshape(-1), grad_features, grad_self, grad_neigh, grad_hidden,
        grad_bias.reshape(-1), grad_out.reshape(-1),
    )


def solution(mesh):
    split, rows, cubes = P(AXES), P(AXES, None), P(AXES, None, None)
    in_specs = (
        rows, split, split, split, cubes, cubes, rows, split, split, P(), P(), P(), P(), P(),
    )
    out_specs = (split, rows, P(), P(), P(), P(), P())
    return jax.shard_map(
        per_device, mesh=mesh, in_specs=in_specs, out_specs=out_specs, check_vma=False
    )
```

time: 492 us -> 214 us (0.43); the launches traced: 485 us -> 213 us
  waiting for transfers between devices: 174 us -> 5.66 us
  other arithmetic: 135 us -> 8.04 us
  blocking collectives: 0 us -> 93.9 us
  Pallas kernels: 0 us -> 86.6 us
  local copies, waits for them, and re-layouts: 71.9 us -> 2.46 us
  matrix products: 54.7 us -> 0 us
  starting transfers between devices: 34 us -> 15.4 us
  between operations: 15.6 us -> 1.38 us
    psum x1 -> x0, waiting for transfers between devices: 117 us -> none  [in_one(): total = lax.psum(vector, axis)]
    unnamed x4 -> x0, other arithmetic: 97.6 us -> none
    all_to_all x0 -> x3, blocking collectives: none -> 93.9 us  [exchange(): return lax.all_to_all(rows, AXES, split_axis=0, concat_axis=0, tiled=True)]
    pallas_call x0 -> x8, Pallas kernels: none -> 86.6 us  [the longest x1 21.1 us: decode(): pl.pallas_call(decode_body, out_shape=(shape_of((1, pairs), F32), shape_o...]
    dot_general x16 -> x0, matrix products: 54.7 us -> none  [the longest x3 23.5 us: contract_rows(): lax.dot_general(left, right, (((0,), (0,)), ((), ())), preferred_element_...]
    all_to_all x5 -> x2, waiting for transfers between devices: 56.5 us -> 5.66 us  [exchange(): return lax.all_to_all(rows, AXES, split_axis=0, concat_axis=0, tiled=True)]
    slice x9 -> x0, local copies, waits for them, and re-layouts: 48.1 us -> none  [the longest x2 43.9 us: per_device(): jnp.zeros((node_rows + 1, table_rows), jnp.float32).at[dst_index, edge_src]]
    scatter-add x2 -> x0, other arithmetic: 22 us -> none  [the longest x1 13 us: per_device(): embedding_grad = jnp.zeros((node_rows, feat_width), jnp.float32).at[wante...]
  transfers between devices with their start and end apart: 6 -> 2, of which waited for: 5 -> 1; matrix products, arithmetic and copies ran while one was open for 38% -> 4% of each run, Pallas kernels for 0% -> 12%
where the time goes in v1:
time: 214 us; the launch traced here: 213 us
  blocking collectives  93.9 us (44%)
  Pallas kernels  86.6 us (40%)
  starting transfers between devices  15.4 us (7%)
  other arithmetic  8.04 us (4%)
  waiting for transfers between devices  5.66 us (3%)
  local copies, waits for them, and re-layouts  2.46 us (1%)
    all_to_all x3, blocking collectives, exchange(): return lax.all_to_all(rows, AXES, split_axis=0, concat_axis=0, tiled=True)  93.9 us
    pallas_call x1, Pallas kernels, decode(): pl.pallas_call(decode_body, out_shape=(shape_of((1, pairs), F32), shape_o...  21.1 us
    pallas_call x1, Pallas kernels, edge_counts(): pl.pallas_call(functools.partial(edges_body, src_blocks), grid=(nodes //...  20.7 us
    pallas_call x1, Pallas kernels, spread(): pl.pallas_call(spread_body, grid=(table // rows,), out_shape=(shape_of((b...  17.1 us
    pallas_call x1, Pallas kernels, embed(): pl.pallas_call(embed_body, grid=(nodes // DST_BLOCK,), out_shape=(shape_o...  15.6 us
    all_to_all x2, starting transfers between devices, exchange(): return lax.all_to_all(rows, AXES, split_axis=0, concat_axis=0, tiled=True)  15.4 us
    sort x1, other arithmetic, per_device(): keys = lax.sort(keys, is_stable=False)  6.92 us
    all_to_all x2, waiting for transfers between devices, exchange(): return lax.all_to_all(rows, AXES, split_axis=0, concat_axis=0, tiled=True)  5.66 us
  transfers between devices with their start and end apart: 2, of which 1 were waited for; matrix products, arithmetic and copies ran while one was open for 4% of the time, Pallas kernels for 12%

profile of v1, /device:TPU:1, one launch (start us, length us, event | category | flops | bytes accessed | tf_op | source)
XLA Modules:
  0.0 213.4 jit_solution(17113536965472757296)
XLA Ops:
  0.6 0.0 copy-start.2
  0.7 0.0 copy-start.3
  0.7 3.6 %send_rows.1 = bf16[128,16,256]{2,1,0:T(8,128)(2,1)} custom-call(s32[1]{0:T(128)} %bitcast.2.slot_ref, s32[8,128]{1,0:T(8,128)} %bitcast.23, s32[16,128]{1,0:T(8,128)} %bitcast.25, bf16[2048,256]{1,0:T(8,128)(2,1)} %feat_ref.5), custom_call_target="tpu_custom_call" | custom-call | flops 1000000000 | bytes 2000000 | tf_op jit(solution)/shard_map/send_rows/pallas_call | solution.py:76
  4.3 11.5 %all-to-all-start = ((bf16[128,16,256]{2,1,0:T(8,128)(2,1)}), bf16[128,16,256]{2,1,0:T(8,128)(2,1)S(1)}, u32[]{:S(2)}, u32[]{:S(2)}) async-start(bf16[128,16,256]{2,1,0:T(8,128)(2,1)} %send_rows.1), calls=%async_computation | async-start | bytes 2097152 | tf_op jit(solution)/shard_map/all_to_all | solution.py:450
  16.4 0.0 copy-done.2
  16.4 0.0 copy-done.3
  16.5 0.1 fusion.5
  16.6 6.9 %sort.7 = s32[16384]{0:T(1024)} sort(s32[16384]{0:T(1024)S(1)} %fusion.5), dimensions={0}, to_apply=%region_1.2 | sort | flops 229376 | bytes 131072 | tf_op jit(solution)/shard_map/sort | solution.py:474
  23.5 1.0 convert_reduce_fusion.starts_ref
  24.5 20.7 %edge_counts.1 = (bf16[3072,2048]{1,0:T(8,128)(2,1)}, f32[8,2048]{1,0:T(8,128)}) custom-call(s32[25]{0:T(128)} %convert_reduce_fusion.starts_ref, s32[128,128]{1,0:T(8,128)} %bitcast.22), custom_call_target="tpu_custom_call" | custom-call | flops 14000000000 | bytes 13000000 | tf_op jit(solution)/shard_map/edge_counts/pallas_call | solution.py:136
  45.2 0.0 all-to-all-done.arrived_ref
  45.2 0.0 copy-start
  45.2 1.0 copy-done
  46.2 15.6 %embed.1 = (bf16[2048,256]{1,0:T(8,128)(2,1)}, bf16[2048,256]{1,0:T(8,128)(2,1)}, s32[16,128]{1,0:T(8,128)}) custom-call(bf16[3072,2048]{1,0:T(8,128)(2,1)} %get-tuple-element.23.count_ref, bf16[128,16,256]{2,1,0:T(8,128)(2,1)} %copy-done, bf16[2048,256]{1,0:T(8,128)(2,1)} %feat_ref.5, f32[8,2048]{1,0:T(8,128)} %get-tuple-element.24.degree_ref, ...), custom_call_target="tpu_custom_call" | custom-call | flops 6000000000 | bytes 16000000 | tf_op jit(solution)/shard_map/embed/pallas_call | solution.py:191
  61.8 39.2 %all_to_all.25 = bf16[128,16,256]{2,1,0:T(8,128)(2,1)} all-to-all(bf16[128,16,256]{2,1,0:T(8,128)(2,1)} %bitcast.20), channel_id=1, replica_groups=mesh['dom'=32,'grp'=4] {'dom','grp'}, dimensions={0} | all-to-all | bytes 2097152 | tf_op jit(solution)/shard_map/all_to_all | solution.py:450
  101.0 21.1 %decode.1 = (f32[1,2048]{1,0:T(1,128)}, bf16[128,24,256]{2,1,0:T(8,128)(2,1)}) custom-call(bf16[2048,256]{1,0:T(8,128)(2,1)} %bitcast.21, s32[2,2048]{1,0:T(2,128)} %bitcast.24, s32[1,2048]{1,0:T(1,128)} %bitcast.26, f32[1,2048]{1,0:T(1,128)} %bitcast.27, bf16[512,256]{1,0:T(8,128)(2,1)} %hid_ref.1, f32[1,256]{1,0:T(1,128)} %bitcast.28, f32[1,256]{1,0:T(1,128)} %bitcast.29), custom_call_target="tpu_custom_call" | custom-call | flops 10000000000 | bytes 4000000 | tf_op jit(solution)/shard_map/decode/pallas_call | solution.py:286
  122.1 30.2 %all_to_all.26.back_ref = bf16[128,24,256]{2,1,0:T(8,128)(2,1)} all-to-all(bf16[128,24,256]{2,1,0:T(8,128)(2,1)} %get-tuple-element.27), channel_id=1, replica_groups=mesh['dom'=32,'grp'=4] {'dom','grp'}, dimensions={0} | all-to-all | bytes 3145728 | tf_op jit(solution)/shard_map/all_to_all | solution.py:450
  152.2 17.1 %spread.1 = (bf16[128,16,256]{2,1,0:T(8,128)(2,1)}, f32[2048,256]{1,0:T(8,128)}, f32[8,128]{1,0:T(8,128)}) custom-call(bf16[3072,2048]{1,0:T(8,128)(2,1)} %get-tuple-element.23.count_ref, bf16[128,24,256]{2,1,0:T(8,128)(2,1)} %all_to_all.26.back_ref, s32[16,128]{1,0:T(8,128)} %get-tuple-element.28.want_ref, bf16[2048,256]{1,0:T(8,128)(2,1)} %feat_ref.5, ...), custom_call_target="tpu_custom_call" | custom-call | flops 7000000000 | bytes 20000000 | tf_op jit(solution)/shard_map/spread/pallas_call | solution.py:353
  169.4 0.0 copy-start.4
  169.4 24.5 %all_to_all.27.back_ref = bf16[128,16,256]{2,1,0:T(8,128)(2,1)} all-to-all(bf16[128,16,256]{2,1,0:T(8,128)(2,1)} %get-tuple-element.31), channel_id=1, replica_groups=mesh['dom'=32,'grp'=4] {'dom','grp'}, dimensions={0} | all-to-all | bytes 2097152 | tf_op jit(solution)/shard_map/all_to_all | solution.py:450
  193.9 2.1 chunk.1
  196.0 3.9 %all-to-all-start.4 = ((bf16[128,8,128]{2,1,0:T(8,128)(2,1)}), bf16[128,8,128]{2,1,0:T(8,128)(2,1)S(1)}, u32[]{:S(2)}, u32[]{:S(2)}) async-start(bf16[128,8,128]{2,1,0:T(8,128)(2,1)} %chunk.1), calls=%async_computation.4 | async-start | bytes 524288 | tf_op jit(solution)/shard_map/all_to_all | solution.py:450
  199.9 0.0 copy-done.4
  199.9 0.1 copy.23
  200.0 0.7 reshape_squeeze.3.halo_ref
  200.7 4.6 %final.1 = (f32[2048,256]{1,0:T(8,128)}, f32[512,256]{1,0:T(8,128)}, f32[2,128]{1,0:T(2,128)}, f32[2,128]{1,0:T(2,128)}) custom-call(f32[2048,256]{1,0:T(8,128)} %get-tuple-element.30.direct_ref, bf16[128,16,256]{2,1,0:T(8,128)(2,1)} %all_to_all.27.back_ref, s32[8,128]{1,0:T(8,128)} %reshape_squeeze.3.halo_ref, f32[8,128]{1,0:T(8,128)} %get-tuple-element.32.small_ref), custom_call_target="tpu_custom_call" | custom-call | flops 2000000000 | bytes 6000000 | tf_op jit(solution)/shard_map/final/pallas_call | solution.py:413
  205.3 5.7 %all-to-all-done.4.pieces_ref = bf16[128,8,128]{2,1,0:T(8,128)(2,1)S(1)} async-done(((bf16[128,8,128]{2,1,0:T(8,128)(2,1)}), bf16[128,8,128]{2,1,0:T(8,128)(2,1)S(1)}, u32[]{:S(2)}, u32[]{:S(2)}) %all-to-all-start.4) | async-done | bytes 262176 | tf_op jit(solution)/shard_map/all_to_all | solution.py:450
  211.0 0.0 copy-start.1
  211.0 0.7 copy-done.1
  211.7 1.8 weights.1
  (1 shorter events, 0.0 us)
Async XLA Ops:
  0.6 15.8 %copy-start.2 = (s32[16384]{0:T(1024)S(1)}, s32[16384]{0:T(1024)}, u32[]{:S(2)}) copy-start(s32[16384]{0:T(1024)} %param.16) | copy-start | bytes 196612
  0.7 15.8 %copy-start.3 = (s32[16384]{0:T(1024)S(1)}, s32[16384]{0:T(1024)}, u32[]{:S(2)}) copy-start(s32[16384]{0:T(1024)} %param.15) | copy-start | bytes 196612
  4.3 40.9 %all-to-all-start = ((bf16[128,16,256]{2,1,0:T(8,128)(2,1)}), bf16[128,16,256]{2,1,0:T(8,128)(2,1)S(1)}, u32[]{:S(2)}, u32[]{:S(2)}) async-start(bf16[128,16,256]{2,1,0:T(8,128)(2,1)} %send_rows.1), calls=%async_computation | async-start | bytes 2097152 | tf_op jit(solution)/shard_map/all_to_all | solution.py:450
  45.2 1.0 copy-start
  169.4 30.5 %copy-start.4 = (s32[1,128,8]{1,2,0:T(8,128)S(1)}, s32[1,128,8]{1,2,0:T(8,128)}, u32[]{:S(2)}) copy-start(s32[1,128,8]{1,2,0:T(8,128)} %param.18) | copy-start | bytes 12292
  196.0 15.0 %all-to-all-start.4 = ((bf16[128,8,128]{2,1,0:T(8,128)(2,1)}), bf16[128,8,128]{2,1,0:T(8,128)(2,1)S(1)}, u32[]{:S(2)}, u32[]{:S(2)}) async-start(bf16[128,8,128]{2,1,0:T(8,128)(2,1)} %chunk.1), calls=%async_computation.4 | async-start | bytes 524288 | tf_op jit(solution)/shard_map/all_to_all | solution.py:450
  211.0 0.7 copy-start.1

commit v2 on v1

v2 whole, which is shorter than its diff:
```python
import functools

import jax
import jax.numpy as jnp
from jax import lax
from jax.experimental import pallas as pl
from jax.experimental.pallas import tpu as pltpu
from jax.sharding import PartitionSpec as P

BF16, F32, I16, I32 = jnp.bfloat16, jnp.float32, jnp.int16, jnp.int32
NN = (((1,), (0,)), ((), ()))
NT = (((1,), (1,)), ((), ()))
TN = (((0,), (0,)), ((), ()))
AXES = ("dom", "grp")
DST_BLOCK = 256
SRC_BLOCK = 1024
SEND_MIB, EDGES_MIB, EMBED_MIB, DECODE_MIB, SPREAD_MIB = 8, 24, 24, 16, 24
CHUNK_MIB, FINAL_MIB, WEIGHTS_MIB = 8, 16, 8


def limit(mib):
    return pltpu.CompilerParams(vmem_limit_bytes=mib * 1024 * 1024)


def mm(left, right, dims=NN):
    return lax.dot_general(left, right, dims, preferred_element_type=F32)


def spread_hot(diff, step, count, axis):
    one, zero = jnp.ones((), BF16), jnp.zeros((), BF16)
    pieces = [jnp.where(diff == jnp.int16(step * k), one, zero) for k in range(count)]
    return jnp.concatenate(pieces, axis=axis)


def hot_rows(row, height):
    width = row.shape[1]
    wide = jnp.broadcast_to(row, (16, width)) - lax.broadcasted_iota(I32, (16, width), 0)
    return spread_hot(wide.astype(I16), 16, height // 16, 0)


def hot_tile(tile, width):
    diff = tile - lax.broadcasted_iota(I32, tile.shape, 1)
    return spread_hot(diff.astype(I16), 128, width // 128, 1)


def whole(memory_space=pltpu.VMEM):
    return pl.BlockSpec(memory_space=memory_space)


def shape_of(shape, dtype):
    return jax.ShapeDtypeStruct(shape, dtype)


def cost(flops, moved):
    return pl.CostEstimate(flops=flops, bytes_accessed=moved, transcendentals=0)


def send_body(slot_ref, halo_ref, want_ref, feat_ref, out_ref):
    parts = out_ref.shape[0]
    want = jnp.transpose(want_ref[...])
    tiled = jnp.concatenate([want] * 8, axis=1)
    lane = lax.broadcasted_iota(I32, tiled.shape, 1)
    mine = lax.shift_right_logical(lane, 4) == slot_ref[0]
    tiled = jnp.where(mine, tiled, 0)
    index = jnp.concatenate(
        [lax.shift_right_logical(tiled, 7).astype(F32), (tiled & 127).astype(F32)], axis=1
    )
    halo = halo_ref[...]
    for at in range(0, parts, 16):
        tile = jnp.concatenate(
            [jnp.broadcast_to(halo[:, p : p + 1], (8, 128)) for p in range(at, at + 16)], axis=0
        )
        rows = mm(hot_tile(tile, feat_ref.shape[0]), feat_ref[...])
        rows = rows.reshape(16, 8, rows.shape[1])
        notes = jnp.broadcast_to(index[at : at + 16, None, :], rows.shape)
        out_ref[at : at + 16] = jnp.concatenate([rows, notes], axis=1).astype(BF16)


def send_rows(slot, halo, want, features):
    parts = want.shape[1]
    return pl.pallas_call(
        send_body,
        out_shape=shape_of((parts, 16, features.shape[1]), BF16),
        in_specs=[whole(pltpu.SMEM), whole(), whole(), whole()],
        out_specs=whole(),
        compiler_params=limit(SEND_MIB),
        cost_estimate=cost(10**9, 2 * 10**6),
        name="send_rows",
    )(slot, halo, want, features)


def edges_body(src_blocks, starts_ref, keys_ref, count_ref, degree_ref, held_ref, acc_ref, sem):
    top = keys_ref.shape[0] - 1
    buckets = degree_ref.shape[1] // DST_BLOCK * src_blocks
    degree_ref[...] = jnp.zeros_like(degree_ref)
    ones = (lax.broadcasted_iota(I32, (16, 512), 0) == 0).astype(F32).astype(BF16)

    def block_of(bucket):
        tall = pl.multiple_of(lax.rem(bucket, src_blocks) * SRC_BLOCK, SRC_BLOCK)
        return bucket // src_blocks, pl.ds(tall, SRC_BLOCK)

    def flush(bucket):
        outer, tall = block_of(bucket)
        return pltpu.make_async_copy(held_ref.at[outer, tall], count_ref.at[outer, tall], sem)

    def products(bucket, row):
        wanted = jnp.where(bucket < buckets, bucket, -1)
        src, dst = [], []
        for i in range(4):
            keys = keys_ref[pl.ds(jnp.minimum(row + i, top), 1), :]
            live = jnp.logical_and(lax.shift_right_logical(keys, 18) == wanted, row + i <= top)
            dst.append(jnp.where(live, lax.shift_right_logical(keys, 10) & 255, -1))
            src.append(keys & 1023)
        src, dst = jnp.concatenate(src, axis=1), jnp.concatenate(dst, axis=1)
        right = hot_rows(dst, DST_BLOCK)
        both = mm(jnp.concatenate([hot_rows(src, SRC_BLOCK), ones], axis=0), right, NT)
        return both[:SRC_BLOCK], both[SRC_BLOCK : SRC_BLOCK + 8]

    def store(bucket, fresh, parts, degree):
        last = jnp.minimum(bucket, buckets - 1)
        outer, _ = block_of(last)
        wide = pl.ds(pl.multiple_of(outer * DST_BLOCK, DST_BLOCK), DST_BLOCK)
        base = lax.rem(last, src_blocks) * SRC_BLOCK
        for i in range(SRC_BLOCK // 256):
            rows = slice(i * 256, (i + 1) * 256)
            total = parts[rows] + jnp.where(fresh, 0.0, acc_ref[rows, :])
            acc_ref[rows, :] = total
            tall = pl.ds(pl.multiple_of(base + i * 256, 256), 256)
            held_ref[outer, tall, :] = total.astype(BF16)
        degree_ref[:, wide] += degree

    def advance(bucket, row):
        last = starts_ref[jnp.minimum(bucket + 1, buckets)]
        ended = (row + 4) * 128 >= last
        after = jnp.minimum(bucket + ended.astype(I32), buckets)
        return after, jnp.where(ended, lax.shift_right_logical(starts_ref[after], 7), row + 4), ended

    def body(carry):
        bucket, row, fresh = carry
        bucket1, row1, ended = advance(bucket, row)
        bucket2, row2, ended1 = advance(bucket1, row1)
        first = products(bucket, row)
        second = products(bucket1, row1)
        store(bucket, fresh == 1, *first)
        store(bucket1, jnp.logical_and(ended, bucket1 < buckets), *second)

        @pl.when(ended)
        def _():
            flush(bucket).start()

        @pl.when(jnp.logical_and(ended1, bucket1 < buckets))
        def _():
            flush(bucket1).start()

        return bucket2, row2, ended1.astype(I32)

    start = (jnp.int32(0), lax.shift_right_logical(starts_ref[0], 7), jnp.int32(1))
    lax.while_loop(lambda carry: carry[0] < buckets, body, start)
    pltpu.make_async_copy(held_ref, count_ref, sem).wait()


def edge_counts(starts, keys, nodes, table):
    blocks = nodes // DST_BLOCK
    return pl.pallas_call(
        functools.partial(edges_body, table // SRC_BLOCK),
        out_shape=(pltpu.HBM((blocks, table, DST_BLOCK), BF16), shape_of((8, nodes), F32)),
        in_specs=[whole(pltpu.SMEM), whole()],
        out_specs=(whole(pltpu.HBM), whole()),
        scratch_shapes=[
            pltpu.VMEM((blocks, table, DST_BLOCK), BF16),
            pltpu.VMEM((SRC_BLOCK, DST_BLOCK), F32),
            pltpu.SemaphoreType.DMA,
        ],
        compiler_params=limit(EDGES_MIB),
        cost_estimate=cost(14 * 10**9, 13 * 10**6),
        name="edge_counts",
    )(starts, keys)


def embed_body(
    count_ref, arrived_ref, feat_ref, degree_ref, self_ref, neigh_ref,
    served_ref, agg_ref, want_ref, held_ref, table_ref, emb_ref, sems,
):
    blocks = count_ref.shape[0]
    copies = [pltpu.make_async_copy(count_ref.at[i], held_ref.at[i], sems.at[i]) for i in range(blocks)]
    for copy in copies:
        copy.start()
    nodes = feat_ref.shape[0]
    table_ref[:, :nodes] = jnp.transpose(feat_ref[...])
    arrived = arrived_ref[...].astype(F32)
    halo = arrived[:, :8, :].reshape(-1, arrived.shape[2]).astype(BF16)
    table_ref[:, nodes:] = jnp.transpose(halo)
    notes = arrived[:, 8:, :]
    grouped = notes.reshape(notes.shape[0] // 8, 8, 8, notes.shape[2])
    summed = jnp.sum(grouped, axis=1)[:, 0, :]
    want = (summed[:, :128] * 128.0 + summed[:, 128:]).astype(I32)
    want_ref[...] = want
    columns = jnp.transpose(want)
    for at in range(0, nodes, DST_BLOCK):
        span = slice(at, at + DST_BLOCK)
        copies[at // DST_BLOCK].wait()
        sums = mm(table_ref[...], held_ref[at // DST_BLOCK])
        degree = jnp.sum(degree_ref[:, span], axis=0, keepdims=True)
        mean = (sums / jnp.maximum(degree, 1.0)).astype(BF16)
        mean = jnp.transpose(mean)
        agg_ref[span, :] = mean
        both = mm(feat_ref[span, :], self_ref[...]) + mm(mean, neigh_ref[...])
        emb_ref[span, :] = both.astype(BF16)
    for k in range(0, columns.shape[1], 8):
        tiles = [jnp.broadcast_to(columns[:, i : i + 1], (128, 128)) for i in range(k, k + 8)]
        hot = hot_tile(jnp.concatenate(tiles, axis=0), nodes)
        served_ref[k * 128 : (k + 8) * 128, :] = mm(hot, emb_ref[...]).astype(BF16)


def embed(counts, arrived, features, degree, w_self, w_neigh):
    blocks, table, _ = counts.shape
    nodes, width = features.shape
    return pl.pallas_call(
        embed_body,
        out_shape=(
            shape_of((nodes, width), BF16),
            shape_of((nodes, width), BF16),
            shape_of((16, 128), I32),
        ),
        in_specs=[whole(pltpu.HBM)] + [whole()] * 5,
        out_specs=(whole(),) * 3,
        scratch_shapes=[
            pltpu.VMEM(counts.shape, BF16),
            pltpu.VMEM((width, table), BF16),
            pltpu.VMEM((nodes, width), BF16),
            pltpu.SemaphoreType.DMA((blocks,)),
        ],
        compiler_params=limit(EMBED_MIB),
        cost_estimate=cost(6 * 10**9, 16 * 10**6),
        name="embed",
    )(counts, arrived, features, degree, w_self, w_neigh)


def decode_body(
    got_ref, ends_ref, label_ref, weight_ref, hid_ref, bias_ref, wout_ref,
    logit_ref, send_ref, both_ref, delta_ref, grad_ref, hidden_ref,
):
    rows, width = got_ref.shape
    pairs = ends_ref.shape[1]
    block = 256
    wide = 1024
    meta = jnp.concatenate(
        [
            ends_ref[...].astype(F32),
            label_ref[...].astype(F32),
            weight_ref[...],
            jnp.zeros((4, pairs), F32),
        ],
        axis=0,
    )
    cols = jnp.transpose(meta)
    ends = cols.astype(I32)
    for side in range(2):
        for at in range(0, pairs, wide):
            tile = jnp.broadcast_to(ends[at : at + wide, side : side + 1], (wide, 128))
            picked = mm(hot_tile(tile, rows), got_ref[...])
            both_ref[at : at + wide, side * width : (side + 1) * width] = picked.astype(BF16)
    bias_sum = jnp.zeros((8, width), F32)
    wout_sum = jnp.zeros((8, width), F32)
    for at in range(0, pairs, block):
        span = slice(at, at + block)
        pre = mm(both_ref[span, :], hid_ref[...]) + bias_ref[...]
        hidden = jnp.maximum(pre, 0.0)
        logits = jnp.sum(hidden * wout_ref[...], axis=1, keepdims=True)
        logit_ref[:, span] = jnp.transpose(jnp.broadcast_to(logits, (block, 128)))[0:1, :]
        slope = cols[span, 3:4] * (jax.nn.sigmoid(logits) - cols[span, 2:3])
        delta = jnp.where(pre > 0, slope * wout_ref[...], 0.0)
        bias_sum += jnp.sum(delta.reshape(block // 8, 8, width), axis=0)
        wout_sum += jnp.sum((slope * hidden).reshape(block // 8, 8, width), axis=0)
        delta = delta.astype(BF16)
        delta_ref[span, :] = delta
        grad_ref[span, :] = mm(delta, hid_ref[...], NT).astype(BF16)
    for at in range(0, rows, wide):
        grad = mm(hot_rows(ends_ref[0:1, :] - at, wide), grad_ref[:, :width])
        grad += mm(hot_rows(ends_ref[1:2, :] - at, wide), grad_ref[:, width:])
        send_ref[at // 16 : (at + wide) // 16, 0:16, :] = grad.reshape(-1, 16, width).astype(BF16)
    hidden_ref[...] = mm(both_ref[...], delta_ref[...], TN)
    bias = jnp.sum(bias_sum, axis=0, keepdims=True)
    wout = jnp.sum(wout_sum, axis=0, keepdims=True)
    lines = []
    for line in (bias, wout):
        high = line.astype(BF16).astype(F32)
        for half in (high, line - high):
            lines += [half[:, :128], half[:, 128:]]
    tail = jnp.concatenate(lines, axis=0)
    total = hidden_ref[...].reshape(-1, 8, width)
    tail = jnp.broadcast_to(tail[None], (total.shape[0], 8, 128))
    even = jnp.concatenate([total[:, :, :128], tail], axis=2)
    odd = jnp.concatenate([total[:, :, 128:], tail], axis=2)
    joined = jnp.stack([even, odd], axis=1).reshape(-1, 8, width)
    send_ref[:, 16:24, :] = joined.astype(BF16)


def decode(got, ends, labels, weights, w_hidden, bias, w_out, parts):
    rows, width = got.shape
    pairs = ends.shape[1]
    return pl.pallas_call(
        decode_body,
        out_shape=(shape_of((1, pairs), F32), shape_of((parts, 24, width), BF16)),
        in_specs=[whole()] * 7,
        out_specs=(whole(), whole()),
        scratch_shapes=[
            pltpu.VMEM((pairs, 2 * width), BF16),
            pltpu.VMEM((pairs, width), BF16),
            pltpu.VMEM((pairs, 2 * width), BF16),
            pltpu.VMEM((2 * width, width), F32),
        ],
        compiler_params=limit(DECODE_MIB),
        cost_estimate=cost(10 * 10**9, 4 * 10**6),
        name="decode",
    )(got, ends, labels, weights, w_hidden, bias, w_out)


def spread_body(
    count_ref, back_ref, want_ref, feat_ref, agg_ref, degree_ref, self_ref, neigh_ref,
    send_ref, direct_ref, small_ref, held_ref, grad_ref, mean_ref, sems,
):
    nodes, width = feat_ref.shape
    rows = 1024
    copies = []
    for i in range(count_ref.shape[1] // rows):
        part = (slice(None), slice(i * rows, (i + 1) * rows))
        copies.append(pltpu.make_async_copy(count_ref.at[part], held_ref.at[part], sems.at[i]))
        copies[-1].start()
    back = back_ref[...].astype(F32)
    tail = jnp.sum(back[:, 16:, :], axis=0)
    small_ref[...] = tail[:, 128:]
    flat = back[:, :16, :].reshape(-1, width).astype(BF16)
    want = jnp.concatenate([want_ref[k : k + 1, :] for k in range(16)], axis=1)
    for at in range(0, nodes, 1024):
        grad_ref[at : at + 1024, :] = mm(hot_rows(want - at, 1024), flat).astype(BF16)
    for at in range(0, nodes, 256):
        grad = grad_ref[at : at + 256, :]
        degree = jnp.sum(degree_ref[:, at : at + 256], axis=0, keepdims=True)
        column = jnp.transpose(jnp.broadcast_to(jnp.maximum(degree, 1.0), (128, 256)))
        scaled = mm(grad, neigh_ref[...], NT) / jnp.concatenate([column, column], axis=1)
        mean_ref[at : at + 256, :] = scaled.astype(BF16)
    both = jnp.concatenate(
        [mm(feat_ref[...], grad_ref[...], TN), mm(agg_ref[...], grad_ref[...], TN)], axis=0
    )
    both = both.reshape(-1, 8, width)
    tail = jnp.broadcast_to(tail[None, :, :128], (both.shape[0], 8, 128))
    even = jnp.concatenate([both[:, :, :128], tail], axis=2)
    odd = jnp.concatenate([both[:, :, 128:], tail], axis=2)
    joined = jnp.stack([even, odd], axis=1).reshape(-1, 8, width)
    send_ref[:, 8:16, :] = joined.astype(BF16)

    def table_rows(at):
        copies[at // rows].wait()
        blocks = range(0, nodes, DST_BLOCK)
        parts = [mm(held_ref[n // DST_BLOCK, at : at + rows, :], mean_ref[n : n + DST_BLOCK, :]) for n in blocks]
        return sum(parts[1:], parts[0])

    for at in range(0, nodes, rows):
        grad = mm(grad_ref[at : at + rows, :], self_ref[...], NT)
        direct_ref[at : at + rows, :] = grad + table_rows(at)
    for at in range(0, count_ref.shape[1] - nodes, rows):
        peers = rows // 8
        grad = table_rows(nodes + at).reshape(peers, 8, width)
        send_ref[at // 8 : at // 8 + peers, 0:8, :] = grad.astype(BF16)


def spread(counts, back, want, features, agg, degree, w_self, w_neigh):
    nodes, width = features.shape
    return pl.pallas_call(
        spread_body,
        out_shape=(
            shape_of((back.shape[0], 16, width), BF16),
            pltpu.HBM((nodes, width), F32),
            shape_of((8, 128), F32),
        ),
        in_specs=[whole(pltpu.HBM)] + [whole()] * 7,
        out_specs=(whole(),) * 3,
        scratch_shapes=[
            pltpu.VMEM(counts.shape, BF16),
            pltpu.VMEM((nodes, width), BF16),
            pltpu.VMEM((nodes, width), BF16),
            pltpu.SemaphoreType.DMA((counts.shape[1] // 1024,)),
        ],
        compiler_params=limit(SPREAD_MIB),
        cost_estimate=cost(7 * 10**9, 20 * 10**6),
        name="spread",
    )(counts, back, want, features, agg, degree, w_self, w_neigh)


def chunk_body(back_ref, out_ref):
    tail = jnp.sum(back_ref[:, 8:, :].astype(F32), axis=0)[:, :128]
    out_ref[...] = jnp.broadcast_to(tail[None], out_ref.shape).astype(BF16)


def chunk(back):
    return pl.pallas_call(
        chunk_body,
        out_shape=shape_of((back.shape[0], 8, 128), BF16),
        in_specs=[whole()],
        out_specs=whole(),
        compiler_params=limit(CHUNK_MIB),
        cost_estimate=cost(10**6, 10**6),
        name="chunk",
    )(back)


def join_lanes(pieces):
    pieces = pieces.reshape(-1, 2, 8, 128)
    return jnp.concatenate([pieces[:, 0], pieces[:, 1]], axis=2).reshape(-1, 256)


def final_body(
    direct_ref, back_ref, halo_ref, small_ref, out_ref, hidden_ref, bias_ref, wout_ref, held_ref, sems
):
    rows = 512
    copies = []
    for i in range(out_ref.shape[0] // rows):
        part = slice(i * rows, (i + 1) * rows)
        copies.append(pltpu.make_async_copy(direct_ref.at[part], held_ref.at[part], sems.at[i]))
        copies[-1].start()
    back = back_ref[...].astype(F32)
    width = back.shape[2]
    flat = back[:, :8, :].reshape(-1, width).astype(BF16)
    halo = jnp.concatenate([halo_ref[k : k + 1, :] for k in range(8)], axis=1)
    for i, copy in enumerate(copies):
        part = slice(i * rows, (i + 1) * rows)
        extra = mm(hot_rows(halo - i * rows, rows), flat)
        copy.wait()
        out_ref[part, :] = held_ref[part, :] + extra
    hidden_ref[...] = join_lanes(back[:, 8:, 128:])
    bias_ref[...] = small_ref[0:2, :] + small_ref[2:4, :]
    wout_ref[...] = small_ref[4:6, :] + small_ref[6:8, :]


def final(direct, back, halo, small):
    nodes, width = direct.shape
    return pl.pallas_call(
        final_body,
        out_shape=(
            shape_of((nodes, width), F32),
            shape_of((2 * width, width), F32),
            shape_of((2, 128), F32),
            shape_of((2, 128), F32),
        ),
        in_specs=[whole(pltpu.HBM)] + [whole()] * 3,
        out_specs=(whole(),) * 4,
        scratch_shapes=[
            pltpu.VMEM((nodes, width), F32),
            pltpu.SemaphoreType.DMA((nodes // 512,)),
        ],
        compiler_params=limit(FINAL_MIB),
        cost_estimate=cost(2 * 10**9, 6 * 10**6),
        name="final",
    )(direct, back, halo, small)


def weights_body(pieces_ref, self_ref, neigh_ref):
    both = join_lanes(pieces_ref[...].astype(F32))
    half = both.shape[0] // 2
    self_ref[...] = both[:half, :]
    neigh_ref[...] = both[half:, :]


def weights(pieces):
    shape = shape_of((256, 256), F32)
    return pl.pallas_call(
        weights_body,
        out_shape=(shape, shape),
        in_specs=[whole()],
        out_specs=(whole(), whole()),
        compiler_params=limit(WEIGHTS_MIB),
        cost_estimate=cost(10**6, 10**6),
        name="weights",
    )(pieces)


def exchange(rows):
    return lax.all_to_all(rows, AXES, split_axis=0, concat_axis=0, tiled=True)


def per_device(
    features, edge_src, edge_dst, edge_count, halo_index, request_rows, pair_ends,
    labels, pair_weight, w_self, w_neigh, w_hidden, b_hidden, w_out,
):
    nodes, width = features.shape
    parts, halo_len = halo_index.shape[1:]
    table = nodes + parts * halo_len
    slots = edge_src.shape[0]
    me = lax.axis_index("dom") * lax.axis_size("grp") + lax.axis_index("grp")

    sent = send_rows((me % 8).reshape(1), halo_index[0].T, request_rows[0].T, features)
    arrived = exchange(sent)

    src_blocks = table // SRC_BLOCK
    buckets = nodes // DST_BLOCK * src_blocks
    bucket = edge_dst // DST_BLOCK * src_blocks + edge_src // SRC_BLOCK
    packed = (bucket << 18) | ((edge_dst % DST_BLOCK) << 10) | (edge_src % SRC_BLOCK)
    live = jnp.arange(slots, dtype=I32) < edge_count[0]
    keys = jnp.where(live, packed, buckets << 18)
    bounds = jnp.arange(buckets + 1, dtype=I32) << 18
    starts = jnp.sum((keys[None, :] < bounds[:, None]).astype(I32), axis=1)
    keys = lax.sort(keys, is_stable=False)
    counts, degree = edge_counts(starts, keys.reshape(slots // 128, 128), nodes, table)

    counts = pltpu.with_memory_space_constraint(counts, pltpu.HBM)
    served, agg, want = embed(counts, arrived, features, degree, w_self, w_neigh)
    got = exchange(served.reshape(parts, -1, width)).reshape(-1, width)
    logits, pair_back = decode(
        got, pair_ends.T, labels.reshape(1, -1), pair_weight.reshape(1, -1),
        w_hidden, b_hidden.reshape(1, -1), w_out.reshape(1, -1), parts,
    )
    back = exchange(pair_back)
    halo_back, direct, small = spread(counts, back, want, features, agg, degree, w_self, w_neigh)
    direct = pltpu.with_memory_space_constraint(direct, pltpu.HBM)
    returned = exchange(halo_back)
    pieces = exchange(chunk(returned))
    grad_features, grad_hidden, grad_bias, grad_out = final(
        direct, returned, halo_index[0].reshape(8, -1), small
    )
    grad_self, grad_neigh = weights(pieces)
    return (
        logits.reshape(-1), grad_features, grad_self, grad_neigh, grad_hidden,
        grad_bias.reshape(-1), grad_out.reshape(-1),
    )


def solution(mesh):
    split, rows, cubes = P(AXES), P(AXES, None), P(AXES, None, None)
    in_specs = (
        rows, split, split, split, cubes, cubes, rows, split, split, P(), P(), P(), P(), P(),
    )
    out_specs = (split, rows, P(), P(), P(), P(), P())
    return jax.shard_map(
        per_device, mesh=mesh, in_specs=in_specs, out_specs=out_specs, check_vma=False
    )
```

time: 214 us -> 185 us (0.86)
  Pallas kernels: 86.6 us -> 62.9 us
  blocking collectives: 93.9 us -> 89 us
    pallas_call x3, Pallas kernels: 53.4 us -> 40.7 us  [the longest x1 13.7 us: spread(): pl.pallas_call(spread_body, out_shape=(shape_of((back.shape[0], 16, width...]
    pallas_call x1, Pallas kernels: 21.1 us -> 13.1 us  [decode(): pl.pallas_call(decode_body, out_shape=(shape_of((1, pairs), F32), shape_o...]
    all_to_all x3, blocking collectives: 93.9 us -> 89 us  [exchange(): return lax.all_to_all(rows, AXES, split_axis=0, concat_axis=0, tiled=True)]
  transfers between devices with their start and end apart: 2 -> 2, of which waited for: 1 -> 1; matrix products, arithmetic and copies ran while one was open for 4% -> 4% of each run, Pallas kernels for 12% -> 10%
where the time goes in v2:
time: 185 us; the launch traced here: 184 us
  blocking collectives  89 us (48%)
  Pallas kernels  62.9 us (34%)
  starting transfers between devices  15.4 us (8%)
  other arithmetic  6.9 us (4%)
  waiting for transfers between devices  5.86 us (3%)
  local copies, waits for them, and re-layouts  2.86 us (2%)
    all_to_all x3, blocking collectives, exchange(): return lax.all_to_all(rows, AXES, split_axis=0, concat_axis=0, tiled=True)  89 us
    all_to_all x2, starting transfers between devices, exchange(): return lax.all_to_all(rows, AXES, split_axis=0, concat_axis=0, tiled=True)  15.4 us
    pallas_call x1, Pallas kernels, spread(): pl.pallas_call(spread_body, out_shape=(shape_of((back.shape[0], 16, width...  13.7 us
    pallas_call x1, Pallas kernels, embed(): pl.pallas_call(embed_body, out_shape=(shape_of((nodes, width), BF16), sha...  13.7 us
    pallas_call x1, Pallas kernels, edge_counts(): pl.pallas_call(functools.partial(edges_body, table // SRC_BLOCK), out_sha...  13.3 us
    pallas_call x1, Pallas kernels, decode(): pl.pallas_call(decode_body, out_shape=(shape_of((1, pairs), F32), shape_o...  13.1 us
    sort x1, other arithmetic, per_device(): keys = lax.sort(keys, is_stable=False)  6.28 us
    all_to_all x2, waiting for transfers between devices, exchange(): return lax.all_to_all(rows, AXES, split_axis=0, concat_axis=0, tiled=True)  5.86 us
  transfers between devices with their start and end apart: 2, of which 1 were waited for; matrix products, arithmetic and copies ran while one was open for 4% of the time, Pallas kernels for 10%

profile of v2, /device:TPU:1, one launch (start us, length us, event | category | flops | bytes accessed | tf_op | source)
XLA Modules:
  0.0 184.4 jit_solution(1529756267816403394)
XLA Ops:
  0.6 0.0 copy-start
  0.7 0.7 copy-done
  1.3 0.0 copy-start.2
  1.3 1.2 copy-done.2
  2.6 0.0 copy-start.8
  2.6 0.7 copy-done.8
  3.3 0.0 copy-start.13
  3.3 0.0 copy-start.14
  3.3 2.3 %send_rows.1 = bf16[128,16,256]{2,1,0:T(8,128)(2,1)} custom-call(s32[1]{0:T(128)} %bitcast.2.slot_ref, s32[8,128]{1,0:T(8,128)S(1)} %bitcast.23, s32[16,128]{1,0:T(8,128)S(1)} %bitcast.25, bf16[2048,256]{1,0:T(8,128)(2,1)S(1)} %copy-done.2), custom_call_target="tpu_custom_call" | custom-call | flops 1000000000 | bytes 2000000 | tf_op jit(solution)/shard_map/send_rows/pallas_call | solution.py:81
  5.6 11.5 %all-to-all-start = ((bf16[128,16,256]{2,1,0:T(8,128)(2,1)}), bf16[128,16,256]{2,1,0:T(8,128)(2,1)S(1)}, u32[]{:S(2)}, u32[]{:S(2)}) async-start(bf16[128,16,256]{2,1,0:T(8,128)(2,1)} %send_rows.1), calls=%async_computation | async-start | bytes 2097152 | tf_op jit(solution)/shard_map/all_to_all | solution.py:479
  17.7 0.0 copy-done.13
  17.8 0.0 copy-done.14
  17.8 0.1 fusion.5
  17.9 6.3 %sort.7 = s32[16384]{0:T(1024)S(1)} sort(s32[16384]{0:T(1024)S(1)} %fusion.5), dimensions={0}, to_apply=%region_1.2 | sort | flops 229376 | bytes 131072 | tf_op jit(solution)/shard_map/sort | solution.py:503
  24.2 0.5 convert_reduce_fusion.starts_ref
  24.7 0.0 copy-start.3
  24.7 0.0 copy-start.5
  24.7 0.0 copy-start.6
  24.7 13.3 %edge_counts.1 = (bf16[8,3072,256]{2,1,0:T(8,128)(2,1)}, f32[8,2048]{1,0:T(8,128)S(1)}) custom-call(s32[25]{0:T(128)S(1)} %convert_reduce_fusion.starts_ref, s32[128,128]{1,0:T(8,128)S(1)} %bitcast.22), custom_call_target="tpu_custom_call" | custom-call | flops 14000000000 | bytes 13000000 | tf_op jit(solution)/shard_map/edge_counts/pallas_call | solution.py:164
  38.0 0.0 all-to-all-done.arrived_ref
  38.0 0.0 copy-done.3
  38.0 0.0 copy-done.5
  38.0 0.0 copy-done.6
  38.1 13.7 %embed.1 = (bf16[2048,256]{1,0:T(8,128)(2,1)S(1)}, bf16[2048,256]{1,0:T(8,128)(2,1)S(1)}, s32[16,128]{1,0:T(8,128)S(1)}) custom-call(bf16[8,3072,256]{2,1,0:T(8,128)(2,1)} %get-tuple-element.23.count_ref, bf16[128,16,256]{2,1,0:T(8,128)(2,1)S(1)} %all-to-all-done.arrived_ref, bf16[2048,256]{1,0:T(8,128)(2,1)S(1)} %copy-done.3, ...), custom_call_target="tpu_custom_call" | custom-call | flops 6000000000 | bytes 16000000 | tf_op jit(solution)/shard_map/embed/pallas_call | solution.py:218
  51.7 0.0 copy-start.4
  51.7 0.0 copy-start.7
  51.7 0.0 copy-start.9
  51.8 0.0 copy-start.10
  51.8 0.0 copy-start.11
  51.8 0.0 copy-start.12
  51.8 37.3 %all_to_all.25 = bf16[128,16,256]{2,1,0:T(8,128)(2,1)S(1)} all-to-all(bf16[128,16,256]{2,1,0:T(8,128)(2,1)S(1)} %bitcast.20), channel_id=1, replica_groups=mesh['dom'=32,'grp'=4] {'dom','grp'}, dimensions={0} | all-to-all | bytes 2097152 | tf_op jit(solution)/shard_map/all_to_all | solution.py:479
  89.1 0.0 copy-done.4
  89.1 0.0 copy-done.7
  89.1 0.0 copy-done.9
  89.1 0.0 copy-done.10
  89.1 0.0 copy-done.11
  89.1 0.0 copy-done.12
  89.1 13.1 %decode.1 = (f32[1,2048]{1,0:T(1,128)}, bf16[128,24,256]{2,1,0:T(8,128)(2,1)S(1)}) custom-call(bf16[2048,256]{1,0:T(8,128)(2,1)S(1)} %bitcast.21, s32[2,2048]{1,0:T(2,128)S(1)} %bitcast.24, s32[1,2048]{1,0:T(1,128)S(1)} %bitcast.26, f32[1,2048]{1,0:T(1,128)S(1)} %bitcast.27, bf16[512,256]{1,0:T(8,128)(2,1)S(1)} %copy-done.4, f32[1,256]{1,0:T(1,128)S(1)} %bitcast.28, ...), custom_call_target="tpu_custom_call" | custom-call | flops 10000000000 | bytes 4000000 | tf_op jit(solution)/shard_map/decode/pallas_call | solution.py:302
  102.2 28.8 %all_to_all.26.back_ref = bf16[128,24,256]{2,1,0:T(8,128)(2,1)S(1)} all-to-all(bf16[128,24,256]{2,1,0:T(8,128)(2,1)S(1)} %get-tuple-element.27), channel_id=1, replica_groups=mesh['dom'=32,'grp'=4] {'dom','grp'}, dimensions={0} | all-to-all | bytes 3145728 | tf_op jit(solution)/shard_map/all_to_all | solution.py:479
  131.1 13.7 %spread.1 = (bf16[128,16,256]{2,1,0:T(8,128)(2,1)S(1)}, f32[2048,256]{1,0:T(8,128)}, f32[8,128]{1,0:T(8,128)S(1)}) custom-call(bf16[8,3072,256]{2,1,0:T(8,128)(2,1)} %get-tuple-element.23.count_ref, bf16[128,24,256]{2,1,0:T(8,128)(2,1)S(1)} %all_to_all.26.back_ref, s32[16,128]{1,0:T(8,128)S(1)} %get-tuple-element.28.want_ref, ...), custom_call_target="tpu_custom_call" | custom-call | flops 7000000000 | bytes 20000000 | tf_op jit(solution)/shard_map/spread/pallas_call | solution.py:370
  144.8 0.0 copy-start.1
  144.8 22.9 %all_to_all.27.back_ref = bf16[128,16,256]{2,1,0:T(8,128)(2,1)S(1)} all-to-all(bf16[128,16,256]{2,1,0:T(8,128)(2,1)S(1)} %get-tuple-element.31), channel_id=1, replica_groups=mesh['dom'=32,'grp'=4] {'dom','grp'}, dimensions={0} | all-to-all | bytes 2097152 | tf_op jit(solution)/shard_map/all_to_all | solution.py:479
  167.7 0.9 chunk.1
  168.6 3.9 %all-to-all-start.4 = ((bf16[128,8,128]{2,1,0:T(8,128)(2,1)}), bf16[128,8,128]{2,1,0:T(8,128)(2,1)S(1)}, u32[]{:S(2)}, u32[]{:S(2)}) async-start(bf16[128,8,128]{2,1,0:T(8,128)(2,1)} %chunk.1), calls=%async_computation.4 | async-start | bytes 524288 | tf_op jit(solution)/shard_map/all_to_all | solution.py:479
  172.5 0.0 copy-done.1
  172.5 0.1 copy.23
  172.6 0.1 reshape_squeeze.3.halo_ref
  172.7 5.0 %final.1 = (f32[2048,256]{1,0:T(8,128)}, f32[512,256]{1,0:T(8,128)}, f32[2,128]{1,0:T(2,128)}, f32[2,128]{1,0:T(2,128)}) custom-call(f32[2048,256]{1,0:T(8,128)} %get-tuple-element.30.direct_ref, bf16[128,16,256]{2,1,0:T(8,128)(2,1)S(1)} %all_to_all.27.back_ref, s32[8,128]{1,0:T(8,128)S(1)} %reshape_squeeze.3.halo_ref, f32[8,128]{1,0:T(8,128)S(1)} %get-tuple-element.32.small_ref), custom_call_target="tpu_custom_call" | custom-call | flops 2000000000 | bytes 6000000 | tf_op jit(solution)/shard_map/final/pallas_call | solution.py:438
  177.8 5.9 %all-to-all-done.4.pieces_ref = bf16[128,8,128]{2,1,0:T(8,128)(2,1)S(1)} async-done(((bf16[128,8,128]{2,1,0:T(8,128)(2,1)}), bf16[128,8,128]{2,1,0:T(8,128)(2,1)S(1)}, u32[]{:S(2)}, u32[]{:S(2)}) %all-to-all-start.4) | async-done | bytes 262176 | tf_op jit(solution)/shard_map/all_to_all | solution.py:479
  183.6 0.8 weights.1
  (1 shorter events, 0.0 us)
Async XLA Ops:
  0.6 0.7 copy-start
  1.3 1.2 copy-start.2
  2.6 0.7 copy-start.8
  3.3 14.5 %copy-start.13 = (s32[16384]{0:T(1024)S(1)}, s32[16384]{0:T(1024)}, u32[]{:S(2)}) copy-start(s32[16384]{0:T(1024)} %param.16) | copy-start | bytes 196612
  3.3 14.5 %copy-start.14 = (s32[16384]{0:T(1024)S(1)}, s32[16384]{0:T(1024)}, u32[]{:S(2)}) copy-start(s32[16384]{0:T(1024)} %param.15) | copy-start | bytes 196612
  5.6 32.4 %all-to-all-start = ((bf16[128,16,256]{2,1,0:T(8,128)(2,1)}), bf16[128,16,256]{2,1,0:T(8,128)(2,1)S(1)}, u32[]{:S(2)}, u32[]{:S(2)}) async-start(bf16[128,16,256]{2,1,0:T(8,128)(2,1)} %send_rows.1), calls=%async_computation | async-start | bytes 2097152 | tf_op jit(solution)/shard_map/all_to_all | solution.py:479
  24.7 13.4 %copy-start.3 = (bf16[2048,256]{1,0:T(8,128)(2,1)S(1)}, bf16[2048,256]{1,0:T(8,128)(2,1)}, u32[]{:S(2)}) copy-start(bf16[2048,256]{1,0:T(8,128)(2,1)} %feat_ref.5) | copy-start | bytes 3145732
  24.7 13.4 %copy-start.5 = (bf16[256,256]{1,0:T(8,128)(2,1)S(1)}, bf16[256,256]{1,0:T(8,128)(2,1)}, u32[]{:S(2)}) copy-start(bf16[256,256]{1,0:T(8,128)(2,1)} %self_ref.3) | copy-start | bytes 393220
  24.7 13.4 %copy-start.6 = (bf16[256,256]{1,0:T(8,128)(2,1)S(1)}, bf16[256,256]{1,0:T(8,128)(2,1)}, u32[]{:S(2)}) copy-start(bf16[256,256]{1,0:T(8,128)(2,1)} %neigh_ref.3) | copy-start | bytes 393220
  51.7 37.3 %copy-start.4 = (bf16[512,256]{1,0:T(8,128)(2,1)S(1)}, bf16[512,256]{1,0:T(8,128)(2,1)}, u32[]{:S(2)}) copy-start(bf16[512,256]{1,0:T(8,128)(2,1)} %hid_ref.1) | copy-start | bytes 786436
  51.7 37.3 %copy-start.7 = (s32[2048,2]{0,1:T(2,128)S(1)}, s32[2048,2]{0,1:T(2,128)}, u32[]{:S(2)}) copy-start(s32[2048,2]{0,1:T(2,128)} %param.20) | copy-start | bytes 49156
  51.7 37.3 %copy-start.9 = (s32[2048]{0:T(1024)S(1)}, s32[2048]{0:T(1024)}, u32[]{:S(2)}) copy-start(s32[2048]{0:T(1024)} %param.21) | copy-start | bytes 24580
  51.8 37.3 %copy-start.10 = (f32[2048]{0:T(1024)S(1)}, f32[2048]{0:T(1024)}, u32[]{:S(2)}) copy-start(f32[2048]{0:T(1024)} %param.22) | copy-start | bytes 24580
  51.8 37.3 %copy-start.11 = (f32[256]{0:T(256)S(1)}, f32[256]{0:T(256)}, u32[]{:S(2)}) copy-start(f32[256]{0:T(256)} %param.26) | copy-start | bytes 3076
  51.8 37.3 %copy-start.12 = (f32[256]{0:T(256)S(1)}, f32[256]{0:T(256)}, u32[]{:S(2)}) copy-start(f32[256]{0:T(256)} %param.27) | copy-start | bytes 3076
  144.8 27.7 %copy-start.1 = (s32[1,128,8]{1,2,0:T(8,128)S(1)}, s32[1,128,8]{1,2,0:T(8,128)}, u32[]{:S(2)}) copy-start(s32[1,128,8]{1,2,0:T(8,128)} %param.18) | copy-start | bytes 12292
  168.6 15.0 %all-to-all-start.4 = ((bf16[128,8,128]{2,1,0:T(8,128)(2,1)}), bf16[128,8,128]{2,1,0:T(8,128)(2,1)S(1)}, u32[]{:S(2)}, u32[]{:S(2)}) async-start(bf16[128,8,128]{2,1,0:T(8,128)(2,1)} %chunk.1), calls=%async_computation.4 | async-start | bytes 524288 | tf_op jit(solution)/shard_map/all_to_all | solution.py:479

commit v3 on v2

--- a/solution.py
+++ b/solution.py
@@ -13,8 +13,10 @@
 TN = (((0,), (0,)), ((), ()))
 AXES = ("dom", "grp")
 DST_BLOCK = 256
-SRC_BLOCK = 1024
-SEND_MIB, EDGES_MIB, EMBED_MIB, DECODE_MIB, SPREAD_MIB = 8, 24, 24, 16, 24
+SRC_BLOCK = 256
+VISITS = 8
+UNROLL = 2
+SEND_MIB, EDGES_MIB, EMBED_MIB, DECODE_MIB, SPREAD_MIB = 8, 24, 24, 16, 20
 CHUNK_MIB, FINAL_MIB, WEIGHTS_MIB = 8, 16, 8
 
 
@@ -38,9 +40,16 @@
     return spread_hot(wide.astype(I16), 16, height // 16, 0)
 
 
+def lane_diff(tile):
+    return (tile - lax.broadcasted_iota(I32, tile.shape, 1)).astype(I16)
+
+
+def hot_lanes(diff, width):
+    return spread_hot(diff, 128, width // 128, 1)
+
+
 def hot_tile(tile, width):
-    diff = tile - lax.broadcasted_iota(I32, tile.shape, 1)
-    return spread_hot(diff.astype(I16), 128, width // 128, 1)
+    return hot_lanes(lane_diff(tile), width)
 
 
 def whole(memory_space=pltpu.VMEM):
@@ -66,14 +75,12 @@
         [lax.shift_right_logical(tiled, 7).astype(F32), (tiled & 127).astype(F32)], axis=1
     )
     halo = halo_ref[...]
-    for at in range(0, parts, 16):
-        tile = jnp.concatenate(
-            [jnp.broadcast_to(halo[:, p : p + 1], (8, 128)) for p in range(at, at + 16)], axis=0
-        )
-        rows = mm(hot_tile(tile, feat_ref.shape[0]), feat_ref[...])
-        rows = rows.reshape(16, 8, rows.shape[1])
-        notes = jnp.broadcast_to(index[at : at + 16, None, :], rows.shape)
-        out_ref[at : at + 16] = jnp.concatenate([rows, notes], axis=1).astype(BF16)
+    tiles = [jnp.broadcast_to(halo[:, p : p + 1], (8, 128)) for p in range(parts)]
+    diff = lane_diff(jnp.concatenate(tiles, axis=0))
+    rows = mm(hot_lanes(diff, feat_ref.shape[0]), feat_ref[...])
+    rows = rows.reshape(parts, 8, rows.shape[1])
+    notes = jnp.broadcast_to(index[:, None, :], rows.shape)
+    out_ref[...] = jnp.concatenate([rows, notes], axis=1).astype(BF16)
 
 
 def send_rows(slot, halo, want, features):
@@ -137,22 +144,21 @@
 
     def body(carry):
         bucket, row, fresh = carry
-        bucket1, row1, ended = advance(bucket, row)
-        bucket2, row2, ended1 = advance(bucket1, row1)
-        first = products(bucket, row)
-        second = products(bucket1, row1)
-        store(bucket, fresh == 1, *first)
-        store(bucket1, jnp.logical_and(ended, bucket1 < buckets), *second)
-
-        @pl.when(ended)
-        def _():
-            flush(bucket).start()
-
-        @pl.when(jnp.logical_and(ended1, bucket1 < buckets))
-        def _():
-            flush(bucket1).start()
-
-        return bucket2, row2, ended1.astype(I32)
+        visits = []
+        for _ in range(VISITS):
+            after, following, ended = advance(bucket, row)
+            visits.append((bucket, row, fresh == 1, ended))
+            bucket, row = after, following
+            fresh = jnp.logical_and(ended, bucket < buckets).astype(I32)
+        made = [products(*visit[:2]) for visit in visits]
+        for visit, both in zip(visits, made):
+            store(visit[0], visit[2], *both)
+        for visit in visits:
+            @pl.when(jnp.logical_and(visit[3], visit[0] < buckets))
+            def _(visit=visit):
+                flush(visit[0]).start()
+
+        return bucket, row, fresh
 
     start = (jnp.int32(0), lax.shift_right_logical(starts_ref[0], 7), jnp.int32(1))
     lax.while_loop(lambda carry: carry[0] < buckets, body, start)
@@ -196,16 +202,19 @@
     want = (summed[:, :128] * 128.0 + summed[:, 128:]).astype(I32)
     want_ref[...] = want
     columns = jnp.transpose(want)
-    for at in range(0, nodes, DST_BLOCK):
-        span = slice(at, at + DST_BLOCK)
-        copies[at // DST_BLOCK].wait()
-        sums = mm(table_ref[...], held_ref[at // DST_BLOCK])
+    def node_block(i, carry):
+        span = pl.ds(pl.multiple_of(i * DST_BLOCK, DST_BLOCK), DST_BLOCK)
+        pltpu.make_async_copy(count_ref.at[i], held_ref.at[i], sems.at[i]).wait()
+        sums = mm(table_ref[...], held_ref[i])
         degree = jnp.sum(degree_ref[:, span], axis=0, keepdims=True)
         mean = (sums / jnp.maximum(degree, 1.0)).astype(BF16)
         mean = jnp.transpose(mean)
         agg_ref[span, :] = mean
         both = mm(feat_ref[span, :], self_ref[...]) + mm(mean, neigh_ref[...])
         emb_ref[span, :] = both.astype(BF16)
+        return carry
+
+    lax.fori_loop(0, nodes // DST_BLOCK, node_block, 0)
     for k in range(0, columns.shape[1], 8):
         tiles = [jnp.broadcast_to(columns[:, i : i + 1], (128, 128)) for i in range(k, k + 8)]
         hot = hot_tile(jnp.concatenate(tiles, axis=0), nodes)
@@ -318,28 +327,33 @@
 
 def spread_body(
     count_ref, back_ref, want_ref, feat_ref, agg_ref, degree_ref, self_ref, neigh_ref,
-    send_ref, direct_ref, small_ref, held_ref, grad_ref, mean_ref, sems,
+    send_ref, direct_ref, small_ref, grad_ref, mean_ref,
 ):
     nodes, width = feat_ref.shape
     rows = 1024
-    copies = []
-    for i in range(count_ref.shape[1] // rows):
-        part = (slice(None), slice(i * rows, (i + 1) * rows))
-        copies.append(pltpu.make_async_copy(count_ref.at[part], held_ref.at[part], sems.at[i]))
-        copies[-1].start()
     back = back_ref[...].astype(F32)
     tail = jnp.sum(back[:, 16:, :], axis=0)
     small_ref[...] = tail[:, 128:]
     flat = back[:, :16, :].reshape(-1, width).astype(BF16)
     want = jnp.concatenate([want_ref[k : k + 1, :] for k in range(16)], axis=1)
-    for at in range(0, nodes, 1024):
-        grad_ref[at : at + 1024, :] = mm(hot_rows(want - at, 1024), flat).astype(BF16)
-    for at in range(0, nodes, 256):
-        grad = grad_ref[at : at + 256, :]
-        degree = jnp.sum(degree_ref[:, at : at + 256], axis=0, keepdims=True)
+
+    def gather(i, carry):
+        at = i * rows
+        span = pl.ds(pl.multiple_of(at, rows), rows)
+        grad_ref[span, :] = mm(hot_rows(want - at, rows), flat).astype(BF16)
+        return carry
+
+    lax.fori_loop(0, nodes // rows, gather, 0)
+
+    def scale(i, carry):
+        span = pl.ds(pl.multiple_of(i * 256, 256), 256)
+        degree = jnp.sum(degree_ref[:, span], axis=0, keepdims=True)
         column = jnp.transpose(jnp.broadcast_to(jnp.maximum(degree, 1.0), (128, 256)))
-        scaled = mm(grad, neigh_ref[...], NT) / jnp.concatenate([column, column], axis=1)
-        mean_ref[at : at + 256, :] = scaled.astype(BF16)
+        scaled = mm(grad_ref[span, :], neigh_ref[...], NT) / jnp.concatenate([column, column], axis=1)
+        mean_ref[span, :] = scaled.astype(BF16)
+        return carry
+
+    lax.fori_loop(0, nodes // 256, scale, 0, unroll=UNROLL)
     both = jnp.concatenate(
         [mm(feat_ref[...], grad_ref[...], TN), mm(agg_ref[...], grad_ref[...], TN)], axis=0
     )
@@ -351,14 +365,17 @@
     send_ref[:, 8:16, :] = joined.astype(BF16)
 
     def table_rows(at):
-        copies[at // rows].wait()
         blocks = range(0, nodes, DST_BLOCK)
-        parts = [mm(held_ref[n // DST_BLOCK, at : at + rows, :], mean_ref[n : n + DST_BLOCK, :]) for n in blocks]
+        span = pl.ds(pl.multiple_of(at, rows), rows)
+        parts = [mm(count_ref[n // DST_BLOCK, span, :], mean_ref[n : n + DST_BLOCK, :]) for n in blocks]
         return sum(parts[1:], parts[0])
 
-    for at in range(0, nodes, rows):
-        grad = mm(grad_ref[at : at + rows, :], self_ref[...], NT)
-        direct_ref[at : at + rows, :] = grad + table_rows(at)
+    def own(i, carry):
+        span = pl.ds(pl.multiple_of(i * rows, rows), rows)
+        direct_ref[span, :] = mm(grad_ref[span, :], self_ref[...], NT) + table_rows(i * rows)
+        return carry
+
+    lax.fori_loop(0, nodes // rows, own, 0)
     for at in range(0, count_ref.shape[1] - nodes, rows):
         peers = rows // 8
         grad = table_rows(nodes + at).reshape(peers, 8, width)
@@ -374,14 +391,9 @@
             pltpu.HBM((nodes, width), F32),
             shape_of((8, 128), F32),
         ),
-        in_specs=[whole(pltpu.HBM)] + [whole()] * 7,
+        in_specs=[whole()] * 8,
         out_specs=(whole(),) * 3,
-        scratch_shapes=[
-            pltpu.VMEM(counts.shape, BF16),
-            pltpu.VMEM((nodes, width), BF16),
-            pltpu.VMEM((nodes, width), BF16),
-            pltpu.SemaphoreType.DMA((counts.shape[1] // 1024,)),
-        ],
+        scratch_shapes=[pltpu.VMEM((nodes, width), BF16), pltpu.VMEM((nodes, width), BF16)],
         compiler_params=limit(SPREAD_MIB),
         cost_estimate=cost(7 * 10**9, 20 * 10**6),
         name="spread",
@@ -423,11 +435,15 @@
     width = back.shape[2]
     flat = back[:, :8, :].reshape(-1, width).astype(BF16)
     halo = jnp.concatenate([halo_ref[k : k + 1, :] for k in range(8)], axis=1)
-    for i, copy in enumerate(copies):
-        part = slice(i * rows, (i + 1) * rows)
+
+    def add(i, carry):
+        part = pl.ds(pl.multiple_of(i * rows, rows), rows)
         extra = mm(hot_rows(halo - i * rows, rows), flat)
-        copy.wait()
+        pltpu.make_async_copy(direct_ref.at[part], held_ref.at[part], sems.at[i]).wait()
         out_ref[part, :] = held_ref[part, :] + extra
+        return carry
+
+    lax.fori_loop(0, len(copies), add, 0)
     hidden_ref[...] = join_lanes(back[:, 8:, 128:])
     bias_ref[...] = small_ref[0:2, :] + small_ref[2:4, :]
     wout_ref[...] = small_ref[4:6, :] + small_ref[6:8, :]
@@ -503,8 +519,8 @@
     keys = lax.sort(keys, is_stable=False)
     counts, degree = edge_counts(starts, keys.reshape(slots // 128, 128), nodes, table)
 
-    counts = pltpu.with_memory_space_constraint(counts, pltpu.HBM)
-    served, agg, want = embed(counts, arrived, features, degree, w_self, w_neigh)
+    fixed = pltpu.with_memory_space_constraint(counts, pltpu.HBM)
+    served, agg, want = embed(fixed, arrived, features, degree, w_self, w_neigh)
     got = exchange(served.reshape(parts, -1, width)).reshape(-1, width)
     logits, pair_back = decode(
         got, pair_ends.T, labels.reshape(1, -1), pair_weight.reshape(1, -1),

time: 185 us -> 169 us (0.914)
  Pallas kernels: 62.9 us -> 53.7 us
  blocking collectives: 89 us -> 80.4 us
    all_to_all x3, blocking collectives: 89 us -> 80.4 us  [exchange(): return lax.all_to_all(rows, AXES, split_axis=0, concat_axis=0, tiled=True)]
    pallas_call x1, Pallas kernels: 13.7 us -> 8.64 us  [spread(): pl.pallas_call(spread_body, out_shape=(shape_of((back.shape[0], 16, width...]
    pallas_call x1, Pallas kernels: 13.7 us -> 11.4 us  [embed(): pl.pallas_call(embed_body, out_shape=(shape_of((nodes, width), BF16), sha...]
  transfers between devices with their start and end apart: 2 -> 2, of which waited for: 1 -> 1; matrix products, arithmetic and copies ran while one was open for 4% -> 5% of each run, Pallas kernels for 10% -> 10%
where the time goes in v3:
time: 169 us; the launch traced here: 168 us
  blocking collectives  80.4 us (48%)
  Pallas kernels  53.7 us (32%)
  starting transfers between devices  15.4 us (9%)
  other arithmetic  7.45 us (4%)
  waiting for transfers between devices  6.82 us (4%)
  local copies, waits for them, and re-layouts  2.88 us (2%)
    all_to_all x3, blocking collectives, exchange(): return lax.all_to_all(rows, AXES, split_axis=0, concat_axis=0, tiled=True)  80.4 us
    all_to_all x2, starting transfers between devices, exchange(): return lax.all_to_all(rows, AXES, split_axis=0, concat_axis=0, tiled=True)  15.4 us
    pallas_call x1, Pallas kernels, decode(): pl.pallas_call(decode_body, out_shape=(shape_of((1, pairs), F32), shape_o...  13.1 us
    pallas_call x1, Pallas kernels, edge_counts(): pl.pallas_call(functools.partial(edges_body, table // SRC_BLOCK), out_sha...  12.4 us
    pallas_call x1, Pallas kernels, embed(): pl.pallas_call(embed_body, out_shape=(shape_of((nodes, width), BF16), sha...  11.4 us
    pallas_call x1, Pallas kernels, spread(): pl.pallas_call(spread_body, out_shape=(shape_of((back.shape[0], 16, width...  8.64 us
    all_to_all x2, waiting for transfers between devices, exchange(): return lax.all_to_all(rows, AXES, split_axis=0, concat_axis=0, tiled=True)  6.82 us
    sort x1, other arithmetic, per_device(): keys = lax.sort(keys, is_stable=False)  6.28 us
  transfers between devices with their start and end apart: 2, of which 1 were waited for; matrix products, arithmetic and copies ran while one was open for 5% of the time, Pallas kernels for 10%

profile of v3, /device:TPU:1, one launch (start us, length us, event | category | flops | bytes accessed | tf_op | source)
XLA Modules:
  0.0 168.2 jit_solution(1211417463525505012)
XLA Ops:
  0.6 0.0 copy-start
  0.7 0.7 copy-done
  1.3 0.0 copy-start.2
  1.3 1.2 copy-done.2
  2.6 0.0 copy-start.8
  2.6 0.7 copy-done.8
  3.3 0.0 copy-start.13
  3.3 0.0 copy-start.14
  3.3 2.3 %send_rows.1 = bf16[128,16,256]{2,1,0:T(8,128)(2,1)} custom-call(s32[1]{0:T(128)} %bitcast.2.slot_ref, s32[8,128]{1,0:T(8,128)S(1)} %bitcast.23, s32[16,128]{1,0:T(8,128)S(1)} %bitcast.25, bf16[2048,256]{1,0:T(8,128)(2,1)S(1)} %copy-done.2), custom_call_target="tpu_custom_call" | custom-call | flops 1000000000 | bytes 2000000 | tf_op jit(solution)/shard_map/send_rows/pallas_call | solution.py:88
  5.6 11.5 %all-to-all-start = ((bf16[128,16,256]{2,1,0:T(8,128)(2,1)}), bf16[128,16,256]{2,1,0:T(8,128)(2,1)S(1)}, u32[]{:S(2)}, u32[]{:S(2)}) async-start(bf16[128,16,256]{2,1,0:T(8,128)(2,1)} %send_rows.1), calls=%async_computation | async-start | bytes 2097152 | tf_op jit(solution)/shard_map/all_to_all | solution.py:495
  17.7 0.0 copy-done.13
  17.7 0.0 copy-done.14
  17.8 0.1 fusion.5
  17.9 6.3 %sort.7 = s32[16384]{0:T(1024)S(1)} sort(s32[16384]{0:T(1024)S(1)} %fusion.5), dimensions={0}, to_apply=%region_1.2 | sort | flops 229376 | bytes 131072 | tf_op jit(solution)/shard_map/sort | solution.py:519
  24.2 1.0 convert_reduce_fusion.starts_ref
  25.2 0.0 copy-start.3
  25.2 0.0 copy-start.5
  25.2 0.0 copy-start.6
  25.3 12.4 %edge_counts.1 = (bf16[8,3072,256]{2,1,0:T(8,128)(2,1)}, f32[8,2048]{1,0:T(8,128)S(1)}) custom-call(s32[97]{0:T(128)S(1)} %convert_reduce_fusion.starts_ref, s32[128,128]{1,0:T(8,128)S(1)} %bitcast.22), custom_call_target="tpu_custom_call" | custom-call | flops 14000000000 | bytes 13000000 | tf_op jit(solution)/shard_map/edge_counts/pallas_call | solution.py:170
  37.7 0.0 all-to-all-done.arrived_ref
  37.7 0.0 copy-done.3
  37.7 0.0 copy-done.5
  37.7 0.0 copy-done.6
  37.7 11.4 %embed.1 = (bf16[2048,256]{1,0:T(8,128)(2,1)S(1)}, bf16[2048,256]{1,0:T(8,128)(2,1)S(1)}, s32[16,128]{1,0:T(8,128)S(1)}) custom-call(bf16[8,3072,256]{2,1,0:T(8,128)(2,1)} %get-tuple-element.23.count_ref, bf16[128,16,256]{2,1,0:T(8,128)(2,1)S(1)} %all-to-all-done.arrived_ref, bf16[2048,256]{1,0:T(8,128)(2,1)S(1)} %copy-done.3, ...), custom_call_target="tpu_custom_call" | custom-call | flops 6000000000 | bytes 16000000 | tf_op jit(solution)/shard_map/embed/pallas_call | solution.py:227
  49.1 0.0 copy-start.4
  49.1 0.0 copy-start.7
  49.2 0.0 copy-start.9
  49.2 0.0 copy-start.10
  49.2 0.0 copy-start.11
  49.2 0.0 copy-start.12
  49.2 0.0 slice-start
  49.2 28.6 %all_to_all.25 = bf16[128,16,256]{2,1,0:T(8,128)(2,1)S(1)} all-to-all(bf16[128,16,256]{2,1,0:T(8,128)(2,1)S(1)} %bitcast.20), channel_id=1, replica_groups=mesh['dom'=32,'grp'=4] {'dom','grp'}, dimensions={0} | all-to-all | bytes 2097152 | tf_op jit(solution)/shard_map/all_to_all | solution.py:495
  77.9 0.0 copy-done.4
  77.9 0.0 copy-done.7
  77.9 0.0 copy-done.9
  77.9 0.0 copy-done.10
  77.9 0.0 copy-done.11
  77.9 0.0 copy-done.12
  77.9 0.0 slice-start.1
  77.9 0.0 slice-start.2
  77.9 13.1 %decode.1 = (f32[1,2048]{1,0:T(1,128)}, bf16[128,24,256]{2,1,0:T(8,128)(2,1)S(1)}) custom-call(bf16[2048,256]{1,0:T(8,128)(2,1)S(1)} %bitcast.21, s32[2,2048]{1,0:T(2,128)S(1)} %bitcast.24, s32[1,2048]{1,0:T(1,128)S(1)} %bitcast.26, f32[1,2048]{1,0:T(1,128)S(1)} %bitcast.27, bf16[512,256]{1,0:T(8,128)(2,1)S(1)} %copy-done.4, f32[1,256]{1,0:T(1,128)S(1)} %bitcast.28, ...), custom_call_target="tpu_custom_call" | custom-call | flops 10000000000 | bytes 4000000 | tf_op jit(solution)/shard_map/decode/pallas_call | solution.py:311
  91.0 28.9 %all_to_all.26.back_ref = bf16[128,24,256]{2,1,0:T(8,128)(2,1)S(1)} all-to-all(bf16[128,24,256]{2,1,0:T(8,128)(2,1)S(1)} %get-tuple-element.27), channel_id=1, replica_groups=mesh['dom'=32,'grp'=4] {'dom','grp'}, dimensions={0} | all-to-all | bytes 3145728 | tf_op jit(solution)/shard_map/all_to_all | solution.py:495
  119.9 0.0 slice-done
  119.9 0.0 slice-done.1
  119.9 0.0 slice-done.2
  119.9 8.6 %spread.1 = (bf16[128,16,256]{2,1,0:T(8,128)(2,1)S(1)}, f32[2048,256]{1,0:T(8,128)}, f32[8,128]{1,0:T(8,128)S(1)}) custom-call(bf16[8,3072,256]{2,1,0:T(8,128)(2,1)S(1)} %bitcast.31, bf16[128,24,256]{2,1,0:T(8,128)(2,1)S(1)} %all_to_all.26.back_ref, s32[16,128]{1,0:T(8,128)S(1)} %get-tuple-element.28.want_ref, bf16[2048,256]{1,0:T(8,128)(2,1)S(1)} %copy-done.3, ...), custom_call_target="tpu_custom_call" | custom-call | flops 7000000000 | bytes 20000000 | tf_op jit(solution)/shard_map/spread/pallas_call | solution.py:387
  128.6 0.0 copy-start.1
  128.6 22.9 %all_to_all.27.back_ref = bf16[128,16,256]{2,1,0:T(8,128)(2,1)S(1)} all-to-all(bf16[128,16,256]{2,1,0:T(8,128)(2,1)S(1)} %get-tuple-element.31), channel_id=1, replica_groups=mesh['dom'=32,'grp'=4] {'dom','grp'}, dimensions={0} | all-to-all | bytes 2097152 | tf_op jit(solution)/shard_map/all_to_all | solution.py:495
  151.5 0.9 chunk.1
  152.4 3.9 %all-to-all-start.4 = ((bf16[128,8,128]{2,1,0:T(8,128)(2,1)}), bf16[128,8,128]{2,1,0:T(8,128)(2,1)S(1)}, u32[]{:S(2)}, u32[]{:S(2)}) async-start(bf16[128,8,128]{2,1,0:T(8,128)(2,1)} %chunk.1), calls=%async_computation.4 | async-start | bytes 524288 | tf_op jit(solution)/shard_map/all_to_all | solution.py:495
  156.3 0.0 copy-done.1
  156.3 0.1 copy.23
  156.4 0.1 reshape_squeeze.3.halo_ref
  156.5 4.1 %final.1 = (f32[2048,256]{1,0:T(8,128)}, f32[512,256]{1,0:T(8,128)}, f32[2,128]{1,0:T(2,128)}, f32[2,128]{1,0:T(2,128)}) custom-call(f32[2048,256]{1,0:T(8,128)} %get-tuple-element.30.direct_ref, bf16[128,16,256]{2,1,0:T(8,128)(2,1)S(1)} %all_to_all.27.back_ref, s32[8,128]{1,0:T(8,128)S(1)} %reshape_squeeze.3.halo_ref, f32[8,128]{1,0:T(8,128)S(1)} %get-tuple-element.32.small_ref), custom_call_target="tpu_custom_call" | custom-call | flops 2000000000 | bytes 6000000 | tf_op jit(solution)/shard_map/final/pallas_call | solution.py:454
  160.6 6.8 %all-to-all-done.4.pieces_ref = bf16[128,8,128]{2,1,0:T(8,128)(2,1)S(1)} async-done(((bf16[128,8,128]{2,1,0:T(8,128)(2,1)}), bf16[128,8,128]{2,1,0:T(8,128)(2,1)S(1)}, u32[]{:S(2)}, u32[]{:S(2)}) %all-to-all-start.4) | async-done | bytes 262176 | tf_op jit(solution)/shard_map/all_to_all | solution.py:495
  167.4 0.8 weights.1
  (2 shorter events, 0.0 us)
Async XLA Ops:
  0.6 0.7 copy-start
  1.3 1.2 copy-start.2
  2.6 0.7 copy-start.8
  3.3 14.5 %copy-start.13 = (s32[16384]{0:T(1024)S(1)}, s32[16384]{0:T(1024)}, u32[]{:S(2)}) copy-start(s32[16384]{0:T(1024)} %param.16) | copy-start | bytes 196612
  3.3 14.5 %copy-start.14 = (s32[16384]{0:T(1024)S(1)}, s32[16384]{0:T(1024)}, u32[]{:S(2)}) copy-start(s32[16384]{0:T(1024)} %param.15) | copy-start | bytes 196612
  5.6 32.1 %all-to-all-start = ((bf16[128,16,256]{2,1,0:T(8,128)(2,1)}), bf16[128,16,256]{2,1,0:T(8,128)(2,1)S(1)}, u32[]{:S(2)}, u32[]{:S(2)}) async-start(bf16[128,16,256]{2,1,0:T(8,128)(2,1)} %send_rows.1), calls=%async_computation | async-start | bytes 2097152 | tf_op jit(solution)/shard_map/all_to_all | solution.py:495
  25.2 12.5 %copy-start.3 = (bf16[2048,256]{1,0:T(8,128)(2,1)S(1)}, bf16[2048,256]{1,0:T(8,128)(2,1)}, u32[]{:S(2)}) copy-start(bf16[2048,256]{1,0:T(8,128)(2,1)} %feat_ref.5) | copy-start | bytes 3145732
  25.2 12.5 %copy-start.5 = (bf16[256,256]{1,0:T(8,128)(2,1)S(1)}, bf16[256,256]{1,0:T(8,128)(2,1)}, u32[]{:S(2)}) copy-start(bf16[256,256]{1,0:T(8,128)(2,1)} %self_ref.3) | copy-start | bytes 393220
  25.2 12.5 %copy-start.6 = (bf16[256,256]{1,0:T(8,128)(2,1)S(1)}, bf16[256,256]{1,0:T(8,128)(2,1)}, u32[]{:S(2)}) copy-start(bf16[256,256]{1,0:T(8,128)(2,1)} %neigh_ref.3) | copy-start | bytes 393220
  49.1 28.7 %copy-start.4 = (bf16[512,256]{1,0:T(8,128)(2,1)S(1)}, bf16[512,256]{1,0:T(8,128)(2,1)}, u32[]{:S(2)}) copy-start(bf16[512,256]{1,0:T(8,128)(2,1)} %hid_ref.1) | copy-start | bytes 786436
  49.1 28.7 %copy-start.7 = (s32[2048,2]{0,1:T(2,128)S(1)}, s32[2048,2]{0,1:T(2,128)}, u32[]{:S(2)}) copy-start(s32[2048,2]{0,1:T(2,128)} %param.20) | copy-start | bytes 49156
  49.2 28.7 %copy-start.9 = (s32[2048]{0:T(1024)S(1)}, s32[2048]{0:T(1024)}, u32[]{:S(2)}) copy-start(s32[2048]{0:T(1024)} %param.21) | copy-start | bytes 24580
  49.2 28.7 %copy-start.10 = (f32[2048]{0:T(1024)S(1)}, f32[2048]{0:T(1024)}, u32[]{:S(2)}) copy-start(f32[2048]{0:T(1024)} %param.22) | copy-start | bytes 24580
  49.2 28.7 %copy-start.11 = (f32[256]{0:T(256)S(1)}, f32[256]{0:T(256)}, u32[]{:S(2)}) copy-start(f32[256]{0:T(256)} %param.26) | copy-start | bytes 3076
  49.2 28.7 %copy-start.12 = (f32[256]{0:T(256)S(1)}, f32[256]{0:T(256)}, u32[]{:S(2)}) copy-start(f32[256]{0:T(256)} %param.27) | copy-start | bytes 3076
  49.2 70.7 %slice-start = ((s8[12582912]{0:T(1024)(128)(4,1)}), s8[4194304]{0:T(1024)(128)(4,1)S(1)}, s32[]{:S(2)}) async-start(s8[12582912]{0:T(1024)(128)(4,1)} %bitcast.30), calls=%async_computation.5 | async-start | bytes 8388608
  77.9 42.0 %slice-start.1 = ((s8[12582912]{0:T(1024)(128)(4,1)}), s8[4194304]{0:T(1024)(128)(4,1)S(1)}, s32[]{:S(2)}) async-start(s8[12582912]{0:T(1024)(128)(4,1)} %bitcast.30), calls=%async_computation.6 | async-start | bytes 8388608
  77.9 42.0 %slice-start.2 = ((s8[12582912]{0:T(1024)(128)(4,1)}), s8[4194304]{0:T(1024)(128)(4,1)S(1)}, s32[]{:S(2)}) async-start(s8[12582912]{0:T(1024)(128)(4,1)} %bitcast.30), calls=%async_computation.7 | async-start | bytes 8388608
  128.6 27.7 %copy-start.1 = (s32[1,128,8]{1,2,0:T(8,128)S(1)}, s32[1,128,8]{1,2,0:T(8,128)}, u32[]{:S(2)}) copy-start(s32[1,128,8]{1,2,0:T(8,128)} %param.18) | copy-start | bytes 12292
  152.4 15.0 %all-to-all-start.4 = ((bf16[128,8,128]{2,1,0:T(8,128)(2,1)}), bf16[128,8,128]{2,1,0:T(8,128)(2,1)S(1)}, u32[]{:S(2)}, u32[]{:S(2)}) async-start(bf16[128,8,128]{2,1,0:T(8,128)(2,1)} %chunk.1), calls=%async_computation.4 | async-start | bytes 524288 | tf_op jit(solution)/shard_map/all_to_all | solution.py:495

commit v4 on v3

--- a/solution.py
+++ b/solution.py
@@ -16,7 +16,8 @@
 SRC_BLOCK = 256
 VISITS = 8
 UNROLL = 2
-SEND_MIB, EDGES_MIB, EMBED_MIB, DECODE_MIB, SPREAD_MIB = 8, 24, 24, 16, 20
+SEND_MIB, EDGES_MIB, EMBED_MIB, DECODE_MIB, SPREAD_MIB = 8, 24, 24, 16, 16
+DIRECT_MIB = 16
 CHUNK_MIB, FINAL_MIB, WEIGHTS_MIB = 8, 16, 8
 
 
@@ -64,7 +65,13 @@
     return pl.CostEstimate(flops=flops, bytes_accessed=moved, transcendentals=0)
 
 
-def send_body(slot_ref, halo_ref, want_ref, feat_ref, out_ref):
+def send_body(slot_ref, halo_hbm, want_hbm, feat_hbm, out_ref, halo_ref, want_ref, feat_ref, sems):
+    pairs = ((halo_hbm, halo_ref), (want_hbm, want_ref), (feat_hbm, feat_ref))
+    copies = [pltpu.make_async_copy(*pair, sems.at[i]) for i, pair in enumerate(pairs)]
+    for copy in copies:
+        copy.start()
+    copies[0].wait()
+    copies[1].wait()
     parts = out_ref.shape[0]
     want = jnp.transpose(want_ref[...])
     tiled = jnp.concatenate([want] * 8, axis=1)
@@ -77,6 +84,7 @@
     halo = halo_ref[...]
     tiles = [jnp.broadcast_to(halo[:, p : p + 1], (8, 128)) for p in range(parts)]
     diff = lane_diff(jnp.concatenate(tiles, axis=0))
+    copies[2].wait()
     rows = mm(hot_lanes(diff, feat_ref.shape[0]), feat_ref[...])
     rows = rows.reshape(parts, 8, rows.shape[1])
     notes = jnp.broadcast_to(index[:, None, :], rows.shape)
@@ -88,8 +96,14 @@
     return pl.pallas_call(
         send_body,
         out_shape=shape_of((parts, 16, features.shape[1]), BF16),
-        in_specs=[whole(pltpu.SMEM), whole(), whole(), whole()],
+        in_specs=[whole(pltpu.SMEM)] + [whole(pltpu.HBM)] * 3,
         out_specs=whole(),
+        scratch_shapes=[
+            pltpu.VMEM(halo.shape, I32),
+            pltpu.VMEM(want.shape, I32),
+            pltpu.VMEM(features.shape, BF16),
+            pltpu.SemaphoreType.DMA((3,)),
+        ],
         compiler_params=limit(SEND_MIB),
         cost_estimate=cost(10**9, 2 * 10**6),
         name="send_rows",
@@ -185,7 +199,7 @@
 
 def embed_body(
     count_ref, arrived_ref, feat_ref, degree_ref, self_ref, neigh_ref,
-    served_ref, agg_ref, want_ref, held_ref, table_ref, emb_ref, sems,
+    served_ref, agg_ref, want_ref, held_ref, table_ref, mean_ref, emb_ref, sems,
 ):
     blocks = count_ref.shape[0]
     copies = [pltpu.make_async_copy(count_ref.at[i], held_ref.at[i], sems.at[i]) for i in range(blocks)]
@@ -207,14 +221,15 @@
         pltpu.make_async_copy(count_ref.at[i], held_ref.at[i], sems.at[i]).wait()
         sums = mm(table_ref[...], held_ref[i])
         degree = jnp.sum(degree_ref[:, span], axis=0, keepdims=True)
-        mean = (sums / jnp.maximum(degree, 1.0)).astype(BF16)
-        mean = jnp.transpose(mean)
-        agg_ref[span, :] = mean
-        both = mm(feat_ref[span, :], self_ref[...]) + mm(mean, neigh_ref[...])
+        mean_ref[:, span] = (sums / jnp.maximum(degree, 1.0)).astype(BF16)
+        return carry
+
+    lax.fori_loop(0, nodes // DST_BLOCK, node_block, 0)
+    agg_ref[...] = jnp.transpose(mean_ref[...])
+    for at in range(0, nodes, 1024):
+        span = slice(at, at + 1024)
+        both = mm(feat_ref[span, :], self_ref[...]) + mm(agg_ref[span, :], neigh_ref[...])
         emb_ref[span, :] = both.astype(BF16)
-        return carry
-
-    lax.fori_loop(0, nodes // DST_BLOCK, node_block, 0)
     for k in range(0, columns.shape[1], 8):
         tiles = [jnp.broadcast_to(columns[:, i : i + 1], (128, 128)) for i in range(k, k + 8)]
         hot = hot_tile(jnp.concatenate(tiles, axis=0), nodes)
@@ -236,6 +251,7 @@
         scratch_shapes=[
             pltpu.VMEM(counts.shape, BF16),
             pltpu.VMEM((width, table), BF16),
+            pltpu.VMEM((width, nodes), BF16),
             pltpu.VMEM((nodes, width), BF16),
             pltpu.SemaphoreType.DMA((blocks,)),
         ],
@@ -326,11 +342,13 @@
 
 
 def spread_body(
-    count_ref, back_ref, want_ref, feat_ref, agg_ref, degree_ref, self_ref, neigh_ref,
-    send_ref, direct_ref, small_ref, grad_ref, mean_ref,
+    count_ref, back_ref, want_ref, feat_ref, agg_ref, degree_ref, neigh_ref,
+    send_hbm, small_ref, grad_hbm, mean_hbm, send_ref, grad_ref, mean_ref, held_ref, sem, out_sems,
 ):
     nodes, width = feat_ref.shape
     rows = 1024
+    copy = pltpu.make_async_copy(count_ref.at[:, nodes : nodes + held_ref.shape[1]], held_ref, sem)
+    copy.start()
     back = back_ref[...].astype(F32)
     tail = jnp.sum(back[:, 16:, :], axis=0)
     small_ref[...] = tail[:, 128:]
@@ -353,7 +371,13 @@
         mean_ref[span, :] = scaled.astype(BF16)
         return carry
 
-    lax.fori_loop(0, nodes // 256, scale, 0, unroll=UNROLL)
+    lax.fori_loop(0, nodes // 256, scale, 0, unroll=2)
+    halves = [(slice(None), slice(0, 8)), (slice(None), slice(8, 16))]
+    pairs = [(send_ref.at[half], send_hbm.at[half]) for half in halves]
+    pairs += [(grad_ref, grad_hbm), (mean_ref, mean_hbm)]
+    leaving = [pltpu.make_async_copy(*pair, out_sems.at[i]) for i, pair in enumerate(pairs)]
+    leaving[2].start()
+    leaving[3].start()
     both = jnp.concatenate(
         [mm(feat_ref[...], grad_ref[...], TN), mm(agg_ref[...], grad_ref[...], TN)], axis=0
     )
@@ -363,58 +387,100 @@
     odd = jnp.concatenate([both[:, :, 128:], tail], axis=2)
     joined = jnp.stack([even, odd], axis=1).reshape(-1, 8, width)
     send_ref[:, 8:16, :] = joined.astype(BF16)
-
-    def table_rows(at):
-        blocks = range(0, nodes, DST_BLOCK)
-        span = pl.ds(pl.multiple_of(at, rows), rows)
-        parts = [mm(count_ref[n // DST_BLOCK, span, :], mean_ref[n : n + DST_BLOCK, :]) for n in blocks]
-        return sum(parts[1:], parts[0])
+    leaving[1].start()
+    copy.wait()
+    blocks = range(0, nodes, DST_BLOCK)
+    parts = [mm(held_ref[n // DST_BLOCK], mean_ref[n : n + DST_BLOCK, :]) for n in blocks]
+    grad = sum(parts[1:], parts[0]).reshape(-1, 8, width)
+    send_ref[:, 0:8, :] = grad.astype(BF16)
+    leaving[0].start()
+    for copy in leaving:
+        copy.wait()
+
+
+def spread(counts, back, want, features, agg, degree, w_neigh):
+    blocks, table, _ = counts.shape
+    nodes, width = features.shape
+    return pl.pallas_call(
+        spread_body,
+        out_shape=(
+            pltpu.HBM((back.shape[0], 16, width), BF16),
+            shape_of((8, 128), F32),
+            pltpu.HBM((nodes, width), BF16),
+            pltpu.HBM((nodes, width), BF16),
+        ),
+        in_specs=[whole(pltpu.HBM)] + [whole()] * 6,
+        out_specs=(whole(pltpu.HBM), whole(), whole(pltpu.HBM), whole(pltpu.HBM)),
+        scratch_shapes=[
+            pltpu.VMEM((back.shape[0], 16, width), BF16),
+            pltpu.VMEM((nodes, width), BF16),
+            pltpu.VMEM((nodes, width), BF16),
+            pltpu.VMEM((blocks, table - nodes, DST_BLOCK), BF16),
+            pltpu.SemaphoreType.DMA,
+            pltpu.SemaphoreType.DMA((4,)),
+        ],
+        compiler_params=limit(SPREAD_MIB),
+        cost_estimate=cost(5 * 10**9, 10 * 10**6),
+        name="spread",
+    )(counts, back, want, features, agg, degree, w_neigh)
+
+
+def direct_body(count_ref, grad_ref, mean_ref, self_ref, out_ref, held_ref, sems):
+    nodes = out_ref.shape[0]
+    rows = 512
+
+    def fetch(i):
+        span = pl.ds(pl.multiple_of(i * rows, rows), rows)
+        return pltpu.make_async_copy(count_ref.at[:, span], held_ref.at[:, span], sems.at[i])
+
+    for i in range(nodes // rows):
+        fetch(i).start()
 
     def own(i, carry):
         span = pl.ds(pl.multiple_of(i * rows, rows), rows)
-        direct_ref[span, :] = mm(grad_ref[span, :], self_ref[...], NT) + table_rows(i * rows)
+        blocks = range(0, nodes, DST_BLOCK)
+        total = mm(grad_ref[span, :], self_ref[...], NT)
+        fetch(i).wait()
+        parts = [mm(held_ref[n // DST_BLOCK, span, :], mean_ref[n : n + DST_BLOCK, :]) for n in blocks]
+        out_ref[span, :] = sum(parts[1:], parts[0]) + total
         return carry
 
     lax.fori_loop(0, nodes // rows, own, 0)
-    for at in range(0, count_ref.shape[1] - nodes, rows):
-        peers = rows // 8
-        grad = table_rows(nodes + at).reshape(peers, 8, width)
-        send_ref[at // 8 : at // 8 + peers, 0:8, :] = grad.astype(BF16)
-
-
-def spread(counts, back, want, features, agg, degree, w_self, w_neigh):
-    nodes, width = features.shape
-    return pl.pallas_call(
-        spread_body,
-        out_shape=(
-            shape_of((back.shape[0], 16, width), BF16),
-            pltpu.HBM((nodes, width), F32),
-            shape_of((8, 128), F32),
-        ),
-        in_specs=[whole()] * 8,
-        out_specs=(whole(),) * 3,
-        scratch_shapes=[pltpu.VMEM((nodes, width), BF16), pltpu.VMEM((nodes, width), BF16)],
-        compiler_params=limit(SPREAD_MIB),
-        cost_estimate=cost(7 * 10**9, 20 * 10**6),
-        name="spread",
-    )(counts, back, want, features, agg, degree, w_self, w_neigh)
-
-
-def chunk_body(back_ref, out_ref):
+
+
+def direct_rows(counts, grad, mean, w_self):
+    nodes, width = grad.shape
+    return pl.pallas_call(
+        direct_body,
+        out_shape=pltpu.HBM((nodes, width), F32),
+        in_specs=[whole(pltpu.HBM)] + [whole()] * 3,
+        out_specs=whole(),
+        scratch_shapes=[
+            pltpu.VMEM((counts.shape[0], nodes, DST_BLOCK), BF16),
+            pltpu.SemaphoreType.DMA((nodes // 512,)),
+        ],
+        compiler_params=limit(DIRECT_MIB),
+        cost_estimate=cost(3 * 10**9, 12 * 10**6),
+        name="direct_rows",
+    )(counts, grad, mean, w_self)
+
+
+def chunk_body(back_ref, direct_ref, out_ref):
+    del direct_ref
     tail = jnp.sum(back_ref[:, 8:, :].astype(F32), axis=0)[:, :128]
     out_ref[...] = jnp.broadcast_to(tail[None], out_ref.shape).astype(BF16)
 
 
-def chunk(back):
+def chunk(back, direct):
     return pl.pallas_call(
         chunk_body,
         out_shape=shape_of((back.shape[0], 8, 128), BF16),
-        in_specs=[whole()],
+        in_specs=[whole(), whole(pltpu.HBM)],
         out_specs=whole(),
         compiler_params=limit(CHUNK_MIB),
         cost_estimate=cost(10**6, 10**6),
         name="chunk",
-    )(back)
+    )(back, direct)
 
 
 def join_lanes(pieces):
@@ -505,7 +571,8 @@
     slots = edge_src.shape[0]
     me = lax.axis_index("dom") * lax.axis_size("grp") + lax.axis_index("grp")
 
-    sent = send_rows((me % 8).reshape(1), halo_index[0].T, request_rows[0].T, features)
+    held = [pltpu.with_memory_space_constraint(x, pltpu.HBM) for x in (halo_index[0].T, request_rows[0].T, features)]
+    sent = send_rows((me % 8).reshape(1), *held)
     arrived = exchange(sent)
 
     src_blocks = table // SRC_BLOCK
@@ -527,10 +594,11 @@
         w_hidden, b_hidden.reshape(1, -1), w_out.reshape(1, -1), parts,
     )
     back = exchange(pair_back)
-    halo_back, direct, small = spread(counts, back, want, features, agg, degree, w_self, w_neigh)
+    halo_back, small, grad, mean = spread(fixed, back, want, features, agg, degree, w_neigh)
+    returned = exchange(halo_back)
+    direct = direct_rows(fixed, grad, mean, w_self)
     direct = pltpu.with_memory_space_constraint(direct, pltpu.HBM)
-    returned = exchange(halo_back)
-    pieces = exchange(chunk(returned))
+    pieces = exchange(chunk(returned, direct))
     grad_features, grad_hidden, grad_bias, grad_out = final(
         direct, returned, halo_index[0].reshape(8, -1), small
     )

time: 169 us -> 164 us (0.970)
  blocking collectives: 80.4 us -> 58.6 us
  waiting for transfers between devices: 6.82 us -> 19.8 us
  starting transfers between devices: 15.4 us -> 19.3 us
  local copies, waits for them, and re-layouts: 2.88 us -> 0.27 us
  Pallas kernels: 53.7 us -> 56.1 us
    all_to_all x3 -> x2, blocking collectives: 80.4 us -> 58.6 us  [exchange(): return lax.all_to_all(rows, AXES, split_axis=0, concat_axis=0, tiled=True)]
    all_to_all x2 -> x3, waiting for transfers between devices: 6.82 us -> 19.8 us  [exchange(): return lax.all_to_all(rows, AXES, split_axis=0, concat_axis=0, tiled=True)]
    pallas_call x1 -> x2, Pallas kernels: 8.64 us -> 13.4 us  [the longest x1 6.78 us: direct_rows(): pl.pallas_call(direct_body, out_shape=pltpu.HBM((nodes, width), F32), in_...]
    all_to_all x2 -> x3, starting transfers between devices: 15.4 us -> 19.3 us  [exchange(): return lax.all_to_all(rows, AXES, split_axis=0, concat_axis=0, tiled=True)]
    unnamed x37 -> x29, local copies, waits for them, and re-layouts: 2.78 us -> 0.18 us
    pallas_call x1, Pallas kernels: 11.4 us -> 9.05 us  [embed(): pl.pallas_call(embed_body, out_shape=(shape_of((nodes, width), BF16), sha...]
  transfers between devices with their start and end apart: 2 -> 3, of which waited for: 1 -> 3; matrix products, arithmetic and copies ran while one was open for 5% -> 5% of each run, Pallas kernels for 10% -> 13%
where the time goes in v4:
time: 164 us; the launch traced here: 163 us
  blocking collectives  58.6 us (36%)
  Pallas kernels  56.1 us (34%)
  waiting for transfers between devices  19.8 us (12%)
  starting transfers between devices  19.3 us (12%)
  other arithmetic  7.45 us (5%)
    all_to_all x2, blocking collectives, exchange(): return lax.all_to_all(rows, AXES, split_axis=0, concat_axis=0, tiled=True)  58.6 us
    all_to_all x3, waiting for transfers between devices, exchange(): return lax.all_to_all(rows, AXES, split_axis=0, concat_axis=0, tiled=True)  19.8 us
    all_to_all x3, starting transfers between devices, exchange(): return lax.all_to_all(rows, AXES, split_axis=0, concat_axis=0, tiled=True)  19.3 us
    pallas_call x1, Pallas kernels, decode(): pl.pallas_call(decode_body, out_shape=(shape_of((1, pairs), F32), shape_o...  13.2 us
    pallas_call x1, Pallas kernels, edge_counts(): pl.pallas_call(functools.partial(edges_body, table // SRC_BLOCK), out_sha...  11.2 us
    pallas_call x1, Pallas kernels, embed(): pl.pallas_call(embed_body, out_shape=(shape_of((nodes, width), BF16), sha...  9.05 us
    pallas_call x1, Pallas kernels, direct_rows(): pl.pallas_call(direct_body, out_shape=pltpu.HBM((nodes, width), F32), in_...  6.78 us
    pallas_call x1, Pallas kernels, spread(): pl.pallas_call(spread_body, out_shape=(pltpu.HBM((back.shape[0], 16, widt...  6.62 us
  transfers between devices with their start and end apart: 3, of which 3 were waited for; matrix products, arithmetic and copies ran while one was open for 5% of the time, Pallas kernels for 13%

profile of v4, /device:TPU:1, one launch (start us, length us, event | category | flops | bytes accessed | tf_op | source)
XLA Modules:
  0.0 163.2 jit_solution(17053288793457929169)
XLA Ops:
  0.6 0.0 copy-start.11
  0.7 0.0 copy-start.12
  0.7 3.6 %send_rows.1 = bf16[128,16,256]{2,1,0:T(8,128)(2,1)} custom-call(s32[1]{0:T(128)} %bitcast.2.slot_ref, s32[8,128]{1,0:T(8,128)} %bitcast.28, s32[16,128]{1,0:T(8,128)} %bitcast.29, bf16[2048,256]{1,0:T(8,128)(2,1)} %feat_ref.3), custom_call_target="tpu_custom_call" | custom-call | flops 1000000000 | bytes 2000000 | tf_op jit(solution)/shard_map/send_rows/pallas_call | solution.py:96
  4.2 11.5 %all-to-all-start = ((bf16[128,16,256]{2,1,0:T(8,128)(2,1)}), bf16[128,16,256]{2,1,0:T(8,128)(2,1)S(1)}, u32[]{:S(2)}, u32[]{:S(2)}) async-start(bf16[128,16,256]{2,1,0:T(8,128)(2,1)} %send_rows.1), calls=%async_computation | async-start | bytes 2097152 | tf_op jit(solution)/shard_map/all_to_all | solution.py:561
  16.4 0.0 copy-done.11
  16.4 0.0 copy-done.12
  16.4 0.1 fusion.5
  16.6 6.3 %sort.7 = s32[16384]{0:T(1024)S(1)} sort(s32[16384]{0:T(1024)S(1)} %fusion.5), dimensions={0}, to_apply=%region_1.2 | sort | flops 229376 | bytes 131072 | tf_op jit(solution)/shard_map/sort | solution.py:586
  22.9 1.0 convert_reduce_fusion.starts_ref
  23.9 0.0 copy-start.2
  23.9 0.0 copy-start.3
  23.9 0.0 copy-start.5
  23.9 11.2 %edge_counts.1 = (bf16[8,3072,256]{2,1,0:T(8,128)(2,1)}, f32[8,2048]{1,0:T(8,128)S(1)}) custom-call(s32[97]{0:T(128)S(1)} %convert_reduce_fusion.starts_ref, s32[128,128]{1,0:T(8,128)S(1)} %bitcast.22), custom_call_target="tpu_custom_call" | custom-call | flops 14000000000 | bytes 13000000 | tf_op jit(solution)/shard_map/edge_counts/pallas_call | solution.py:184
  35.1 0.2 all-to-all-done.arrived_ref
  35.3 0.0 copy-done.2
  35.3 0.0 copy-done.3
  35.3 0.0 copy-done.5
  35.3 9.1 %embed.1 = (bf16[2048,256]{1,0:T(8,128)(2,1)S(1)}, bf16[2048,256]{1,0:T(8,128)(2,1)S(1)}, s32[16,128]{1,0:T(8,128)S(1)}) custom-call(bf16[8,3072,256]{2,1,0:T(8,128)(2,1)} %get-tuple-element.24.count_ref, bf16[128,16,256]{2,1,0:T(8,128)(2,1)S(1)} %all-to-all-done.arrived_ref, bf16[2048,256]{1,0:T(8,128)(2,1)S(1)} %copy-done.3, ...), custom_call_target="tpu_custom_call" | custom-call | flops 6000000000 | bytes 16000000 | tf_op jit(solution)/shard_map/embed/pallas_call | solution.py:242
  44.3 0.0 copy-start.4
  44.4 0.0 copy-start.6
  44.4 0.0 copy-start.7
  44.4 0.0 copy-start.8
  44.4 0.0 copy-start.9
  44.4 0.0 copy-start.10
  44.4 29.7 %all_to_all.25 = bf16[128,16,256]{2,1,0:T(8,128)(2,1)S(1)} all-to-all(bf16[128,16,256]{2,1,0:T(8,128)(2,1)S(1)} %bitcast.20), channel_id=1, replica_groups=mesh['dom'=32,'grp'=4] {'dom','grp'}, dimensions={0} | all-to-all | bytes 2097152 | tf_op jit(solution)/shard_map/all_to_all | solution.py:561
  74.2 0.0 copy-done.4
  74.2 0.0 copy-done.6
  74.2 0.0 copy-done.7
  74.2 0.0 copy-done.8
  74.2 0.0 copy-done.9
  74.2 0.0 copy-done.10
  74.2 13.2 %decode.1 = (f32[1,2048]{1,0:T(1,128)}, bf16[128,24,256]{2,1,0:T(8,128)(2,1)S(1)}) custom-call(bf16[2048,256]{1,0:T(8,128)(2,1)S(1)} %bitcast.21, s32[2,2048]{1,0:T(2,128)S(1)} %bitcast.23, s32[1,2048]{1,0:T(1,128)S(1)} %bitcast.24, f32[1,2048]{1,0:T(1,128)S(1)} %bitcast.25, bf16[512,256]{1,0:T(8,128)(2,1)S(1)} %copy-done.4, f32[1,256]{1,0:T(1,128)S(1)} %bitcast.26, ...), custom_call_target="tpu_custom_call" | custom-call | flops 10000000000 | bytes 4000000 | tf_op jit(solution)/shard_map/decode/pallas_call | solution.py:327
  87.4 28.9 %all_to_all.26.back_ref = bf16[128,24,256]{2,1,0:T(8,128)(2,1)S(1)} all-to-all(bf16[128,24,256]{2,1,0:T(8,128)(2,1)S(1)} %get-tuple-element.28), channel_id=1, replica_groups=mesh['dom'=32,'grp'=4] {'dom','grp'}, dimensions={0} | all-to-all | bytes 3145728 | tf_op jit(solution)/shard_map/all_to_all | solution.py:561
  116.2 6.6 %spread.1 = (bf16[128,16,256]{2,1,0:T(8,128)(2,1)}, f32[8,128]{1,0:T(8,128)S(1)}, bf16[2048,256]{1,0:T(8,128)(2,1)}, bf16[2048,256]{1,0:T(8,128)(2,1)}) custom-call(bf16[8,3072,256]{2,1,0:T(8,128)(2,1)} %get-tuple-element.24.count_ref, bf16[128,24,256]{2,1,0:T(8,128)(2,1)S(1)} %all_to_all.26.back_ref, s32[16,128]{1,0:T(8,128)S(1)} %get-tuple-element.29.want_ref, ...), custom_call_target="tpu_custom_call" | custom-call | flops 5000000000 | bytes 10000000 | tf_op jit(solution)/shard_map/spread/pallas_call | solution.py:404
  122.9 0.0 copy-start
  122.9 0.0 copy-start.1
  122.9 3.9 %all-to-all-start.3 = ((bf16[128,16,256]{2,1,0:T(8,128)(2,1)}), bf16[128,16,256]{2,1,0:T(8,128)(2,1)S(1)}, u32[]{:S(2)}, u32[]{:S(2)}) async-start(bf16[128,16,256]{2,1,0:T(8,128)(2,1)} %get-tuple-element.33), calls=%async_computation.3 | async-start | bytes 2097152 | tf_op jit(solution)/shard_map/all_to_all | solution.py:561
  126.8 0.0 copy-done
  126.8 0.0 copy-done.1
  126.8 6.8 %direct_rows.1.direct_ref = f32[2048,256]{1,0:T(8,128)} custom-call(bf16[8,3072,256]{2,1,0:T(8,128)(2,1)} %get-tuple-element.24.count_ref, bf16[2048,256]{1,0:T(8,128)(2,1)S(1)} %copy-done, bf16[2048,256]{1,0:T(8,128)(2,1)S(1)} %copy-done.1, bf16[256,256]{1,0:T(8,128)(2,1)S(1)} %copy-done.2), custom_call_target="tpu_custom_call" | custom-call | flops 3000000000 | bytes 12000000 | tf_op jit(solution)/shard_map/direct_rows/pallas_call | solution.py:453
  133.6 0.0 copy-start.13
  133.6 12.8 %all-to-all-done.3.back_ref = bf16[128,16,256]{2,1,0:T(8,128)(2,1)S(1)} async-done(((bf16[128,16,256]{2,1,0:T(8,128)(2,1)}), bf16[128,16,256]{2,1,0:T(8,128)(2,1)S(1)}, u32[]{:S(2)}, u32[]{:S(2)}) %all-to-all-start.3) | async-done | bytes 1048608 | tf_op jit(solution)/shard_map/all_to_all | solution.py:561
  146.5 0.9 chunk.1
  147.3 3.9 %all-to-all-start.4 = ((bf16[128,8,128]{2,1,0:T(8,128)(2,1)}), bf16[128,8,128]{2,1,0:T(8,128)(2,1)S(1)}, u32[]{:S(2)}, u32[]{:S(2)}) async-start(bf16[128,8,128]{2,1,0:T(8,128)(2,1)} %chunk.1), calls=%async_computation.4 | async-start | bytes 524288 | tf_op jit(solution)/shard_map/all_to_all | solution.py:561
  151.3 0.0 copy-done.13
  151.3 0.1 copy.23
  151.4 0.1 reshape_squeeze.3.halo_ref
  151.5 4.1 %final.1 = (f32[2048,256]{1,0:T(8,128)}, f32[512,256]{1,0:T(8,128)}, f32[2,128]{1,0:T(2,128)}, f32[2,128]{1,0:T(2,128)}) custom-call(f32[2048,256]{1,0:T(8,128)} %direct_rows.1.direct_ref, bf16[128,16,256]{2,1,0:T(8,128)(2,1)S(1)} %all-to-all-done.3.back_ref, s32[8,128]{1,0:T(8,128)S(1)} %reshape_squeeze.3.halo_ref, f32[8,128]{1,0:T(8,128)S(1)} %get-tuple-element.34.small_ref), custom_call_target="tpu_custom_call" | custom-call | flops 2000000000 | bytes 6000000 | tf_op jit(solution)/shard_map/final/pallas_call | solution.py:520
  155.5 6.8 %all-to-all-done.4.pieces_ref = bf16[128,8,128]{2,1,0:T(8,128)(2,1)S(1)} async-done(((bf16[128,8,128]{2,1,0:T(8,128)(2,1)}), bf16[128,8,128]{2,1,0:T(8,128)(2,1)S(1)}, u32[]{:S(2)}, u32[]{:S(2)}) %all-to-all-start.4) | async-done | bytes 262176 | tf_op jit(solution)/shard_map/all_to_all | solution.py:561
  162.4 0.8 weights.1
  (1 shorter events, 0.0 us)
Async XLA Ops:
  0.6 15.8 %copy-start.11 = (s32[16384]{0:T(1024)S(1)}, s32[16384]{0:T(1024)}, u32[]{:S(2)}) copy-start(s32[16384]{0:T(1024)} %param.16) | copy-start | bytes 196612
  0.7 15.8 %copy-start.12 = (s32[16384]{0:T(1024)S(1)}, s32[16384]{0:T(1024)}, u32[]{:S(2)}) copy-start(s32[16384]{0:T(1024)} %param.15) | copy-start | bytes 196612
  4.2 31.0 %all-to-all-start = ((bf16[128,16,256]{2,1,0:T(8,128)(2,1)}), bf16[128,16,256]{2,1,0:T(8,128)(2,1)S(1)}, u32[]{:S(2)}, u32[]{:S(2)}) async-start(bf16[128,16,256]{2,1,0:T(8,128)(2,1)} %send_rows.1), calls=%async_computation | async-start | bytes 2097152 | tf_op jit(solution)/shard_map/all_to_all | solution.py:561
  23.9 11.4 %copy-start.2 = (bf16[256,256]{1,0:T(8,128)(2,1)S(1)}, bf16[256,256]{1,0:T(8,128)(2,1)}, u32[]{:S(2)}) copy-start(bf16[256,256]{1,0:T(8,128)(2,1)} %self_ref.3) | copy-start | bytes 393220
  23.9 11.4 %copy-start.3 = (bf16[2048,256]{1,0:T(8,128)(2,1)S(1)}, bf16[2048,256]{1,0:T(8,128)(2,1)}, u32[]{:S(2)}) copy-start(bf16[2048,256]{1,0:T(8,128)(2,1)} %feat_ref.3) | copy-start | bytes 3145732
  23.9 11.4 %copy-start.5 = (bf16[256,256]{1,0:T(8,128)(2,1)S(1)}, bf16[256,256]{1,0:T(8,128)(2,1)}, u32[]{:S(2)}) copy-start(bf16[256,256]{1,0:T(8,128)(2,1)} %neigh_ref.3) | copy-start | bytes 393220
  44.3 29.8 %copy-start.4 = (bf16[512,256]{1,0:T(8,128)(2,1)S(1)}, bf16[512,256]{1,0:T(8,128)(2,1)}, u32[]{:S(2)}) copy-start(bf16[512,256]{1,0:T(8,128)(2,1)} %hid_ref.1) | copy-start | bytes 786436
  44.4 29.8 %copy-start.6 = (s32[2048,2]{0,1:T(2,128)S(1)}, s32[2048,2]{0,1:T(2,128)}, u32[]{:S(2)}) copy-start(s32[2048,2]{0,1:T(2,128)} %param.20) | copy-start | bytes 49156
  44.4 29.8 %copy-start.7 = (s32[2048]{0:T(1024)S(1)}, s32[2048]{0:T(1024)}, u32[]{:S(2)}) copy-start(s32[2048]{0:T(1024)} %param.21) | copy-start | bytes 24580
  44.4 29.8 %copy-start.8 = (f32[2048]{0:T(1024)S(1)}, f32[2048]{0:T(1024)}, u32[]{:S(2)}) copy-start(f32[2048]{0:T(1024)} %param.22) | copy-start | bytes 24580
  44.4 29.8 %copy-start.9 = (f32[256]{0:T(256)S(1)}, f32[256]{0:T(256)}, u32[]{:S(2)}) copy-start(f32[256]{0:T(256)} %param.26) | copy-start | bytes 3076
  44.4 29.8 %copy-start.10 = (f32[256]{0:T(256)S(1)}, f32[256]{0:T(256)}, u32[]{:S(2)}) copy-start(f32[256]{0:T(256)} %param.27) | copy-start | bytes 3076
  122.9 4.0 %copy-start = (bf16[2048,256]{1,0:T(8,128)(2,1)S(1)}, bf16[2048,256]{1,0:T(8,128)(2,1)}, u32[]{:S(2)}) copy-start(bf16[2048,256]{1,0:T(8,128)(2,1)} %get-tuple-element.31.grad_ref) | copy-start | bytes 3145732
  122.9 4.0 %copy-start.1 = (bf16[2048,256]{1,0:T(8,128)(2,1)S(1)}, bf16[2048,256]{1,0:T(8,128)(2,1)}, u32[]{:S(2)}) copy-start(bf16[2048,256]{1,0:T(8,128)(2,1)} %get-tuple-element.32.mean_ref) | copy-start | bytes 3145732
  122.9 23.6 %all-to-all-start.3 = ((bf16[128,16,256]{2,1,0:T(8,128)(2,1)}), bf16[128,16,256]{2,1,0:T(8,128)(2,1)S(1)}, u32[]{:S(2)}, u32[]{:S(2)}) async-start(bf16[128,16,256]{2,1,0:T(8,128)(2,1)} %get-tuple-element.33), calls=%async_computation.3 | async-start | bytes 2097152 | tf_op jit(solution)/shard_map/all_to_all | solution.py:561
  133.6 17.6 %copy-start.13 = (s32[1,128,8]{1,2,0:T(8,128)S(1)}, s32[1,128,8]{1,2,0:T(8,128)}, u32[]{:S(2)}) copy-start(s32[1,128,8]{1,2,0:T(8,128)} %param.18) | copy-start | bytes 12292
  147.3 15.0 %all-to-all-start.4 = ((bf16[128,8,128]{2,1,0:T(8,128)(2,1)}), bf16[128,8,128]{2,1,0:T(8,128)(2,1)S(1)}, u32[]{:S(2)}, u32[]{:S(2)}) async-start(bf16[128,8,128]{2,1,0:T(8,128)(2,1)} %chunk.1), calls=%async_computation.4 | async-start | bytes 524288 | tf_op jit(solution)/shard_map/all_to_all | solution.py:561

commit v5 on v4

--- a/solution.py
+++ b/solution.py
@@ -78,24 +78,23 @@
     lane = lax.broadcasted_iota(I32, tiled.shape, 1)
     mine = lax.shift_right_logical(lane, 4) == slot_ref[0]
     tiled = jnp.where(mine, tiled, 0)
-    index = jnp.concatenate(
-        [lax.shift_right_logical(tiled, 7).astype(F32), (tiled & 127).astype(F32)], axis=1
-    )
+    high, low = lax.shift_right_logical(tiled, 7).astype(F32), (tiled & 127).astype(F32)
     halo = halo_ref[...]
     tiles = [jnp.broadcast_to(halo[:, p : p + 1], (8, 128)) for p in range(parts)]
     diff = lane_diff(jnp.concatenate(tiles, axis=0))
     copies[2].wait()
     rows = mm(hot_lanes(diff, feat_ref.shape[0]), feat_ref[...])
     rows = rows.reshape(parts, 8, rows.shape[1])
-    notes = jnp.broadcast_to(index[:, None, :], rows.shape)
-    out_ref[...] = jnp.concatenate([rows, notes], axis=1).astype(BF16)
+    upper = lax.broadcasted_iota(I32, (parts, 8, 128), 1) < 4
+    notes = jnp.where(upper, high[:, None, :], low[:, None, :])
+    out_ref[...] = jnp.concatenate([rows[:, :, :128], rows[:, :, 128:], notes], axis=1).astype(BF16)
 
 
 def send_rows(slot, halo, want, features):
     parts = want.shape[1]
     return pl.pallas_call(
         send_body,
-        out_shape=shape_of((parts, 16, features.shape[1]), BF16),
+        out_shape=shape_of((parts, 24, 128), BF16),
         in_specs=[whole(pltpu.SMEM)] + [whole(pltpu.HBM)] * 3,
         out_specs=whole(),
         scratch_shapes=[
@@ -108,6 +107,67 @@
         cost_estimate=cost(10**9, 2 * 10**6),
         name="send_rows",
     )(slot, halo, want, features)
+
+
+def sort_body(src_blocks, blocks, live_ref, src_ref, dst_ref, out_ref):
+    shape = (8, 128)
+    count = src_ref.shape[0] // 8
+    dead = blocks << 18
+    sub = lax.broadcasted_iota(I32, shape, 0)
+    lane = lax.broadcasted_iota(I32, shape, 1)
+    shift = SRC_BLOCK.bit_length() - 1
+    keys = []
+    for v in range(count):
+        src, dst = src_ref[8 * v : 8 * v + 8, :], dst_ref[8 * v : 8 * v + 8, :]
+        block = lax.shift_right_logical(dst, 8) * src_blocks + lax.shift_right_logical(src, shift)
+        packed = (block << 18) | ((dst & 255) << 10) | (src & (SRC_BLOCK - 1))
+        keys.append(jnp.where(1024 * v + 128 * sub + lane < live_ref[0], packed, dead))
+    bits = [None] * 4
+    bits += [-(lax.shift_right_logical(sub, b) & 1) for b in range(3)]
+    bits += [-(lax.shift_right_logical(lane, b) & 1) for b in range(7)]
+    total = len(bits)
+
+    def flips(k):
+        if k == 0 or k == total:
+            return [0] * count
+        if k < 4:
+            return [-((v >> k) & 1) for v in range(count)]
+        return [bits[k]] * count
+
+    for k in range(1, total + 1):
+        for v, (old, new) in enumerate(zip(flips(k - 1), flips(k))):
+            for flip in (old, new):
+                if not isinstance(flip, int):
+                    keys[v] = keys[v] ^ flip
+                elif flip:
+                    keys[v] = ~keys[v]
+        for j in reversed(range(k)):
+            if j < 4:
+                for v in range(count):
+                    if not (v >> j) & 1:
+                        a, b = keys[v], keys[v | 1 << j]
+                        keys[v], keys[v | 1 << j] = jnp.minimum(a, b), jnp.maximum(a, b)
+                continue
+            axis, step, size = (0, 1 << (j - 4), 8) if j < 7 else (1, 1 << (j - 7), 128)
+            low = bits[j] == 0
+            for v in range(count):
+                key = keys[v]
+                after = pltpu.roll(key, size - step, axis)
+                before = after if 2 * step == size else pltpu.roll(key, step, axis)
+                keys[v] = jnp.where(low, jnp.minimum(key, after), jnp.maximum(key, before))
+    out_ref[...] = jnp.transpose(jnp.concatenate(keys, axis=0))
+
+
+def sort_edges(live, src, dst, src_blocks, blocks):
+    return pl.pallas_call(
+        functools.partial(sort_body, src_blocks, blocks),
+        out_shape=shape_of(src.shape, I32),
+        in_specs=[whole(pltpu.SMEM), whole(), whole()],
+        out_specs=whole(),
+        compiler_params=limit(8),
+        cost_estimate=cost(10**9, 2 * 10**5),
+        name="sort_edges",
+    )(live, src, dst)
 
 
 def edges_body(src_blocks, starts_ref, keys_ref, count_ref, degree_ref, held_ref, acc_ref, sem):
@@ -208,12 +268,13 @@
     nodes = feat_ref.shape[0]
     table_ref[:, :nodes] = jnp.transpose(feat_ref[...])
     arrived = arrived_ref[...].astype(F32)
-    halo = arrived[:, :8, :].reshape(-1, arrived.shape[2]).astype(BF16)
-    table_ref[:, nodes:] = jnp.transpose(halo)
-    notes = arrived[:, 8:, :]
+    for half in range(2):
+        halo = arrived[:, 8 * half : 8 * half + 8, :].reshape(-1, 128).astype(BF16)
+        table_ref[128 * half : 128 * half + 128, nodes:] = jnp.transpose(halo)
+    notes = arrived[:, 16:, :]
     grouped = notes.reshape(notes.shape[0] // 8, 8, 8, notes.shape[2])
-    summed = jnp.sum(grouped, axis=1)[:, 0, :]
-    want = (summed[:, :128] * 128.0 + summed[:, 128:]).astype(I32)
+    summed = jnp.sum(grouped, axis=1)
+    want = (summed[:, 0, :] * 128.0 + summed[:, 4, :]).astype(I32)
     want_ref[...] = want
     columns = jnp.transpose(want)
     def node_block(i, carry):
@@ -267,7 +328,7 @@
 ):
     rows, width = got_ref.shape
     pairs = ends_ref.shape[1]
-    block = 256
+    block = 512
     wide = 1024
     meta = jnp.concatenate(
         [
@@ -577,14 +638,11 @@
 
     src_blocks = table // SRC_BLOCK
     buckets = nodes // DST_BLOCK * src_blocks
-    bucket = edge_dst // DST_BLOCK * src_blocks + edge_src // SRC_BLOCK
-    packed = (bucket << 18) | ((edge_dst % DST_BLOCK) << 10) | (edge_src % SRC_BLOCK)
-    live = jnp.arange(slots, dtype=I32) < edge_count[0]
-    keys = jnp.where(live, packed, buckets << 18)
+    square = (slots // 128, 128)
+    keys = sort_edges(edge_count, edge_src.reshape(square), edge_dst.reshape(square), src_blocks, buckets)
     bounds = jnp.arange(buckets + 1, dtype=I32) << 18
-    starts = jnp.sum((keys[None, :] < bounds[:, None]).astype(I32), axis=1)
-    keys = lax.sort(keys, is_stable=False)
-    counts, degree = edge_counts(starts, keys.reshape(slots // 128, 128), nodes, table)
+    starts = jnp.sum((keys.reshape(1, -1) < bounds[:, None]).astype(I32), axis=1)
+    counts, degree = edge_counts(starts, keys, nodes, table)
 
     fixed = pltpu.with_memory_space_constraint(counts, pltpu.HBM)
     served, agg, want = embed(fixed, arrived, features, degree, w_self, w_neigh)

time: 164 us -> 159 us (0.970)
  other arithmetic: 7.45 us -> 1.03 us
    sort x1 -> x0, other arithmetic: 6.28 us -> none  [per_device(): keys = lax.sort(keys, is_stable=False)]
    pallas_call x1 -> x2, Pallas kernels: 3.58 us -> 6.12 us  [the longest x1 3.45 us: send_rows(): pl.pallas_call(send_body, out_shape=shape_of((parts, 24, 128), BF16), in_...]
  transfers between devices with their start and end apart: 3 -> 3, of which waited for: 3 -> 3; matrix products, arithmetic and copies ran while one was open for 5% -> 1% of each run, Pallas kernels for 13% -> 16%
where the time goes in v5:
time: 159 us; the launch traced here: 158 us
  Pallas kernels  57.7 us (36%)
  blocking collectives  57.7 us (36%)
  waiting for transfers between devices  20.8 us (13%)
  starting transfers between devices  19.3 us (12%)
    all_to_all x2, blocking collectives, exchange(): return lax.all_to_all(rows, AXES, split_axis=0, concat_axis=0, tiled=True)  57.7 us
    all_to_all x3, waiting for transfers between devices, exchange(): return lax.all_to_all(rows, AXES, split_axis=0, concat_axis=0, tiled=True)  20.8 us
    all_to_all x3, starting transfers between devices, exchange(): return lax.all_to_all(rows, AXES, split_axis=0, concat_axis=0, tiled=True)  19.3 us
    pallas_call x1, Pallas kernels, decode(): pl.pallas_call(decode_body, out_shape=(shape_of((1, pairs), F32), shape_o...  12.3 us
    pallas_call x1, Pallas kernels, edge_counts(): pl.pallas_call(functools.partial(edges_body, table // SRC_BLOCK), out_sha...  11.2 us
    pallas_call x1, Pallas kernels, embed(): pl.pallas_call(embed_body, out_shape=(shape_of((nodes, width), BF16), sha...  9.06 us
    pallas_call x1, Pallas kernels, direct_rows(): pl.pallas_call(direct_body, out_shape=pltpu.HBM((nodes, width), F32), in_...  6.76 us
    pallas_call x1, Pallas kernels, spread(): pl.pallas_call(spread_body, out_shape=(pltpu.HBM((back.shape[0], 16, widt...  6.62 us
  transfers between devices with their start and end apart: 3, of which 3 were waited for; matrix products, arithmetic and copies ran while one was open for 1% of the time, Pallas kernels for 16%

profile of v5, /device:TPU:1, one launch (start us, length us, event | category | flops | bytes accessed | tf_op | source)
XLA Modules:
  0.0 158.4 jit_solution(7748932823011756709)
XLA Ops:
  0.6 0.0 copy-start.6
  0.7 0.0 copy-start.7
  0.7 3.5 %send_rows.1 = bf16[128,24,128]{2,1,0:T(8,128)(2,1)} custom-call(s32[1]{0:T(128)} %bitcast.3.slot_ref, s32[8,128]{1,0:T(8,128)} %bitcast.30, s32[16,128]{1,0:T(8,128)} %bitcast.31, bf16[2048,256]{1,0:T(8,128)(2,1)} %feat_ref.3), custom_call_target="tpu_custom_call" | custom-call | flops 1000000000 | bytes 2000000 | tf_op jit(solution)/shard_map/send_rows/pallas_call | solution.py:95
  4.1 11.5 %all-to-all-start = ((bf16[128,24,128]{2,1,0:T(8,128)(2,1)}), bf16[128,24,128]{2,1,0:T(8,128)(2,1)S(1)}, u32[]{:S(2)}, u32[]{:S(2)}) async-start(bf16[128,24,128]{2,1,0:T(8,128)(2,1)} %send_rows.1), calls=%async_computation | async-start | bytes 1572864 | tf_op jit(solution)/shard_map/all_to_all | solution.py:622
  16.3 0.0 copy-done.6
  16.3 0.0 copy-done.7
  16.3 2.7 %sort_edges.1.keys_ref = s32[128,128]{1,0:T(8,128)S(1)} custom-call(s32[1]{0:T(128)S(6)} %copy.24.live_ref, s32[128,128]{1,0:T(8,128)S(1)} %bitcast.23, s32[128,128]{1,0:T(8,128)S(1)} %bitcast.24), custom_call_target="tpu_custom_call" | custom-call | flops 1000000000 | bytes 200000 | tf_op jit(solution)/shard_map/sort_edges/pallas_call | solution.py:162
  19.0 1.0 convert_reduce_fusion.starts_ref
  20.0 0.0 copy-start.2
  20.0 0.0 copy-start.3
  20.0 0.0 copy-start.5
  20.0 11.2 %edge_counts.1 = (bf16[8,3072,256]{2,1,0:T(8,128)(2,1)}, f32[8,2048]{1,0:T(8,128)S(1)}) custom-call(s32[97]{0:T(128)S(1)} %convert_reduce_fusion.starts_ref, s32[128,128]{1,0:T(8,128)S(1)} %sort_edges.1.keys_ref), custom_call_target="tpu_custom_call" | custom-call | flops 14000000000 | bytes 13000000 | tf_op jit(solution)/shard_map/edge_counts/pallas_call | solution.py:244
  31.2 1.1 all-to-all-done.arrived_ref
  32.3 0.0 copy-done.2
  32.3 0.0 copy-done.3
  32.3 0.0 copy-done.5
  32.4 9.1 %embed.1 = (bf16[2048,256]{1,0:T(8,128)(2,1)S(1)}, bf16[2048,256]{1,0:T(8,128)(2,1)S(1)}, s32[16,128]{1,0:T(8,128)S(1)}) custom-call(bf16[8,3072,256]{2,1,0:T(8,128)(2,1)} %get-tuple-element.24.count_ref, bf16[128,24,128]{2,1,0:T(8,128)(2,1)S(1)} %all-to-all-done.arrived_ref, bf16[2048,256]{1,0:T(8,128)(2,1)S(1)} %copy-done.3, ...), custom_call_target="tpu_custom_call" | custom-call | flops 6000000000 | bytes 16000000 | tf_op jit(solution)/shard_map/embed/pallas_call | solution.py:303
  41.4 0.0 copy-start.4
  41.4 0.0 copy-start.8
  41.4 0.0 copy-start.9
  41.5 0.0 copy-start.10
  41.5 0.0 copy-start.11
  41.5 0.0 copy-start.12
  41.5 28.8 %all_to_all.25 = bf16[128,16,256]{2,1,0:T(8,128)(2,1)S(1)} all-to-all(bf16[128,16,256]{2,1,0:T(8,128)(2,1)S(1)} %bitcast.20), channel_id=1, replica_groups=mesh['dom'=32,'grp'=4] {'dom','grp'}, dimensions={0} | all-to-all | bytes 2097152 | tf_op jit(solution)/shard_map/all_to_all | solution.py:622
  70.3 0.0 copy-done.4
  70.3 0.0 copy-done.8
  70.3 0.0 copy-done.9
  70.3 0.0 copy-done.10
  70.3 0.0 copy-done.11
  70.3 0.0 copy-done.12
  70.3 12.3 %decode.1 = (f32[1,2048]{1,0:T(1,128)}, bf16[128,24,256]{2,1,0:T(8,128)(2,1)S(1)}) custom-call(bf16[2048,256]{1,0:T(8,128)(2,1)S(1)} %bitcast.21, s32[2,2048]{1,0:T(2,128)S(1)} %bitcast.25, s32[1,2048]{1,0:T(1,128)S(1)} %bitcast.26, f32[1,2048]{1,0:T(1,128)S(1)} %bitcast.27, bf16[512,256]{1,0:T(8,128)(2,1)S(1)} %copy-done.4, f32[1,256]{1,0:T(1,128)S(1)} %bitcast.28, ...), custom_call_target="tpu_custom_call" | custom-call | flops 10000000000 | bytes 4000000 | tf_op jit(solution)/shard_map/decode/pallas_call | solution.py:388
  82.6 28.9 %all_to_all.26.back_ref = bf16[128,24,256]{2,1,0:T(8,128)(2,1)S(1)} all-to-all(bf16[128,24,256]{2,1,0:T(8,128)(2,1)S(1)} %get-tuple-element.28), channel_id=1, replica_groups=mesh['dom'=32,'grp'=4] {'dom','grp'}, dimensions={0} | all-to-all | bytes 3145728 | tf_op jit(solution)/shard_map/all_to_all | solution.py:622
  111.5 6.6 %spread.1 = (bf16[128,16,256]{2,1,0:T(8,128)(2,1)}, f32[8,128]{1,0:T(8,128)S(1)}, bf16[2048,256]{1,0:T(8,128)(2,1)}, bf16[2048,256]{1,0:T(8,128)(2,1)}) custom-call(bf16[8,3072,256]{2,1,0:T(8,128)(2,1)} %get-tuple-element.24.count_ref, bf16[128,24,256]{2,1,0:T(8,128)(2,1)S(1)} %all_to_all.26.back_ref, s32[16,128]{1,0:T(8,128)S(1)} %get-tuple-element.29.want_ref, ...), custom_call_target="tpu_custom_call" | custom-call | flops 5000000000 | bytes 10000000 | tf_op jit(solution)/shard_map/spread/pallas_call | solution.py:465
  118.1 0.0 copy-start
  118.1 0.0 copy-start.1
  118.1 3.9 %all-to-all-start.3 = ((bf16[128,16,256]{2,1,0:T(8,128)(2,1)}), bf16[128,16,256]{2,1,0:T(8,128)(2,1)S(1)}, u32[]{:S(2)}, u32[]{:S(2)}) async-start(bf16[128,16,256]{2,1,0:T(8,128)(2,1)} %get-tuple-element.33), calls=%async_computation.3 | async-start | bytes 2097152 | tf_op jit(solution)/shard_map/all_to_all | solution.py:622
  122.1 0.0 copy-done
  122.1 0.0 copy-done.1
  122.1 6.8 %direct_rows.1.direct_ref = f32[2048,256]{1,0:T(8,128)} custom-call(bf16[8,3072,256]{2,1,0:T(8,128)(2,1)} %get-tuple-element.24.count_ref, bf16[2048,256]{1,0:T(8,128)(2,1)S(1)} %copy-done, bf16[2048,256]{1,0:T(8,128)(2,1)S(1)} %copy-done.1, bf16[256,256]{1,0:T(8,128)(2,1)S(1)} %copy-done.2), custom_call_target="tpu_custom_call" | custom-call | flops 3000000000 | bytes 12000000 | tf_op jit(solution)/shard_map/direct_rows/pallas_call | solution.py:514
  128.9 0.0 copy-start.13
  128.9 12.9 %all-to-all-done.3.back_ref = bf16[128,16,256]{2,1,0:T(8,128)(2,1)S(1)} async-done(((bf16[128,16,256]{2,1,0:T(8,128)(2,1)}), bf16[128,16,256]{2,1,0:T(8,128)(2,1)S(1)}, u32[]{:S(2)}, u32[]{:S(2)}) %all-to-all-start.3) | async-done | bytes 1048608 | tf_op jit(solution)/shard_map/all_to_all | solution.py:622
  141.7 0.9 chunk.1
  142.6 3.9 %all-to-all-start.4 = ((bf16[128,8,128]{2,1,0:T(8,128)(2,1)}), bf16[128,8,128]{2,1,0:T(8,128)(2,1)S(1)}, u32[]{:S(2)}, u32[]{:S(2)}) async-start(bf16[128,8,128]{2,1,0:T(8,128)(2,1)} %chunk.1), calls=%async_computation.4 | async-start | bytes 524288 | tf_op jit(solution)/shard_map/all_to_all | solution.py:622
  146.5 0.0 copy-done.13
  146.5 0.1 copy.23
  146.6 0.1 reshape_squeeze.3.halo_ref
  146.7 4.1 %final.1 = (f32[2048,256]{1,0:T(8,128)}, f32[512,256]{1,0:T(8,128)}, f32[2,128]{1,0:T(2,128)}, f32[2,128]{1,0:T(2,128)}) custom-call(f32[2048,256]{1,0:T(8,128)} %direct_rows.1.direct_ref, bf16[128,16,256]{2,1,0:T(8,128)(2,1)S(1)} %all-to-all-done.3.back_ref, s32[8,128]{1,0:T(8,128)S(1)} %reshape_squeeze.3.halo_ref, f32[8,128]{1,0:T(8,128)S(1)} %get-tuple-element.34.small_ref), custom_call_target="tpu_custom_call" | custom-call | flops 2000000000 | bytes 6000000 | tf_op jit(solution)/shard_map/final/pallas_call | solution.py:581
  150.8 6.8 %all-to-all-done.4.pieces_ref = bf16[128,8,128]{2,1,0:T(8,128)(2,1)S(1)} async-done(((bf16[128,8,128]{2,1,0:T(8,128)(2,1)}), bf16[128,8,128]{2,1,0:T(8,128)(2,1)S(1)}, u32[]{:S(2)}, u32[]{:S(2)}) %all-to-all-start.4) | async-done | bytes 262176 | tf_op jit(solution)/shard_map/all_to_all | solution.py:622
  157.6 0.8 weights.1
  (1 shorter events, 0.0 us)
Async XLA Ops:
  0.6 15.6 %copy-start.6 = (s32[16384]{0:T(1024)S(1)}, s32[16384]{0:T(1024)}, u32[]{:S(2)}) copy-start(s32[16384]{0:T(1024)} %param.15) | copy-start | bytes 196612
  0.7 15.6 %copy-start.7 = (s32[16384]{0:T(1024)S(1)}, s32[16384]{0:T(1024)}, u32[]{:S(2)}) copy-start(s32[16384]{0:T(1024)} %param.16) | copy-start | bytes 196612
  4.1 28.2 %all-to-all-start = ((bf16[128,24,128]{2,1,0:T(8,128)(2,1)}), bf16[128,24,128]{2,1,0:T(8,128)(2,1)S(1)}, u32[]{:S(2)}, u32[]{:S(2)}) async-start(bf16[128,24,128]{2,1,0:T(8,128)(2,1)} %send_rows.1), calls=%async_computation | async-start | bytes 1572864 | tf_op jit(solution)/shard_map/all_to_all | solution.py:622
  20.0 12.3 %copy-start.2 = (bf16[256,256]{1,0:T(8,128)(2,1)S(1)}, bf16[256,256]{1,0:T(8,128)(2,1)}, u32[]{:S(2)}) copy-start(bf16[256,256]{1,0:T(8,128)(2,1)} %self_ref.3) | copy-start | bytes 393220
  20.0 12.3 %copy-start.3 = (bf16[2048,256]{1,0:T(8,128)(2,1)S(1)}, bf16[2048,256]{1,0:T(8,128)(2,1)}, u32[]{:S(2)}) copy-start(bf16[2048,256]{1,0:T(8,128)(2,1)} %feat_ref.3) | copy-start | bytes 3145732
  20.0 12.3 %copy-start.5 = (bf16[256,256]{1,0:T(8,128)(2,1)S(1)}, bf16[256,256]{1,0:T(8,128)(2,1)}, u32[]{:S(2)}) copy-start(bf16[256,256]{1,0:T(8,128)(2,1)} %neigh_ref.3) | copy-start | bytes 393220
  41.4 28.9 %copy-start.4 = (bf16[512,256]{1,0:T(8,128)(2,1)S(1)}, bf16[512,256]{1,0:T(8,128)(2,1)}, u32[]{:S(2)}) copy-start(bf16[512,256]{1,0:T(8,128)(2,1)} %hid_ref.1) | copy-start | bytes 786436
  41.4 28.9 %copy-start.8 = (s32[2048,2]{0,1:T(2,128)S(1)}, s32[2048,2]{0,1:T(2,128)}, u32[]{:S(2)}) copy-start(s32[2048,2]{0,1:T(2,128)} %param.20) | copy-start | bytes 49156
  41.4 28.8 %copy-start.9 = (s32[2048]{0:T(1024)S(1)}, s32[2048]{0:T(1024)}, u32[]{:S(2)}) copy-start(s32[2048]{0:T(1024)} %param.21) | copy-start | bytes 24580
  41.5 28.8 %copy-start.10 = (f32[2048]{0:T(1024)S(1)}, f32[2048]{0:T(1024)}, u32[]{:S(2)}) copy-start(f32[2048]{0:T(1024)} %param.22) | copy-start | bytes 24580
  41.5 28.8 %copy-start.11 = (f32[256]{0:T(256)S(1)}, f32[256]{0:T(256)}, u32[]{:S(2)}) copy-start(f32[256]{0:T(256)} %param.26) | copy-start | bytes 3076
  41.5 28.8 %copy-start.12 = (f32[256]{0:T(256)S(1)}, f32[256]{0:T(256)}, u32[]{:S(2)}) copy-start(f32[256]{0:T(256)} %param.27) | copy-start | bytes 3076
  118.1 4.0 %copy-start = (bf16[2048,256]{1,0:T(8,128)(2,1)S(1)}, bf16[2048,256]{1,0:T(8,128)(2,1)}, u32[]{:S(2)}) copy-start(bf16[2048,256]{1,0:T(8,128)(2,1)} %get-tuple-element.31.grad_ref) | copy-start | bytes 3145732
  118.1 4.0 %copy-start.1 = (bf16[2048,256]{1,0:T(8,128)(2,1)S(1)}, bf16[2048,256]{1,0:T(8,128)(2,1)}, u32[]{:S(2)}) copy-start(bf16[2048,256]{1,0:T(8,128)(2,1)} %get-tuple-element.32.mean_ref) | copy-start | bytes 3145732
  118.1 23.6 %all-to-all-start.3 = ((bf16[128,16,256]{2,1,0:T(8,128)(2,1)}), bf16[128,16,256]{2,1,0:T(8,128)(2,1)S(1)}, u32[]{:S(2)}, u32[]{:S(2)}) async-start(bf16[128,16,256]{2,1,0:T(8,128)(2,1)} %get-tuple-element.33), calls=%async_computation.3 | async-start | bytes 2097152 | tf_op jit(solution)/shard_map/all_to_all | solution.py:622
  128.9 17.6 %copy-start.13 = (s32[1,128,8]{1,2,0:T(8,128)S(1)}, s32[1,128,8]{1,2,0:T(8,128)}, u32[]{:S(2)}) copy-start(s32[1,128,8]{1,2,0:T(8,128)} %param.18) | copy-start | bytes 12292
  142.6 15.0 %all-to-all-start.4 = ((bf16[128,8,128]{2,1,0:T(8,128)(2,1)}), bf16[128,8,128]{2,1,0:T(8,128)(2,1)S(1)}, u32[]{:S(2)}, u32[]{:S(2)}) async-start(bf16[128,8,128]{2,1,0:T(8,128)(2,1)} %chunk.1), calls=%async_computation.4 | async-start | bytes 524288 | tf_op jit(solution)/shard_map/all_to_all | solution.py:622

commit v6 on v5

--- a/solution.py
+++ b/solution.py
@@ -15,6 +15,7 @@
 DST_BLOCK = 256
 SRC_BLOCK = 256
 VISITS = 8
+KEY_ROWS = 2
 UNROLL = 2
 SEND_MIB, EDGES_MIB, EMBED_MIB, DECODE_MIB, SPREAD_MIB = 8, 24, 24, 16, 16
 DIRECT_MIB = 16
@@ -174,7 +175,7 @@
     top = keys_ref.shape[0] - 1
     buckets = degree_ref.shape[1] // DST_BLOCK * src_blocks
     degree_ref[...] = jnp.zeros_like(degree_ref)
-    ones = (lax.broadcasted_iota(I32, (16, 512), 0) == 0).astype(F32).astype(BF16)
+    ones = (lax.broadcasted_iota(I32, (16, 128 * KEY_ROWS), 0) == 0).astype(F32).astype(BF16)
 
     def block_of(bucket):
         tall = pl.multiple_of(lax.rem(bucket, src_blocks) * SRC_BLOCK, SRC_BLOCK)
@@ -187,7 +188,7 @@
     def products(bucket, row):
         wanted = jnp.where(bucket < buckets, bucket, -1)
         src, dst = [], []
-        for i in range(4):
+        for i in range(KEY_ROWS):
             keys = keys_ref[pl.ds(jnp.minimum(row + i, top), 1), :]
             live = jnp.logical_and(lax.shift_right_logical(keys, 18) == wanted, row + i <= top)
             dst.append(jnp.where(live, lax.shift_right_logical(keys, 10) & 255, -1))
@@ -212,9 +213,9 @@
 
     def advance(bucket, row):
         last = starts_ref[jnp.minimum(bucket + 1, buckets)]
-        ended = (row + 4) * 128 >= last
+        ended = (row + KEY_ROWS) * 128 >= last
         after = jnp.minimum(bucket + ended.astype(I32), buckets)
-        return after, jnp.where(ended, lax.shift_right_logical(starts_ref[after], 7), row + 4), ended
+        return after, jnp.where(ended, lax.shift_right_logical(starts_ref[after], 7), row + KEY_ROWS), ended
 
     def body(carry):
         bucket, row, fresh = carry

time: 159 us -> 157 us (0.987)
  blocking collectives: 57.7 us -> 55.9 us
    all_to_all x2, blocking collectives: 57.7 us -> 55.9 us  [exchange(): return lax.all_to_all(rows, AXES, split_axis=0, concat_axis=0, tiled=True)]
  transfers between devices with their start and end apart: 3 -> 3, of which waited for: 3 -> 3; matrix products, arithmetic and copies ran while one was open for 1% -> 1% of each run, Pallas kernels for 16% -> 15%
where the time goes in v6:
time: 157 us
  Pallas kernels  57.3 us (36%)
  blocking collectives  55.9 us (36%)
  waiting for transfers between devices  21.3 us (14%)
  starting transfers between devices  19.3 us (12%)
  between operations  1.57 us (1%)
    all_to_all x2, blocking collectives, exchange(): return lax.all_to_all(rows, AXES, split_axis=0, concat_axis=0, tiled=True)  55.9 us
    all_to_all x3, waiting for transfers between devices, exchange(): return lax.all_to_all(rows, AXES, split_axis=0, concat_axis=0, tiled=True)  21.3 us
    all_to_all x3, starting transfers between devices, exchange(): return lax.all_to_all(rows, AXES, split_axis=0, concat_axis=0, tiled=True)  19.3 us
    pallas_call x1, Pallas kernels, decode(): pl.pallas_call(decode_body, out_shape=(shape_of((1, pairs), F32), shape_o...  12.3 us
    pallas_call x1, Pallas kernels, edge_counts(): pl.pallas_call(functools.partial(edges_body, table // SRC_BLOCK), out_sha...  10.7 us
    pallas_call x1, Pallas kernels, embed(): pl.pallas_call(embed_body, out_shape=(shape_of((nodes, width), BF16), sha...  9.06 us
    pallas_call x1, Pallas kernels, direct_rows(): pl.pallas_call(direct_body, out_shape=pltpu.HBM((nodes, width), F32), in_...  6.76 us
    pallas_call x1, Pallas kernels, spread(): pl.pallas_call(spread_body, out_shape=(pltpu.HBM((back.shape[0], 16, widt...  6.62 us
  transfers between devices with their start and end apart: 3, of which 3 were waited for; matrix products, arithmetic and copies ran while one was open for 1% of the time, Pallas kernels for 15%

profile of v6, /device:TPU:1, one launch (start us, length us, event | category | flops | bytes accessed | tf_op | source)
XLA Modules:
  0.0 156.7 jit_solution(5024149326161003653)
XLA Ops:
  0.6 0.0 copy-start.6
  0.7 0.0 copy-start.7
  0.7 3.5 %send_rows.1 = bf16[128,24,128]{2,1,0:T(8,128)(2,1)} custom-call(s32[1]{0:T(128)} %bitcast.3.slot_ref, s32[8,128]{1,0:T(8,128)} %bitcast.30, s32[16,128]{1,0:T(8,128)} %bitcast.31, bf16[2048,256]{1,0:T(8,128)(2,1)} %feat_ref.3), custom_call_target="tpu_custom_call" | custom-call | flops 1000000000 | bytes 2000000 | tf_op jit(solution)/shard_map/send_rows/pallas_call | solution.py:96
  4.1 11.5 %all-to-all-start = ((bf16[128,24,128]{2,1,0:T(8,128)(2,1)}), bf16[128,24,128]{2,1,0:T(8,128)(2,1)S(1)}, u32[]{:S(2)}, u32[]{:S(2)}) async-start(bf16[128,24,128]{2,1,0:T(8,128)(2,1)} %send_rows.1), calls=%async_computation | async-start | bytes 1572864 | tf_op jit(solution)/shard_map/all_to_all | solution.py:623
  16.3 0.0 copy-done.6
  16.3 0.0 copy-done.7
  16.3 2.7 %sort_edges.1.keys_ref = s32[128,128]{1,0:T(8,128)S(1)} custom-call(s32[1]{0:T(128)S(6)} %copy.24.live_ref, s32[128,128]{1,0:T(8,128)S(1)} %bitcast.23, s32[128,128]{1,0:T(8,128)S(1)} %bitcast.24), custom_call_target="tpu_custom_call" | custom-call | flops 1000000000 | bytes 200000 | tf_op jit(solution)/shard_map/sort_edges/pallas_call | solution.py:163
  19.0 1.0 convert_reduce_fusion.starts_ref
  20.0 0.0 copy-start.2
  20.0 0.0 copy-start.3
  20.0 0.0 copy-start.5
  20.0 10.7 %edge_counts.1 = (bf16[8,3072,256]{2,1,0:T(8,128)(2,1)}, f32[8,2048]{1,0:T(8,128)S(1)}) custom-call(s32[97]{0:T(128)S(1)} %convert_reduce_fusion.starts_ref, s32[128,128]{1,0:T(8,128)S(1)} %sort_edges.1.keys_ref), custom_call_target="tpu_custom_call" | custom-call | flops 14000000000 | bytes 13000000 | tf_op jit(solution)/shard_map/edge_counts/pallas_call | solution.py:245
  30.8 1.6 %all-to-all-done.arrived_ref = bf16[128,24,128]{2,1,0:T(8,128)(2,1)S(1)} async-done(((bf16[128,24,128]{2,1,0:T(8,128)(2,1)}), bf16[128,24,128]{2,1,0:T(8,128)(2,1)S(1)}, u32[]{:S(2)}, u32[]{:S(2)}) %all-to-all-start) | async-done | bytes 786464 | tf_op jit(solution)/shard_map/all_to_all | solution.py:623
  32.3 0.0 copy-done.2
  32.3 0.0 copy-done.3
  32.3 0.0 copy-done.5
  32.4 9.1 %embed.1 = (bf16[2048,256]{1,0:T(8,128)(2,1)S(1)}, bf16[2048,256]{1,0:T(8,128)(2,1)S(1)}, s32[16,128]{1,0:T(8,128)S(1)}) custom-call(bf16[8,3072,256]{2,1,0:T(8,128)(2,1)} %get-tuple-element.24.count_ref, bf16[128,24,128]{2,1,0:T(8,128)(2,1)S(1)} %all-to-all-done.arrived_ref, bf16[2048,256]{1,0:T(8,128)(2,1)S(1)} %copy-done.3, ...), custom_call_target="tpu_custom_call" | custom-call | flops 6000000000 | bytes 16000000 | tf_op jit(solution)/shard_map/embed/pallas_call | solution.py:304
  41.4 0.0 copy-start.4
  41.4 0.0 copy-start.8
  41.4 0.0 copy-start.9
  41.5 0.0 copy-start.10
  41.5 0.0 copy-start.11
  41.5 0.0 copy-start.12
  41.5 27.1 %all_to_all.25 = bf16[128,16,256]{2,1,0:T(8,128)(2,1)S(1)} all-to-all(bf16[128,16,256]{2,1,0:T(8,128)(2,1)S(1)} %bitcast.20), channel_id=1, replica_groups=mesh['dom'=32,'grp'=4] {'dom','grp'}, dimensions={0} | all-to-all | bytes 2097152 | tf_op jit(solution)/shard_map/all_to_all | solution.py:623
  68.6 0.0 copy-done.4
  68.6 0.0 copy-done.8
  68.6 0.0 copy-done.9
  68.6 0.0 copy-done.10
  68.6 0.0 copy-done.11
  68.6 0.0 copy-done.12
  68.6 12.3 %decode.1 = (f32[1,2048]{1,0:T(1,128)}, bf16[128,24,256]{2,1,0:T(8,128)(2,1)S(1)}) custom-call(bf16[2048,256]{1,0:T(8,128)(2,1)S(1)} %bitcast.21, s32[2,2048]{1,0:T(2,128)S(1)} %bitcast.25, s32[1,2048]{1,0:T(1,128)S(1)} %bitcast.26, f32[1,2048]{1,0:T(1,128)S(1)} %bitcast.27, bf16[512,256]{1,0:T(8,128)(2,1)S(1)} %copy-done.4, f32[1,256]{1,0:T(1,128)S(1)} %bitcast.28, ...), custom_call_target="tpu_custom_call" | custom-call | flops 10000000000 | bytes 4000000 | tf_op jit(solution)/shard_map/decode/pallas_call | solution.py:389
  80.9 28.9 %all_to_all.26.back_ref = bf16[128,24,256]{2,1,0:T(8,128)(2,1)S(1)} all-to-all(bf16[128,24,256]{2,1,0:T(8,128)(2,1)S(1)} %get-tuple-element.28), channel_id=1, replica_groups=mesh['dom'=32,'grp'=4] {'dom','grp'}, dimensions={0} | all-to-all | bytes 3145728 | tf_op jit(solution)/shard_map/all_to_all | solution.py:623
  109.8 6.6 %spread.1 = (bf16[128,16,256]{2,1,0:T(8,128)(2,1)}, f32[8,128]{1,0:T(8,128)S(1)}, bf16[2048,256]{1,0:T(8,128)(2,1)}, bf16[2048,256]{1,0:T(8,128)(2,1)}) custom-call(bf16[8,3072,256]{2,1,0:T(8,128)(2,1)} %get-tuple-element.24.count_ref, bf16[128,24,256]{2,1,0:T(8,128)(2,1)S(1)} %all_to_all.26.back_ref, s32[16,128]{1,0:T(8,128)S(1)} %get-tuple-element.29.want_ref, ...), custom_call_target="tpu_custom_call" | custom-call | flops 5000000000 | bytes 10000000 | tf_op jit(solution)/shard_map/spread/pallas_call | solution.py:466
  116.4 0.0 copy-start
  116.4 0.0 copy-start.1
  116.4 3.9 %all-to-all-start.3 = ((bf16[128,16,256]{2,1,0:T(8,128)(2,1)}), bf16[128,16,256]{2,1,0:T(8,128)(2,1)S(1)}, u32[]{:S(2)}, u32[]{:S(2)}) async-start(bf16[128,16,256]{2,1,0:T(8,128)(2,1)} %get-tuple-element.33), calls=%async_computation.3 | async-start | bytes 2097152 | tf_op jit(solution)/shard_map/all_to_all | solution.py:623
  120.4 0.0 copy-done
  120.4 0.0 copy-done.1
  120.4 6.8 %direct_rows.1.direct_ref = f32[2048,256]{1,0:T(8,128)} custom-call(bf16[8,3072,256]{2,1,0:T(8,128)(2,1)} %get-tuple-element.24.count_ref, bf16[2048,256]{1,0:T(8,128)(2,1)S(1)} %copy-done, bf16[2048,256]{1,0:T(8,128)(2,1)S(1)} %copy-done.1, bf16[256,256]{1,0:T(8,128)(2,1)S(1)} %copy-done.2), custom_call_target="tpu_custom_call" | custom-call | flops 3000000000 | bytes 12000000 | tf_op jit(solution)/shard_map/direct_rows/pallas_call | solution.py:515
  127.1 0.0 copy-start.13
  127.2 12.9 %all-to-all-done.3.back_ref = bf16[128,16,256]{2,1,0:T(8,128)(2,1)S(1)} async-done(((bf16[128,16,256]{2,1,0:T(8,128)(2,1)}), bf16[128,16,256]{2,1,0:T(8,128)(2,1)S(1)}, u32[]{:S(2)}, u32[]{:S(2)}) %all-to-all-start.3) | async-done | bytes 1048608 | tf_op jit(solution)/shard_map/all_to_all | solution.py:623
  140.0 0.9 chunk.1
  140.9 3.9 %all-to-all-start.4 = ((bf16[128,8,128]{2,1,0:T(8,128)(2,1)}), bf16[128,8,128]{2,1,0:T(8,128)(2,1)S(1)}, u32[]{:S(2)}, u32[]{:S(2)}) async-start(bf16[128,8,128]{2,1,0:T(8,128)(2,1)} %chunk.1), calls=%async_computation.4 | async-start | bytes 524288 | tf_op jit(solution)/shard_map/all_to_all | solution.py:623
  144.8 0.0 copy-done.13
  144.8 0.1 copy.23
  144.9 0.1 reshape_squeeze.3.halo_ref
  145.0 4.1 %final.1 = (f32[2048,256]{1,0:T(8,128)}, f32[512,256]{1,0:T(8,128)}, f32[2,128]{1,0:T(2,128)}, f32[2,128]{1,0:T(2,128)}) custom-call(f32[2048,256]{1,0:T(8,128)} %direct_rows.1.direct_ref, bf16[128,16,256]{2,1,0:T(8,128)(2,1)S(1)} %all-to-all-done.3.back_ref, s32[8,128]{1,0:T(8,128)S(1)} %reshape_squeeze.3.halo_ref, f32[8,128]{1,0:T(8,128)S(1)} %get-tuple-element.34.small_ref), custom_call_target="tpu_custom_call" | custom-call | flops 2000000000 | bytes 6000000 | tf_op jit(solution)/shard_map/final/pallas_call | solution.py:582
  149.1 6.8 %all-to-all-done.4.pieces_ref = bf16[128,8,128]{2,1,0:T(8,128)(2,1)S(1)} async-done(((bf16[128,8,128]{2,1,0:T(8,128)(2,1)}), bf16[128,8,128]{2,1,0:T(8,128)(2,1)S(1)}, u32[]{:S(2)}, u32[]{:S(2)}) %all-to-all-start.4) | async-done | bytes 262176 | tf_op jit(solution)/shard_map/all_to_all | solution.py:623
  155.9 0.8 weights.1
  (1 shorter events, 0.0 us)
Async XLA Ops:
  0.6 15.6 %copy-start.6 = (s32[16384]{0:T(1024)S(1)}, s32[16384]{0:T(1024)}, u32[]{:S(2)}) copy-start(s32[16384]{0:T(1024)} %param.15) | copy-start | bytes 196612
  0.7 15.6 %copy-start.7 = (s32[16384]{0:T(1024)S(1)}, s32[16384]{0:T(1024)}, u32[]{:S(2)}) copy-start(s32[16384]{0:T(1024)} %param.16) | copy-start | bytes 196612
  4.1 28.2 %all-to-all-start = ((bf16[128,24,128]{2,1,0:T(8,128)(2,1)}), bf16[128,24,128]{2,1,0:T(8,128)(2,1)S(1)}, u32[]{:S(2)}, u32[]{:S(2)}) async-start(bf16[128,24,128]{2,1,0:T(8,128)(2,1)} %send_rows.1), calls=%async_computation | async-start | bytes 1572864 | tf_op jit(solution)/shard_map/all_to_all | solution.py:623
  20.0 12.3 %copy-start.2 = (bf16[256,256]{1,0:T(8,128)(2,1)S(1)}, bf16[256,256]{1,0:T(8,128)(2,1)}, u32[]{:S(2)}) copy-start(bf16[256,256]{1,0:T(8,128)(2,1)} %self_ref.3) | copy-start | bytes 393220
  20.0 12.3 %copy-start.3 = (bf16[2048,256]{1,0:T(8,128)(2,1)S(1)}, bf16[2048,256]{1,0:T(8,128)(2,1)}, u32[]{:S(2)}) copy-start(bf16[2048,256]{1,0:T(8,128)(2,1)} %feat_ref.3) | copy-start | bytes 3145732
  20.0 12.3 %copy-start.5 = (bf16[256,256]{1,0:T(8,128)(2,1)S(1)}, bf16[256,256]{1,0:T(8,128)(2,1)}, u32[]{:S(2)}) copy-start(bf16[256,256]{1,0:T(8,128)(2,1)} %neigh_ref.3) | copy-start | bytes 393220
  41.4 27.2 %copy-start.4 = (bf16[512,256]{1,0:T(8,128)(2,1)S(1)}, bf16[512,256]{1,0:T(8,128)(2,1)}, u32[]{:S(2)}) copy-start(bf16[512,256]{1,0:T(8,128)(2,1)} %hid_ref.1) | copy-start | bytes 786436
  41.4 27.1 %copy-start.8 = (s32[2048,2]{0,1:T(2,128)S(1)}, s32[2048,2]{0,1:T(2,128)}, u32[]{:S(2)}) copy-start(s32[2048,2]{0,1:T(2,128)} %param.20) | copy-start | bytes 49156
  41.4 27.1 %copy-start.9 = (s32[2048]{0:T(1024)S(1)}, s32[2048]{0:T(1024)}, u32[]{:S(2)}) copy-start(s32[2048]{0:T(1024)} %param.21) | copy-start | bytes 24580
  41.5 27.1 %copy-start.10 = (f32[2048]{0:T(1024)S(1)}, f32[2048]{0:T(1024)}, u32[]{:S(2)}) copy-start(f32[2048]{0:T(1024)} %param.22) | copy-start | bytes 24580
  41.5 27.1 %copy-start.11 = (f32[256]{0:T(256)S(1)}, f32[256]{0:T(256)}, u32[]{:S(2)}) copy-start(f32[256]{0:T(256)} %param.26) | copy-start | bytes 3076
  41.5 27.1 %copy-start.12 = (f32[256]{0:T(256)S(1)}, f32[256]{0:T(256)}, u32[]{:S(2)}) copy-start(f32[256]{0:T(256)} %param.27) | copy-start | bytes 3076
  116.4 3.9 %copy-start = (bf16[2048,256]{1,0:T(8,128)(2,1)S(1)}, bf16[2048,256]{1,0:T(8,128)(2,1)}, u32[]{:S(2)}) copy-start(bf16[2048,256]{1,0:T(8,128)(2,1)} %get-tuple-element.31.grad_ref) | copy-start | bytes 3145732
  116.4 3.9 %copy-start.1 = (bf16[2048,256]{1,0:T(8,128)(2,1)S(1)}, bf16[2048,256]{1,0:T(8,128)(2,1)}, u32[]{:S(2)}) copy-start(bf16[2048,256]{1,0:T(8,128)(2,1)} %get-tuple-element.32.mean_ref) | copy-start | bytes 3145732
  116.4 23.6 %all-to-all-start.3 = ((bf16[128,16,256]{2,1,0:T(8,128)(2,1)}), bf16[128,16,256]{2,1,0:T(8,128)(2,1)S(1)}, u32[]{:S(2)}, u32[]{:S(2)}) async-start(bf16[128,16,256]{2,1,0:T(8,128)(2,1)} %get-tuple-element.33), calls=%async_computation.3 | async-start | bytes 2097152 | tf_op jit(solution)/shard_map/all_to_all | solution.py:623
  127.1 17.6 %copy-start.13 = (s32[1,128,8]{1,2,0:T(8,128)S(1)}, s32[1,128,8]{1,2,0:T(8,128)}, u32[]{:S(2)}) copy-start(s32[1,128,8]{1,2,0:T(8,128)} %param.18) | copy-start | bytes 12292
  140.9 15.0 %all-to-all-start.4 = ((bf16[128,8,128]{2,1,0:T(8,128)(2,1)}), bf16[128,8,128]{2,1,0:T(8,128)(2,1)S(1)}, u32[]{:S(2)}, u32[]{:S(2)}) async-start(bf16[128,8,128]{2,1,0:T(8,128)(2,1)} %chunk.1), calls=%async_computation.4 | async-start | bytes 524288 | tf_op jit(solution)/shard_map/all_to_all | solution.py:623

commit v7 on v6

--- a/solution.py
+++ b/solution.py
@@ -433,7 +433,7 @@
         mean_ref[span, :] = scaled.astype(BF16)
         return carry
 
-    lax.fori_loop(0, nodes // 256, scale, 0, unroll=2)
+    lax.fori_loop(0, nodes // 256, scale, 0, unroll=8)
     halves = [(slice(None), slice(0, 8)), (slice(None), slice(8, 16))]
     pairs = [(send_ref.at[half], send_hbm.at[half]) for half in halves]
     pairs += [(grad_ref, grad_hbm), (mean_ref, mean_hbm)]
@@ -529,7 +529,7 @@
 
 def chunk_body(back_ref, direct_ref, out_ref):
     del direct_ref
-    tail = jnp.sum(back_ref[:, 8:, :].astype(F32), axis=0)[:, :128]
+    tail = jnp.sum(back_ref[:, 8:, :128].astype(F32), axis=0)
     out_ref[...] = jnp.broadcast_to(tail[None], out_ref.shape).astype(BF16)
 
 

time: 157 us -> 157 us (level)
  Pallas kernels: 57.3 us -> 53.8 us
  waiting for transfers between devices: 21.3 us -> 23.9 us
    pallas_call x1, Pallas kernels: 10.7 us -> 8.06 us  [edge_counts(): pl.pallas_call(functools.partial(edges_body, table // SRC_BLOCK), out_sha...]
    all_to_all x3, waiting for transfers between devices: 21.3 us -> 23.9 us  [exchange(): return lax.all_to_all(rows, AXES, split_axis=0, concat_axis=0, tiled=True)]
  transfers between devices with their start and end apart: 3 -> 3, of which waited for: 3 -> 3; matrix products, arithmetic and copies ran while one was open for 1% -> 1% of each run, Pallas kernels for 15% -> 14%
where the time goes in v7:
time: 157 us; the launch traced here: 156 us
  blocking collectives  56.3 us (36%)
  Pallas kernels  53.8 us (34%)
  waiting for transfers between devices  23.9 us (15%)
  starting transfers between devices  19.3 us (12%)
  between operations  1.57 us (1%)
    all_to_all x2, blocking collectives, exchange(): return lax.all_to_all(rows, AXES, split_axis=0, concat_axis=0, tiled=True)  56.3 us
    all_to_all x3, waiting for transfers between devices, exchange(): return lax.all_to_all(rows, AXES, split_axis=0, concat_axis=0, tiled=True)  23.9 us
    all_to_all x3, starting transfers between devices, exchange(): return lax.all_to_all(rows, AXES, split_axis=0, concat_axis=0, tiled=True)  19.3 us
    pallas_call x1, Pallas kernels, decode(): pl.pallas_call(decode_body, out_shape=(shape_of((1, pairs), F32), shape_o...  12.3 us
    pallas_call x1, Pallas kernels, embed(): pl.pallas_call(embed_body, out_shape=(shape_of((nodes, width), BF16), sha...  9.06 us
    pallas_call x1, Pallas kernels, edge_counts(): pl.pallas_call(functools.partial(edges_body, table // SRC_BLOCK), out_sha...  8.06 us
    pallas_call x1, Pallas kernels, direct_rows(): pl.pallas_call(direct_body, out_shape=pltpu.HBM((nodes, width), F32), in_...  6.76 us
    pallas_call x1, Pallas kernels, spread(): pl.pallas_call(spread_body, out_shape=(pltpu.HBM((back.shape[0], 16, widt...  5.76 us
  transfers between devices with their start and end apart: 3, of which 3 were waited for; matrix products, arithmetic and copies ran while one was open for 1% of the time, Pallas kernels for 14%

profile of v7, /device:TPU:1, one launch (start us, length us, event | category | flops | bytes accessed | tf_op | source)
XLA Modules:
  0.0 156.3 jit_solution(3810605394940769033)
XLA Ops:
  0.6 0.0 copy-start.6
  0.7 0.0 copy-start.7
  0.7 3.5 %send_rows.1 = bf16[128,24,128]{2,1,0:T(8,128)(2,1)} custom-call(s32[1]{0:T(128)} %bitcast.3.slot_ref, s32[8,128]{1,0:T(8,128)} %bitcast.30, s32[16,128]{1,0:T(8,128)} %bitcast.31, bf16[2048,256]{1,0:T(8,128)(2,1)} %feat_ref.3), custom_call_target="tpu_custom_call" | custom-call | flops 1000000000 | bytes 2000000 | tf_op jit(solution)/shard_map/send_rows/pallas_call | solution.py:96
  4.1 11.5 %all-to-all-start = ((bf16[128,24,128]{2,1,0:T(8,128)(2,1)}), bf16[128,24,128]{2,1,0:T(8,128)(2,1)S(1)}, u32[]{:S(2)}, u32[]{:S(2)}) async-start(bf16[128,24,128]{2,1,0:T(8,128)(2,1)} %send_rows.1), calls=%async_computation | async-start | bytes 1572864 | tf_op jit(solution)/shard_map/all_to_all | solution.py:623
  16.3 0.0 copy-done.6
  16.3 0.0 copy-done.7
  16.3 2.7 %sort_edges.1.keys_ref = s32[128,128]{1,0:T(8,128)S(1)} custom-call(s32[1]{0:T(128)S(6)} %copy.24.live_ref, s32[128,128]{1,0:T(8,128)S(1)} %bitcast.23, s32[128,128]{1,0:T(8,128)S(1)} %bitcast.24), custom_call_target="tpu_custom_call" | custom-call | flops 1000000000 | bytes 200000 | tf_op jit(solution)/shard_map/sort_edges/pallas_call | solution.py:163
  19.0 1.0 convert_reduce_fusion.starts_ref
  20.0 0.0 copy-start.2
  20.0 0.0 copy-start.3
  20.0 0.0 copy-start.5
  20.0 8.1 %edge_counts.1 = (bf16[8,3072,256]{2,1,0:T(8,128)(2,1)}, f32[8,2048]{1,0:T(8,128)S(1)}) custom-call(s32[97]{0:T(128)S(1)} %convert_reduce_fusion.starts_ref, s32[128,128]{1,0:T(8,128)S(1)} %sort_edges.1.keys_ref), custom_call_target="tpu_custom_call" | custom-call | flops 14000000000 | bytes 13000000 | tf_op jit(solution)/shard_map/edge_counts/pallas_call | solution.py:245
  28.1 4.2 %all-to-all-done.arrived_ref = bf16[128,24,128]{2,1,0:T(8,128)(2,1)S(1)} async-done(((bf16[128,24,128]{2,1,0:T(8,128)(2,1)}), bf16[128,24,128]{2,1,0:T(8,128)(2,1)S(1)}, u32[]{:S(2)}, u32[]{:S(2)}) %all-to-all-start) | async-done | bytes 786464 | tf_op jit(solution)/shard_map/all_to_all | solution.py:623
  32.3 0.0 copy-done.2
  32.3 0.0 copy-done.3
  32.3 0.0 copy-done.5
  32.4 9.1 %embed.1 = (bf16[2048,256]{1,0:T(8,128)(2,1)S(1)}, bf16[2048,256]{1,0:T(8,128)(2,1)S(1)}, s32[16,128]{1,0:T(8,128)S(1)}) custom-call(bf16[8,3072,256]{2,1,0:T(8,128)(2,1)} %get-tuple-element.24.count_ref, bf16[128,24,128]{2,1,0:T(8,128)(2,1)S(1)} %all-to-all-done.arrived_ref, bf16[2048,256]{1,0:T(8,128)(2,1)S(1)} %copy-done.3, ...), custom_call_target="tpu_custom_call" | custom-call | flops 6000000000 | bytes 16000000 | tf_op jit(solution)/shard_map/embed/pallas_call | solution.py:304
  41.4 0.0 copy-start.4
  41.4 0.0 copy-start.8
  41.4 0.0 copy-start.9
  41.5 0.0 copy-start.10
  41.5 0.0 copy-start.11
  41.5 0.0 copy-start.12
  41.5 27.5 %all_to_all.25 = bf16[128,16,256]{2,1,0:T(8,128)(2,1)S(1)} all-to-all(bf16[128,16,256]{2,1,0:T(8,128)(2,1)S(1)} %bitcast.20), channel_id=1, replica_groups=mesh['dom'=32,'grp'=4] {'dom','grp'}, dimensions={0} | all-to-all | bytes 2097152 | tf_op jit(solution)/shard_map/all_to_all | solution.py:623
  69.0 0.0 copy-done.4
  69.0 0.0 copy-done.8
  69.0 0.0 copy-done.9
  69.0 0.0 copy-done.10
  69.0 0.0 copy-done.11
  69.0 0.0 copy-done.12
  69.0 12.3 %decode.1 = (f32[1,2048]{1,0:T(1,128)}, bf16[128,24,256]{2,1,0:T(8,128)(2,1)S(1)}) custom-call(bf16[2048,256]{1,0:T(8,128)(2,1)S(1)} %bitcast.21, s32[2,2048]{1,0:T(2,128)S(1)} %bitcast.25, s32[1,2048]{1,0:T(1,128)S(1)} %bitcast.26, f32[1,2048]{1,0:T(1,128)S(1)} %bitcast.27, bf16[512,256]{1,0:T(8,128)(2,1)S(1)} %copy-done.4, f32[1,256]{1,0:T(1,128)S(1)} %bitcast.28, ...), custom_call_target="tpu_custom_call" | custom-call | flops 10000000000 | bytes 4000000 | tf_op jit(solution)/shard_map/decode/pallas_call | solution.py:389
  81.4 28.8 %all_to_all.26.back_ref = bf16[128,24,256]{2,1,0:T(8,128)(2,1)S(1)} all-to-all(bf16[128,24,256]{2,1,0:T(8,128)(2,1)S(1)} %get-tuple-element.28), channel_id=1, replica_groups=mesh['dom'=32,'grp'=4] {'dom','grp'}, dimensions={0} | all-to-all | bytes 3145728 | tf_op jit(solution)/shard_map/all_to_all | solution.py:623
  110.2 5.8 %spread.1 = (bf16[128,16,256]{2,1,0:T(8,128)(2,1)}, f32[8,128]{1,0:T(8,128)S(1)}, bf16[2048,256]{1,0:T(8,128)(2,1)}, bf16[2048,256]{1,0:T(8,128)(2,1)}) custom-call(bf16[8,3072,256]{2,1,0:T(8,128)(2,1)} %get-tuple-element.24.count_ref, bf16[128,24,256]{2,1,0:T(8,128)(2,1)S(1)} %all_to_all.26.back_ref, s32[16,128]{1,0:T(8,128)S(1)} %get-tuple-element.29.want_ref, ...), custom_call_target="tpu_custom_call" | custom-call | flops 5000000000 | bytes 10000000 | tf_op jit(solution)/shard_map/spread/pallas_call | solution.py:466
  116.0 0.0 copy-start
  116.0 0.0 copy-start.1
  116.0 3.9 %all-to-all-start.3 = ((bf16[128,16,256]{2,1,0:T(8,128)(2,1)}), bf16[128,16,256]{2,1,0:T(8,128)(2,1)S(1)}, u32[]{:S(2)}, u32[]{:S(2)}) async-start(bf16[128,16,256]{2,1,0:T(8,128)(2,1)} %get-tuple-element.33), calls=%async_computation.3 | async-start | bytes 2097152 | tf_op jit(solution)/shard_map/all_to_all | solution.py:623
  119.9 0.0 copy-done
  119.9 0.0 copy-done.1
  119.9 6.8 %direct_rows.1.direct_ref = f32[2048,256]{1,0:T(8,128)} custom-call(bf16[8,3072,256]{2,1,0:T(8,128)(2,1)} %get-tuple-element.24.count_ref, bf16[2048,256]{1,0:T(8,128)(2,1)S(1)} %copy-done, bf16[2048,256]{1,0:T(8,128)(2,1)S(1)} %copy-done.1, bf16[256,256]{1,0:T(8,128)(2,1)S(1)} %copy-done.2), custom_call_target="tpu_custom_call" | custom-call | flops 3000000000 | bytes 12000000 | tf_op jit(solution)/shard_map/direct_rows/pallas_call | solution.py:515
  126.7 0.0 copy-start.13
  126.7 12.9 %all-to-all-done.3.back_ref = bf16[128,16,256]{2,1,0:T(8,128)(2,1)S(1)} async-done(((bf16[128,16,256]{2,1,0:T(8,128)(2,1)}), bf16[128,16,256]{2,1,0:T(8,128)(2,1)S(1)}, u32[]{:S(2)}, u32[]{:S(2)}) %all-to-all-start.3) | async-done | bytes 1048608 | tf_op jit(solution)/shard_map/all_to_all | solution.py:623
  139.6 0.9 chunk.1
  140.4 3.9 %all-to-all-start.4 = ((bf16[128,8,128]{2,1,0:T(8,128)(2,1)}), bf16[128,8,128]{2,1,0:T(8,128)(2,1)S(1)}, u32[]{:S(2)}, u32[]{:S(2)}) async-start(bf16[128,8,128]{2,1,0:T(8,128)(2,1)} %chunk.1), calls=%async_computation.4 | async-start | bytes 524288 | tf_op jit(solution)/shard_map/all_to_all | solution.py:623
  144.3 0.0 copy-done.13
  144.3 0.1 copy.23
  144.5 0.1 reshape_squeeze.3.halo_ref
  144.5 4.1 %final.1 = (f32[2048,256]{1,0:T(8,128)}, f32[512,256]{1,0:T(8,128)}, f32[2,128]{1,0:T(2,128)}, f32[2,128]{1,0:T(2,128)}) custom-call(f32[2048,256]{1,0:T(8,128)} %direct_rows.1.direct_ref, bf16[128,16,256]{2,1,0:T(8,128)(2,1)S(1)} %all-to-all-done.3.back_ref, s32[8,128]{1,0:T(8,128)S(1)} %reshape_squeeze.3.halo_ref, f32[8,128]{1,0:T(8,128)S(1)} %get-tuple-element.34.small_ref), custom_call_target="tpu_custom_call" | custom-call | flops 2000000000 | bytes 6000000 | tf_op jit(solution)/shard_map/final/pallas_call | solution.py:582
  148.6 6.8 %all-to-all-done.4.pieces_ref = bf16[128,8,128]{2,1,0:T(8,128)(2,1)S(1)} async-done(((bf16[128,8,128]{2,1,0:T(8,128)(2,1)}), bf16[128,8,128]{2,1,0:T(8,128)(2,1)S(1)}, u32[]{:S(2)}, u32[]{:S(2)}) %all-to-all-start.4) | async-done | bytes 262176 | tf_op jit(solution)/shard_map/all_to_all | solution.py:623
  155.4 0.8 weights.1
  (1 shorter events, 0.0 us)
Async XLA Ops:
  0.6 15.6 %copy-start.6 = (s32[16384]{0:T(1024)S(1)}, s32[16384]{0:T(1024)}, u32[]{:S(2)}) copy-start(s32[16384]{0:T(1024)} %param.15) | copy-start | bytes 196612
  0.7 15.6 %copy-start.7 = (s32[16384]{0:T(1024)S(1)}, s32[16384]{0:T(1024)}, u32[]{:S(2)}) copy-start(s32[16384]{0:T(1024)} %param.16) | copy-start | bytes 196612
  4.1 28.2 %all-to-all-start = ((bf16[128,24,128]{2,1,0:T(8,128)(2,1)}), bf16[128,24,128]{2,1,0:T(8,128)(2,1)S(1)}, u32[]{:S(2)}, u32[]{:S(2)}) async-start(bf16[128,24,128]{2,1,0:T(8,128)(2,1)} %send_rows.1), calls=%async_computation | async-start | bytes 1572864 | tf_op jit(solution)/shard_map/all_to_all | solution.py:623
  20.0 12.3 %copy-start.2 = (bf16[256,256]{1,0:T(8,128)(2,1)S(1)}, bf16[256,256]{1,0:T(8,128)(2,1)}, u32[]{:S(2)}) copy-start(bf16[256,256]{1,0:T(8,128)(2,1)} %self_ref.3) | copy-start | bytes 393220
  20.0 12.3 %copy-start.3 = (bf16[2048,256]{1,0:T(8,128)(2,1)S(1)}, bf16[2048,256]{1,0:T(8,128)(2,1)}, u32[]{:S(2)}) copy-start(bf16[2048,256]{1,0:T(8,128)(2,1)} %feat_ref.3) | copy-start | bytes 3145732
  20.0 12.3 %copy-start.5 = (bf16[256,256]{1,0:T(8,128)(2,1)S(1)}, bf16[256,256]{1,0:T(8,128)(2,1)}, u32[]{:S(2)}) copy-start(bf16[256,256]{1,0:T(8,128)(2,1)} %neigh_ref.3) | copy-start | bytes 393220
  41.4 27.6 %copy-start.4 = (bf16[512,256]{1,0:T(8,128)(2,1)S(1)}, bf16[512,256]{1,0:T(8,128)(2,1)}, u32[]{:S(2)}) copy-start(bf16[512,256]{1,0:T(8,128)(2,1)} %hid_ref.1) | copy-start | bytes 786436
  41.4 27.6 %copy-start.8 = (s32[2048,2]{0,1:T(2,128)S(1)}, s32[2048,2]{0,1:T(2,128)}, u32[]{:S(2)}) copy-start(s32[2048,2]{0,1:T(2,128)} %param.20) | copy-start | bytes 49156
  41.4 27.6 %copy-start.9 = (s32[2048]{0:T(1024)S(1)}, s32[2048]{0:T(1024)}, u32[]{:S(2)}) copy-start(s32[2048]{0:T(1024)} %param.21) | copy-start | bytes 24580
  41.5 27.6 %copy-start.10 = (f32[2048]{0:T(1024)S(1)}, f32[2048]{0:T(1024)}, u32[]{:S(2)}) copy-start(f32[2048]{0:T(1024)} %param.22) | copy-start | bytes 24580
  41.5 27.5 %copy-start.11 = (f32[256]{0:T(256)S(1)}, f32[256]{0:T(256)}, u32[]{:S(2)}) copy-start(f32[256]{0:T(256)} %param.26) | copy-start | bytes 3076
  41.5 27.5 %copy-start.12 = (f32[256]{0:T(256)S(1)}, f32[256]{0:T(256)}, u32[]{:S(2)}) copy-start(f32[256]{0:T(256)} %param.27) | copy-start | bytes 3076
  116.0 4.0 %copy-start = (bf16[2048,256]{1,0:T(8,128)(2,1)S(1)}, bf16[2048,256]{1,0:T(8,128)(2,1)}, u32[]{:S(2)}) copy-start(bf16[2048,256]{1,0:T(8,128)(2,1)} %get-tuple-element.31.grad_ref) | copy-start | bytes 3145732
  116.0 4.0 %copy-start.1 = (bf16[2048,256]{1,0:T(8,128)(2,1)S(1)}, bf16[2048,256]{1,0:T(8,128)(2,1)}, u32[]{:S(2)}) copy-start(bf16[2048,256]{1,0:T(8,128)(2,1)} %get-tuple-element.32.mean_ref) | copy-start | bytes 3145732
  116.0 23.6 %all-to-all-start.3 = ((bf16[128,16,256]{2,1,0:T(8,128)(2,1)}), bf16[128,16,256]{2,1,0:T(8,128)(2,1)S(1)}, u32[]{:S(2)}, u32[]{:S(2)}) async-start(bf16[128,16,256]{2,1,0:T(8,128)(2,1)} %get-tuple-element.33), calls=%async_computation.3 | async-start | bytes 2097152 | tf_op jit(solution)/shard_map/all_to_all | solution.py:623
  126.7 17.6 %copy-start.13 = (s32[1,128,8]{1,2,0:T(8,128)S(1)}, s32[1,128,8]{1,2,0:T(8,128)}, u32[]{:S(2)}) copy-start(s32[1,128,8]{1,2,0:T(8,128)} %param.18) | copy-start | bytes 12292
  140.4 15.0 %all-to-all-start.4 = ((bf16[128,8,128]{2,1,0:T(8,128)(2,1)}), bf16[128,8,128]{2,1,0:T(8,128)(2,1)S(1)}, u32[]{:S(2)}, u32[]{:S(2)}) async-start(bf16[128,8,128]{2,1,0:T(8,128)(2,1)} %chunk.1), calls=%async_computation.4 | async-start | bytes 524288 | tf_op jit(solution)/shard_map/all_to_all | solution.py:623
